TPU v7x, 32 devices: a whole 2x2x4 slice. The times are simulated.
32 devices in a mesh: dp: 8 (over z, y), dap: 4 (over x, core).
Axes of the slice: x: 2, y: 2, z: 4, core: 2. Of those that a mesh axis runs over, the one named last changes fastest.
Arguments:
- z_pair: bfloat16 [8, 256, 256, 64], P('dp', 'dap')
- pair_mask: int32 [8, 256, 256], P('dp', 'dap')
- dz_out: bfloat16 [8, 256, 256, 64], P('dp', 'dap')
- ln_in: bfloat16 [2, 2, 64], replicated
- w_proj: bfloat16 [2, 64, 320], replicated
- b_proj: bfloat16 [2, 320], replicated
- ln_mid: bfloat16 [2, 2, 64], replicated
- w_out: bfloat16 [2, 64, 64], replicated
- b_out: bfloat16 [2, 64], replicated
Outputs:
- output 1: bfloat16 [8, 256, 256, 64], P('dp', 'dap')
- output 2: bfloat16 [8, 256, 256, 64], P('dp', 'dap')
- output 3: float32 [2, 2, 64], replicated
- output 4: float32 [2, 64, 320], replicated
- output 5: float32 [2, 320], replicated
- output 6: float32 [2, 2, 64], replicated
- output 7: float32 [2, 64, 64], replicated
- output 8: float32 [2, 64], replicated
All inputs are finite; a program needn't handle non-finite values.
Results may differ from a plain program's by a relative error of at most 0.0115083.
Values are sent between devices in bfloat16 or wider.
A program may use at most 1 GiB of HBM per device.

v0:
```python
import functools

import jax
import jax.numpy as jnp
from jax import lax
from jax.experimental import pallas as pl
from jax.experimental.pallas import tpu as pltpu
from jax.sharding import PartitionSpec as P


EPS = 1e-5
F32 = jnp.float32
BF16 = jnp.bfloat16
INTERPRET = False
C = 64
RB = 16
UNROLL = 16
DELAY = 4
LANES = 128
W2 = 256
HALF = 0.5
MEGA = 10 ** 6
GIGA = 10 ** 9
MIB = 2 ** 20
VMEM_LIMIT = 56 * 1024 * 1024


MESH_ID = pl.DeviceIdType.MESH


def dot_nn(a, b):
    return lax.dot_general(a, b, (((1,), (0,)), ((), ())), preferred_element_type=F32)


def dot_nt(a, b):
    return lax.dot_general(a, b, (((1,), (1,)), ((), ())), preferred_element_type=F32)


def dot_tn(a, b):
    return lax.dot_general(a, b, (((0,), (0,)), ((), ())), preferred_element_type=F32)


def norm_rows(zf):
    mean = jnp.mean(zf, axis=0, keepdims=True)
    cen = zf - mean
    var = jnp.mean(cen * cen, axis=0, keepdims=True)
    rstd = lax.rsqrt(var + EPS)
    return cen * rstd, rstd


def staggered(first, second):
    for i in range(RB + DELAY):
        if i < RB:
            first(i)
        if i >= DELAY:
            second(i - DELAY)


def fold(v):
    return v[:, :LANES] + v[:, LANES:]


def to_cmajor(perm, src, dst):
    n = src.shape[-1]
    for grp in range(C // RB):
        blk = src[:, grp * RB:(grp + 1) * RB, :].reshape(W2, n)
        out = dot_nn(perm, blk)
        dst(grp, out.reshape(RB, RB, n))


def to_rows(perm, src, dst):
    n = src.shape[-1]
    for grp in range(C // RB):
        blk = src[grp * RB:(grp + 1) * RB, :, :].reshape(W2, n)
        out = dot_nn(perm, blk)
        dst[:, grp * RB:(grp + 1) * RB, :] = out.reshape(RB, RB, n).astype(BF16)


def split_cols(v, core):
    lo, hi = v[..., :LANES], v[..., LANES:]
    lane = lax.broadcasted_iota(jnp.int32, lo.shape, lo.ndim - 1)
    axis = lo.ndim - 1
    first = jnp.where(lane < C, lo, pltpu.roll(hi, C, axis))
    second = jnp.where(lane < C, pltpu.roll(lo, C, axis), hi)
    mine = jnp.where(core == 0, first, second)
    other = jnp.where(core == 0, second, first)
    return mine, other


KA = C + RB


def prep_kernel(w_proj, b_proj, ln_in, w_out, b_out, wt_aug, wot_aug, gain, lbias, perm, scr):
    n = gain.shape[-1]
    for k in range(2):
        scr[:] = jnp.zeros_like(scr)
        scr[0:C, 0:5 * C] = w_proj[k].astype(F32)
        scr[C:C + 1, 0:5 * C] = b_proj[pl.ds(k, 1), :]
        wt_aug[k] = (HALF * jnp.transpose(scr[:]))[0:5 * C, 0:KA].astype(BF16)
        scr[:] = jnp.zeros_like(scr)
        scr[0:C, 0:C] = w_out[k].astype(F32)
        scr[C:C + 1, 0:C] = b_out[pl.ds(k, 1), :]
        scr[C + 8:C + 10, 0:C] = ln_in[k]
        small = jnp.transpose(scr[:, 0:LANES])
        wot_aug[k] = (HALF * small)[0:C, 0:KA].astype(BF16)
        gain[k] = jnp.broadcast_to(small[0:C, C + 8:C + 9], (C, n))
        lbias[k] = jnp.broadcast_to(small[0:C, C + 9:C + 10], (C, n))
    r = lax.broadcasted_iota(jnp.int32, (W2, W2), 0)
    q = lax.broadcasted_iota(jnp.int32, (W2, W2), 1)
    perm[:] = jnp.where(q == RB * (r % RB) + r // RB, 1.0, 0.0).astype(BF16)


def prepare(n, ln_in, w_proj, b_proj, w_out, b_out):
    sds = jax.ShapeDtypeStruct
    outs = [sds((2, 5 * C, KA), BF16), sds((2, C, KA), BF16), sds((2, C, n), F32), sds((2, C, n), F32), sds((W2, W2), BF16)]
    args = (w_proj, b_proj.astype(F32), ln_in.astype(F32), w_out, b_out.astype(F32))
    return call(prep_kernel, (1,), [full_spec(v.shape) for v in args], [full_spec(o.shape) for o in outs], outs, [pltpu.VMEM((LANES, 384), F32)], MEGA, MIB)(*args)


def with_ones(zh):
    row = lax.broadcasted_iota(jnp.int32, (RB, zh.shape[-1]), 0)
    return jnp.concatenate([zh, jnp.where(row == 0, 1.0, 0.0).astype(BF16)], axis=0)


def pre_fwd_kernel(split, ids, z, *rest):
    n_mask = 2 if split else 1
    masks = rest[:n_mask]
    wt, gain, lbias, perm = rest[n_mask:n_mask + 4]
    outs, (a_s, b_s) = rest[n_mask + 4:-2], rest[-2:]
    step = pl.program_id(0)

    def row(i, carry):
        zn, _ = norm_rows(z[i].astype(F32))
        zh = (zn * gain[:] + lbias[:]).astype(BF16)
        p = dot_nn(wt[0:4 * C], with_ones(zh))
        m = masks[0][pl.ds(i, 1), :]
        if split:
            m = jnp.where(step < 4, m, masks[1][pl.ds(i, 1), :])
        m = m.astype(F32)
        a_s[i] = ((1.0 + jnp.tanh(p[0:C])) * (p[C:2 * C] * m)).astype(BF16)
        b_s[i] = ((1.0 + jnp.tanh(p[2 * C:3 * C])) * (p[3 * C:4 * C] * m)).astype(BF16)
        return carry

    lax.fori_loop(0, RB, row, 0, unroll=UNROLL)

    def put_a(grp, v):
        outs[0][grp * RB:(grp + 1) * RB] = v.astype(BF16)
        if split:
            mine, other = split_cols(v, ids[1])
            outs[2][grp * RB:(grp + 1) * RB] = mine.astype(BF16)
            outs[3][grp * RB:(grp + 1) * RB] = other.astype(BF16)

    def put_b(grp, v):
        outs[1][grp * RB:(grp + 1) * RB] = v.astype(BF16)

    to_cmajor(perm[:], a_s, put_a)
    to_cmajor(perm[:], b_s, put_b)


def full_spec(shape):
    return pl.BlockSpec(shape, lambda s: (0,) * len(shape))


SMEM_SPEC = pl.BlockSpec(memory_space=pltpu.SMEM)


def peer_map(s):
    return (jnp.minimum(s, 3), 0, 0)


def own_map(s):
    return (jnp.maximum(s - 4, 0), 0, 0)


def call(kernel, grid, in_specs, out_specs, out_shape, scratch, flops, bytes_accessed, trans=0):
    return pl.pallas_call(
        kernel,
        grid=grid,
        in_specs=in_specs,
        out_specs=out_specs,
        out_shape=out_shape,
        scratch_shapes=scratch,
        interpret=INTERPRET,
        cost_estimate=pl.CostEstimate(flops=flops, bytes_accessed=bytes_accessed, transcendentals=trans),
        compiler_params=pltpu.CompilerParams(dimension_semantics=("arbitrary",) * len(grid), vmem_limit_bytes=VMEM_LIMIT),
    )


def peer_map2(s):
    return (jnp.minimum(s, 3), 0)


def own_map2(s):
    return (jnp.maximum(s - 4, 0), 0)


def blk_spec(shape, k):
    return pl.BlockSpec((None,) + tuple(shape[1:]), lambda s: (k,) + (0,) * (len(shape) - 1))


def pre_forward(ids, z, masks, par, blk):
    rows, _, n = z.shape
    split = len(masks) == 2
    mspec = [pl.BlockSpec((RB, n), peer_map2), pl.BlockSpec((RB, n), own_map2)] if split else [pl.BlockSpec((RB, n), lambda s: (s, 0))]
    cspec = pl.BlockSpec((C, RB, n), lambda s: (0, s, 0))
    hspec = pl.BlockSpec((C, RB, LANES), lambda s: (0, s, 0))
    out_shape = [jax.ShapeDtypeStruct((C, rows, n), BF16)] * 2
    out_specs = [cspec] * 2
    if split:
        out_shape = out_shape + [jax.ShapeDtypeStruct((C, rows, LANES), BF16)] * 2
        out_specs = out_specs + [hspec] * 2
    wt, _, gain, lbias, perm = par
    fn = call(
        functools.partial(pre_fwd_kernel, split), (rows // RB,),
        [SMEM_SPEC, pl.BlockSpec((RB, C, n), lambda s: (s, 0, 0))] + mspec + [blk_spec(wt.shape, blk), blk_spec(gain.shape, blk), blk_spec(gain.shape, blk), full_spec((W2, W2))],
        out_specs, out_shape, [pltpu.VMEM((RB, C, n), BF16)] * 2, GIGA * rows // LANES, rows * MIB // 8)
    return fn(ids, z, *masks, wt, gain, lbias, perm)


CB = 8


def global_rows(ids, partner):
    x, c = ids[0], ids[1]
    cc = 1 - c if partner else c
    return pl.multiple_of(C * (2 * (1 - x) + cc), C), pl.multiple_of(C * (2 * x + cc), C)


def place(dst, src_mine, src_other, ids):
    for (peer, own), partner in ((src_mine, False), (src_other, True)):
        off_peer, off_own = global_rows(ids, partner)
        dst[pl.ds(off_peer, C), :] = peer
        dst[pl.ds(off_own, C), :] = own


def halves(ref):
    return ref[0:C, :], ref[C:LANES, :]


def tri_out_kernel(ids, ap, ao, bp, bo, qp, qo, x, full):
    for ch in range(CB):
        buf = full.at[ch % 2]
        place(buf, (bp[ch], bo[ch]), (qp[ch], qo[ch]), ids)
        x[ch] = dot_nt(jnp.concatenate([ap[ch], ao[ch]], axis=0), buf[:])


def tri_in_kernel(ids, ak, ar, b, bp, x):
    xx = ids[0]
    for ch in range(CB):
        out = dot_tn(ak[ch], b[ch]) + dot_tn(ar[ch], bp[ch])
        x[ch, pl.ds(pl.multiple_of(C * (1 - xx), C), C), :] = out[0:C]
        x[ch, pl.ds(pl.multiple_of(C * xx, C), C), :] = out[C:LANES]


def tri_in_bwd_kernel(ids, a, b, dx, dxp, da, db, full):
    for ch in range(CB):
        buf = full.at[ch % 2]
        place(buf, halves(dx.at[ch]), halves(dxp.at[ch]), ids)
        da[ch] = dot_nt(b[ch], buf[:]).astype(BF16)
        db[ch] = dot_nn(a[ch], buf[:]).astype(BF16)


def tri_out_bwd_kernel(ids, dx, bp, bo, qp, qo, dxk, dxr, ap, ao, rp, ro, da, db, full, tmp):
    xx = ids[0]
    for ch in range(CB):
        buf = full.at[ch % 2]
        place(buf, (bp[ch], bo[ch]), (qp[ch], qo[ch]), ids)
        da[ch] = dot_nn(dx[ch], buf[:]).astype(BF16)
        tmp[ch % 2] = dot_tn(dxk[ch], jnp.concatenate([ap[ch], ao[ch]], axis=0)) + dot_tn(dxr[ch], jnp.concatenate([rp[ch], ro[ch]], axis=0))
        db[ch] = tmp[ch % 2, pl.ds(pl.multiple_of(C * xx, C), C), :].astype(BF16)


def tri_call(kernel, ids, args, outs, scratch, flops, own_first=False):
    def cspec(shape, row_blk=0):
        return pl.BlockSpec((CB,) + tuple(shape[1:]), lambda s: (s, row_blk, 0))

    nbytes = sum(v.size * v.dtype.itemsize for v in args) + sum(o.size * o.dtype.itemsize for o in outs)
    return call(kernel, (C // CB,), [SMEM_SPEC] + ([cspec((C, C) + args[0].shape[2:], 1)] if own_first else [cspec(args[0].shape)]) + [cspec(v.shape) for v in args[1:]], [cspec(o.shape) for o in outs], outs, scratch, flops, nbytes)(ids, *args)


def mid_norm(x, xh_s, lnmid, blk, xn_s=None, rstd_s=None):
    tot = x[0]
    for c in range(1, C):
        tot = tot + x[c]
    mean = tot * (1.0 / C)
    d = x[0] - mean
    sq = d * d
    for c in range(1, C):
        d = x[c] - mean
        sq = sq + d * d
    rstd = lax.rsqrt(sq * (1.0 / C) + EPS)
    if rstd_s is not None:
        rstd_s[:] = rstd
    for c in range(C):
        xn = (x[c] - mean) * rstd
        if xn_s is not None:
            xn_s[c] = xn
        xh_s[c] = (xn * lnmid[blk, 0, c] + lnmid[blk, 1, c]).astype(BF16)


def gate_of(zf, wt, gain, lbias):
    zn, _ = norm_rows(zf)
    zh = (zn * gain[:] + lbias[:]).astype(BF16)
    return jnp.tanh(dot_nn(wt[4 * C:5 * C], with_ones(zh)))


def post_fwd_kernel(blk, x, zp, zo, wt, gain, lbias, wot, lnmid, perm, zmid, xh_s, xi_s):
    step = pl.program_id(0)
    mid_norm(x, xh_s, lnmid, blk)
    to_rows(perm[:], xh_s, xi_s)

    def row(i, carry):
        zf = jnp.where(step < 4, zp[i], zo[i]).astype(F32)
        t = gate_of(zf, wt, gain, lbias)
        upd = dot_nn(wot[:], with_ones(xi_s[i]))
        zmid[i] = (zf + (1.0 + t) * upd).astype(BF16)
        return carry

    lax.fori_loop(0, RB, row, 0, unroll=UNROLL)


def post_forward(x0, zp, zo, par, lnmid, blk):
    n = zp.shape[-1]
    wt, wot, gain, lbias, perm = par
    fn = call(
        functools.partial(post_fwd_kernel, blk), (8,),
        [pl.BlockSpec((C, RB, n), lambda s: (0, s, 0)), pl.BlockSpec((RB, C, n), peer_map), pl.BlockSpec((RB, C, n), own_map), blk_spec(wt.shape, blk), blk_spec(gain.shape, blk), blk_spec(gain.shape, blk), blk_spec(wot.shape, blk), SMEM_SPEC, full_spec((W2, W2))],
        [pl.BlockSpec((RB, C, n), lambda s: (s, 0, 0))], [jax.ShapeDtypeStruct((LANES, C, n), BF16)],
        [pltpu.VMEM((C, RB, n), BF16), pltpu.VMEM((RB, C, n), BF16)],
        GIGA, 20 * MIB)
    return fn(x0, zp, zo, wt, gain, lbias, wot, lnmid, perm)[0]


def post_bwd_kernel(second, blk, ids, x, zp, zo, dzp, dzo, wt, gain, lbias, wot, wo, lnmid, perm, *rest):
    if second:
        znew, dx, dpg, acc_bg, acc_bo, acc_wo, acc_mg, acc_mb = rest[:8]
    else:
        dx, dxk, dxs, dpg, acc_bg, acc_bo, acc_wo, acc_mg, acc_mb = rest[:9]
    xh_s, xi_s, dxi_s, dub_s, dxc_s, xn_s, r_s = rest[-7:]
    step = pl.program_id(0)

    @pl.when(step == 0)
    def _():
        for acc in (acc_bg, acc_bo, acc_wo, acc_mg, acc_mb):
            acc[:] = jnp.zeros_like(acc)

    mid_norm(x, xh_s, lnmid, blk, xn_s, r_s)
    to_rows(perm[:], xh_s, xi_s)

    sums = [acc_bg[:], acc_bo[:], acc_wo[:]]

    def gates(i):
        if second:
            zf = zp[i].astype(F32)
            dz = jnp.where(step < 4, dzp[i], dzo[i]).astype(F32)
        else:
            zf = jnp.where(step < 4, zp[i], zo[i]).astype(F32)
            dz = dzp[i].astype(F32)
        t = gate_of(zf, wt, gain, lbias)
        upd = dot_nn(wot[:], with_ones(xi_s[i]))
        t1 = 1.0 + t
        if second:
            znew[i] = (zf + t1 * upd).astype(BF16)
        d_upd = (HALF * dz) * t1
        d_pg = d_upd * (upd * (1.0 - t))
        dpg[i] = d_pg.astype(BF16)
        dub_s[i] = d_upd.astype(BF16)
        sums[0] += fold(d_pg)
        sums[1] += fold(d_upd)

    def products(i):
        dxi_s[i] = dot_nn(wo[:], dub_s[i]).astype(BF16)
        sums[2] += dot_nt(dub_s[i], xi_s[i])

    staggered(gates, products)
    acc_bg[:], acc_bo[:], acc_wo[:] = sums

    def put(grp, v):
        dxc_s[grp * RB:(grp + 1) * RB] = v

    to_cmajor(perm[:], dxi_s, put)
    m1 = m2 = None
    for c in range(C):
        dy = dxc_s[c]
        dyx = dy * xn_s[c]
        gn = lnmid[blk, 0, c]
        m1 = dy * gn if m1 is None else m1 + dy * gn
        m2 = dyx * gn if m2 is None else m2 + dyx * gn
        acc_mg[c] += fold(dyx[0:8] + dyx[8:RB])
        acc_mb[c] += fold(dy[0:8] + dy[8:RB])
    m1 = m1 * (1.0 / C)
    m2 = m2 * (1.0 / C)
    rstd = r_s[:]
    for c in range(C):
        v = (rstd * (dxc_s[c] * lnmid[blk, 0, c] - m1 - xn_s[c] * m2))
        dx[c] = v.astype(BF16)
        if not second:
            mine, other = split_cols(v, ids[1])
            dxk[c] = mine.astype(BF16)
            dxs[c] = other.astype(BF16)


def post_backward(ids, second, x, z_parts, dz_parts, par, w_out, lnmid, blk):
    n = x.shape[-1]
    cspec = pl.BlockSpec((C, RB, n), lambda s: (0, s, 0))
    hspec = pl.BlockSpec((C, RB, LANES), lambda s: (0, s, 0))
    rspec = pl.BlockSpec((RB, C, n), lambda s: (s, 0, 0))
    two = [pl.BlockSpec((RB, C, n), peer_map), pl.BlockSpec((RB, C, n), own_map)]
    one = [rspec, SMEM_SPEC]
    zspec, dzspec = (one, two) if second else (two, one)
    z_args = (z_parts[0], ids) if second else z_parts
    dz_args = dz_parts if second else (dz_parts[0], ids)
    acc_shapes = [(C, LANES), (C, LANES), (C, C), (C, 8, LANES), (C, 8, LANES)]
    accs = [jax.ShapeDtypeStruct(s, F32) for s in acc_shapes]
    acc_specs = [full_spec(s) for s in acc_shapes]
    c_out = jax.ShapeDtypeStruct((C, LANES, n), BF16)
    h_out = jax.ShapeDtypeStruct((C, LANES, LANES), BF16)
    r_out = jax.ShapeDtypeStruct((LANES, C, n), BF16)
    if second:
        outs = [jax.ShapeDtypeStruct((C, C, n), BF16), c_out, r_out]
        ospecs = [pl.BlockSpec((RB, C, n), own_map), cspec, rspec]
    else:
        outs = [c_out, h_out, h_out, r_out]
        ospecs = [cspec, hspec, hspec, rspec]
    wt, wot, gain, lbias, perm = par
    fn = call(
        functools.partial(post_bwd_kernel, second, blk), (8,),
        [SMEM_SPEC, cspec] + zspec + dzspec + [blk_spec(wt.shape, blk), blk_spec(gain.shape, blk), blk_spec(gain.shape, blk), blk_spec(wot.shape, blk), blk_spec(w_out.shape, blk), SMEM_SPEC, full_spec((W2, W2))],
        ospecs + acc_specs, outs + accs,
        [pltpu.VMEM((C, RB, n), BF16), pltpu.VMEM((RB, C, n), BF16), pltpu.VMEM((RB, C, n), BF16), pltpu.VMEM((RB, C, n), BF16), pltpu.VMEM((C, RB, n), F32), pltpu.VMEM((C, RB, n), F32), pltpu.VMEM((RB, n), F32)],
        GIGA, 30 * MIB)
    return fn(ids, x, *z_args, *dz_args, wt, gain, lbias, wot, w_out, lnmid, perm)


def pre_bwd_kernel(two, z, da, db, dpg, drp, dro, mp, mo, wt, w, gain, lbias, perm, dz, acc_w, acc_b, acc_g, acc_lb, dai_s, dbi_s, dp_s, zh_s, zn_s, rs_s):
    step = pl.program_id(0)

    @pl.when(step == 0)
    def _():
        for acc in (acc_w, acc_b, acc_g, acc_lb):
            acc[:] = jnp.zeros_like(acc)

    to_rows(perm[:], da, dai_s)
    to_rows(perm[:], db, dbi_s)

    sums = [acc_w[:], acc_g[:], acc_lb[:]]

    def gates(i):
        zn, rstd = norm_rows(z[i].astype(F32))
        zn_s[i] = zn
        rs_s[i] = jnp.broadcast_to(rstd, (8, rstd.shape[-1]))
        zh = (zn * gain[:] + lbias[:]).astype(BF16)
        zh_s[i] = zh
        p = dot_nn(wt[0:4 * C], with_ones(zh))
        m = mp[pl.ds(i, 1), :]
        if two:
            m = jnp.where(step < 4, m, mo[pl.ds(i, 1), :])
        m = HALF * m.astype(F32)
        for side, ref in ((0, dai_s), (1, dbi_s)):
            base = side * 2 * C
            dm = ref[i].astype(F32) * m
            t = jnp.tanh(p[base:base + C])
            dv = dm * (1.0 + t)
            dg = dv * (p[base + C:base + 2 * C] * (1.0 - t))
            for k, d in ((2 * side, dg), (2 * side + 1, dv)):
                acc_b[k * C:(k + 1) * C] += fold(d)
                dp_s[i, k * C:(k + 1) * C] = d.astype(BF16)
        dp_s[i, 4 * C:5 * C] = dpg[i]

    def products(i):
        dp = dp_s[i]
        dzh = dot_nn(w[:], dp).astype(BF16).astype(F32)
        sums[0] += dot_nt(dp, zh_s[i])
        zn, rstd = zn_s[i], rs_s[i, 0:1, :]
        sums[1] += fold(dzh * zn)
        sums[2] += fold(dzh)
        dzn = dzh * gain[:]
        m1 = jnp.mean(dzn, axis=0, keepdims=True)
        m2 = jnp.mean(dzn * zn, axis=0, keepdims=True)
        dzf = rstd * (dzn - m1 - zn * m2)
        if two:
            dr = jnp.where(step < 4, drp[i], dro[i]).astype(F32)
        else:
            dr = drp[i].astype(F32)
        dz[i] = (dr + dzf).astype(BF16)

    staggered(gates, products)
    acc_w[:], acc_g[:], acc_lb[:] = sums


def pre_backward(ids, z, da, db, dpg, dres_parts, masks, par, w_proj, blk, own_only):
    n = z.shape[-1]
    steps = da.shape[1] // RB
    off = 4 if own_only else 0
    two = len(dres_parts) == 2
    cspec = pl.BlockSpec((C, RB, n), lambda s: (0, s, 0))
    rspec = pl.BlockSpec((RB, C, n), lambda s: (s, 0, 0))
    hspec = pl.BlockSpec((RB, C, n), lambda s: (s + off, 0, 0))
    if two:
        drspec = [pl.BlockSpec((RB, C, n), peer_map), pl.BlockSpec((RB, C, n), own_map)]
        mspec = [pl.BlockSpec((RB, n), peer_map2), pl.BlockSpec((RB, n), own_map2)]
        dr_args, m_args = dres_parts, masks
    else:
        drspec = [hspec, SMEM_SPEC]
        mspec = [pl.BlockSpec((RB, n), lambda s: (s, 0)), SMEM_SPEC]
        dr_args, m_args = (dres_parts[0], ids), (masks[0], ids)
    acc_shapes = [(5 * C, C), (4 * C, LANES), (C, LANES), (C, LANES)]
    wt, _, gain, lbias, perm = par
    fn = call(
        functools.partial(pre_bwd_kernel, two), (steps,),
        [rspec, cspec, cspec, hspec] + drspec + mspec + [blk_spec(wt.shape, blk), blk_spec(w_proj.shape, blk), blk_spec(gain.shape, blk), blk_spec(gain.shape, blk), full_spec((W2, W2))],
        [rspec] + [full_spec(s) for s in acc_shapes],
        [jax.ShapeDtypeStruct((steps * RB, C, n), BF16)] + [jax.ShapeDtypeStruct(s, F32) for s in acc_shapes],
        [pltpu.VMEM((RB, C, n), BF16), pltpu.VMEM((RB, C, n), BF16), pltpu.VMEM((RB, 5 * C, n), BF16), pltpu.VMEM((RB, C, n), BF16), pltpu.VMEM((RB, C, n), F32), pltpu.VMEM((RB, 8, n), F32)],
        GIGA * steps // 8, 30 * MIB * steps // 8)
    return fn(z, da, db, dpg, *dr_args, *m_args, wt, w_proj, gain, lbias, perm)


PACK = 512


def grads_kernel(n_dp, n_dap, w0, b0, q0, g0, l0, wo0, o0, mg0, mb0, w1, b1, q1, g1, l1, wo1, o1, mg1, mb1, out, buf, recv_a, red, recv_b, gath, vec, send_a, rcv_a, send_b, rcv_b, send_c, rcv_c, send_d, rcv_d):
    dp, dap = lax.axis_index("dp"), lax.axis_index("dap")
    big, small = PACK // n_dap, PACK // n_dap // n_dp
    bar = pltpu.get_barrier_semaphore()
    for k in range(1, n_dap):
        pl.semaphore_signal(bar, inc=1, device_id=(dp, lax.rem(dap + k, n_dap)), device_id_type=MESH_ID)
    for k in range(1, n_dp):
        pl.semaphore_signal(bar, inc=1, device_id=(lax.rem(dp + k, n_dp), dap), device_id_type=MESH_ID)

    buf[0:5 * C, 0:C] = w0[:]
    buf[0:5 * C, C:2 * C] = HALF * w1[:]
    buf[5 * C:6 * C, 0:C] = HALF * wo0[:]
    buf[5 * C:6 * C, C:2 * C] = HALF * wo1[:]

    def put(k, base, ref, scale):
        v = ref[:]
        if v.ndim == 3:
            v = jnp.sum(v, axis=1)
        rows = v.shape[0]
        tot = scale * jnp.sum(v, axis=1, keepdims=True)
        lane = lax.broadcasted_iota(jnp.int32, (rows, LANES), 1)
        vec[base:base + rows, :] = jnp.where(lane == k, tot, vec[base:base + rows, :])

    vec[:] = jnp.zeros_like(vec)
    put(0, 0, b0, 1.0)
    put(0, 4 * C, q0, HALF)
    put(1, 0, b1, HALF)
    put(1, 4 * C, q1, HALF)
    for k, (ref, scale) in enumerate(((g0, 1.0), (l0, 1.0), (g1, HALF), (l1, HALF), (mg0, HALF), (mb0, HALF), (mg1, HALF), (mb1, HALF), (o0, HALF), (o1, HALF))):
        put(2 + k, 0, ref, scale)
    vt = jnp.transpose(vec[:])
    for t in range(3):
        buf[6 * C + RB * t:6 * C + RB * t + RB, :] = vt[0:RB, LANES * t:LANES * (t + 1)]
    buf[6 * C + 48:PACK, :] = jnp.zeros((PACK - 6 * C - 48, LANES), F32)

    pl.semaphore_wait(bar, n_dap + n_dp - 2)

    def copies(count, make):
        made = [make(k) for k in range(1, count)]
        for cp in made:
            cp.start()
        return made

    def to_dap(k):
        return (dp, lax.rem(dap + k, n_dap))

    def to_dp(k):
        return (lax.rem(dp + k, n_dp), dap)

    def rows_of(idx, size):
        return pl.ds(pl.multiple_of(idx * size, size), size)

    stage = copies(n_dap, lambda k: pltpu.make_async_remote_copy(buf.at[rows_of(lax.rem(dap + k, n_dap), big)], recv_a.at[k - 1], send_a.at[k - 1], rcv_a.at[k - 1], device_id=to_dap(k), device_id_type=MESH_ID))
    tot = buf[rows_of(dap, big), :]
    for k, cp in enumerate(stage):
        cp.wait_recv()
        tot = tot + recv_a[k]
    red[:] = tot
    for cp in stage:
        cp.wait_send()

    stage = copies(n_dp, lambda k: pltpu.make_async_remote_copy(red.at[rows_of(lax.rem(dp + k, n_dp), small)], recv_b.at[k - 1], send_b.at[k - 1], rcv_b.at[k - 1], device_id=to_dp(k), device_id_type=MESH_ID))
    tot = red[rows_of(dp, small), :]
    for k, cp in enumerate(stage):
        cp.wait_recv()
        tot = tot + recv_b[k]
    gath[rows_of(dp, small), :] = tot
    for cp in stage:
        cp.wait_send()

    mine = gath.at[rows_of(dp, small)]
    stage = copies(n_dp, lambda k: pltpu.make_async_remote_copy(mine, mine, send_c.at[k - 1], rcv_c.at[k - 1], device_id=to_dp(k), device_id_type=MESH_ID))
    for cp in stage:
        cp.wait()

    stage = copies(n_dap, lambda k: pltpu.make_async_remote_copy(gath, out.at[rows_of(dap, big)], send_d.at[k - 1], rcv_d.at[k - 1], device_id=to_dap(k), device_id_type=MESH_ID))
    out[rows_of(dap, big), :] = gath[:]
    for cp in stage:
        cp.wait()


def sum_grads(n_dp, n_dap, parts):
    big, small = PACK // n_dap, PACK // n_dap // n_dp
    dma = pltpu.SemaphoreType.DMA
    return pl.pallas_call(
        functools.partial(grads_kernel, n_dp, n_dap),
        out_shape=jax.ShapeDtypeStruct((PACK, LANES), F32),
        in_specs=[pl.BlockSpec(memory_space=pltpu.VMEM)] * len(parts),
        out_specs=pl.BlockSpec(memory_space=pltpu.VMEM),
        scratch_shapes=[pltpu.VMEM((PACK, LANES), F32), pltpu.VMEM((n_dap - 1, big, LANES), F32), pltpu.VMEM((big, LANES), F32), pltpu.VMEM((max(n_dp - 1, 1), small, LANES), F32), pltpu.VMEM((big, LANES), F32), pltpu.VMEM((384, LANES), F32)]
        + [dma((n_dap - 1,))] * 2 + [dma((max(n_dp - 1, 1),))] * 4 + [dma((n_dap - 1,))] * 2,
        name="grad_sum",
        cost_estimate=pl.CostEstimate(flops=MEGA, bytes_accessed=MIB, transcendentals=0),
        compiler_params=pltpu.CompilerParams(collective_id=0, has_side_effects=True),
    )(*parts)


def unpack_kernel(src, ln_in, gw, bp, lm, gwo, bo):
    t = jnp.transpose(src[0:6 * C, :])
    for k in range(2):
        gw[k] = t[k * C:(k + 1) * C, 0:5 * C]
        gwo[k] = t[k * C:(k + 1) * C, 5 * C:6 * C]
    base = 6 * C
    bp[:, 0:LANES] = src[base:base + 2, :]
    bp[:, LANES:W2] = src[base + RB:base + 18, :]
    bp[:, W2:320] = src[base + 32:base + 34, 0:C]
    for k in range(2):
        ln_in[k] = src[base + 2 + 2 * k:base + 4 + 2 * k, 0:C]
        lm[k] = src[base + 6 + 2 * k:base + 8 + 2 * k, 0:C]
    bo[:] = src[base + 10:base + 12, 0:C]


def unpack(flat):
    outs = [jax.ShapeDtypeStruct(s, F32) for s in ((2, 2, C), (2, C, 5 * C), (2, 5 * C), (2, 2, C), (2, C, C), (2, C))]
    return call(unpack_kernel, (1,), [full_spec(flat.shape)], [full_spec(o.shape) for o in outs], outs, [], MEGA, MIB)(flat)


SUM = sum_grads


def solution(mesh):
    def plan(z_pair, pair_mask, dz_out, ln_in, w_proj, b_proj, ln_mid, w_out, b_out):
        n = z_pair.shape[2]
        dap = lax.axis_index("dap")
        ids = jnp.stack([dap // 2, dap % 2]).astype(jnp.int32)
        x_pairs = [(0, 2), (2, 0), (1, 3), (3, 1)]
        c_pairs = [(0, 1), (1, 0), (2, 3), (3, 2)]

        def over_x(v):
            return lax.ppermute(v, "dap", x_pairs)

        def over_c(v):
            return lax.ppermute(v, "dap", c_pairs)

        par = prepare(n, ln_in, w_proj, b_proj, w_out, b_out)
        lnmid = ln_mid.astype(F32)
        m_own = pair_mask[0]
        z_own = jnp.transpose(z_pair[0], (0, 2, 1))
        dz_own = jnp.transpose(dz_out[0], (0, 2, 1))
        m_peer = over_x(m_own)
        z_peer = over_x(z_own)
        z_peer, dz_src = lax.optimization_barrier((z_peer, dz_own))
        dz_peer = over_x(dz_src)
        masks = (m_peer, m_own)

        sds = jax.ShapeDtypeStruct
        full = pltpu.VMEM((2, n, n), BF16)
        ao, bo = pre_forward(ids, z_own, (m_own,), par, 0)
        qo, ro = over_c(bo), over_c(ao)
        ap, bp = pre_forward(ids, z_peer, (m_peer,), par, 0)
        qp, rp = over_c(bp), over_c(ap)
        (x0,) = tri_call(tri_out_kernel, ids, (ap, ao, bp, bo, qp, qo), [sds((C, LANES, n), F32)], [full], GIGA)
        z_mid = post_forward(x0, z_peer, z_own, par, lnmid, 0)
        a1, b1, a1k, a1s = pre_forward(ids, z_mid, masks, par, 1)
        a1r = over_c(a1s)
        b1p = over_c(b1)
        (x1,) = tri_call(tri_in_kernel, ids, (a1k, a1r, b1, b1p), [sds((C, LANES, n), F32)], [], GIGA)
        z_new, dx1, dpg1, bg1, bo1, wo1, mg1, mb1 = post_backward(ids, True, x1, (z_mid,), (dz_peer, dz_own), par, w_out, lnmid, 1)
        dx1p = over_c(dx1)
        da1, db1 = tri_call(tri_in_bwd_kernel, ids, (a1, b1, dx1, dx1p), [sds((C, LANES, n), BF16)] * 2, [full], GIGA)
        dz_mid, w1, b1s, g1, lb1 = pre_backward(ids, z_mid, da1, db1, dpg1, (dz_peer, dz_own), masks, par, w_proj, 1, False)
        dx0, dx0k, dx0s, dpg0, bg0, bo0, wo0, mg0, mb0 = post_backward(ids, False, x0, (z_peer, z_own), (dz_mid,), par, w_out, lnmid, 0)
        dx0r = over_c(dx0s)
        da0, db0 = tri_call(tri_out_bwd_kernel, ids, (dx0, bp, bo, qp, qo, dx0k, dx0r, ap, ao, rp, ro), [sds((C, C, n), BF16)] * 2, [full, pltpu.VMEM((2, LANES, n), F32)], GIGA, own_first=True)
        dz, w0, b0s, g0, lb0 = pre_backward(ids, z_own, da0, db0, dpg0, (dz_mid,), (m_own,), par, w_proj, 0, True)

        flat = SUM(mesh.shape["dp"], mesh.shape["dap"], (w0, b0s, bg0, g0, lb0, wo0, bo0, mg0, mb0, w1, b1s, bg1, g1, lb1, wo1, bo1, mg1, mb1))
        g_ln_in, gw, g_bp, g_lm, gwo, g_bo = unpack(flat)
        z_res = jnp.transpose(z_new, (0, 2, 1))[None]
        dz_res = jnp.transpose(dz, (0, 2, 1))[None]
        return z_res, dz_res, g_ln_in, gw, g_bp, g_lm, gwo, g_bo

    row_spec = P("dp", "dap")
    return jax.shard_map(plan, mesh=mesh, in_specs=(row_spec, row_spec, row_spec, P(), P(), P(), P(), P(), P()), out_specs=(row_spec, row_spec, P(), P(), P(), P(), P(), P()), check_vma=False)
```

profile of v0, /device:TPU:0, one launch (start us, length us, event | category | flops | bytes accessed | tf_op | source)
XLA Modules:
  0.0 293.2 jit_solution(4293880527171882823)
XLA Ops:
  0.6 3.0 %collective-permute-start = (bf16[64,64,256]{2,1,0:T(8,128)(2,1)}, bf16[64,64,256]{2,1,0:T(8,128)(2,1)S(1)}, u32[]{:S(2)}, u32[]{:S(2)}) collective-permute-start(bf16[64,64,256]{2,1,0:T(8,128)(2,1)} %bitcast.15), channel_id=1, source_target_pairs={{0,2},{2,0},{1,3},{3,1},{4,6},{6,4},{5,7},{7,5},{8,10},{10,8},{9,1... | collective-permute-start | bytes 6291464 | tf_op jit(solution)/shard_map/ppermute | solution.py:651
  3.7 0.1 collective-permute-start.1
  3.7 0.6 pad_add_fusion.ids.zo.dzo.dro.mo
  4.3 1.3 convert_element_type.12.b_proj
  5.6 1.3 convert_element_type.13.ln_in
  6.8 1.2 convert_element_type.14.b_out
  8.1 1.9 shard_map.152
  10.0 0.0 copy-start.10
  10.0 7.4 %shard_map.154 = (bf16[64,64,256]{2,1,0:T(8,128)(2,1)}, bf16[64,64,256]{2,1,0:T(8,128)(2,1)}) custom-call(s32[2]{0:T(128)} %pad_add_fusion.ids.zo.dzo.dro.mo, bf16[64,64,256]{2,1,0:T(8,128)(2,1)} %bitcast.16, s32[64,256]{1,0:T(8,128)} %bitcast.24, bf16[2,320,80]{2,1,0:T(8,128)(2,1)} %get-tuple-element.61.rest_1_.wt.rest_2_, ...), custom_call_target="tpu_custom_call" | custom-call | flops 500000000 | bytes 8388608 | tf_op jit(solution)/shard_map/pallas_call | solution.py:217
  17.4 0.0 collective-permute-start.3
  17.4 32.8 %collective-permute-done.z.zp = bf16[64,64,256]{2,1,0:T(8,128)(2,1)S(1)} collective-permute-done((bf16[64,64,256]{2,1,0:T(8,128)(2,1)}, bf16[64,64,256]{2,1,0:T(8,128)(2,1)S(1)}, u32[]{:S(2)}, u32[]{:S(2)}) %collective-permute-start) | collective-permute-done | bytes 2097184 | tf_op jit(solution)/shard_map/ppermute | solution.py:651
  50.2 0.0 copy-start
  50.2 0.7 collective-permute-done.1.rest_0_.mp
  50.9 0.6 copy-done
  51.5 0.0 copy-start.9
  51.5 0.6 copy-done.9
  52.2 7.3 %shard_map.153 = (bf16[64,64,256]{2,1,0:T(8,128)(2,1)}, bf16[64,64,256]{2,1,0:T(8,128)(2,1)}) custom-call(s32[2]{0:T(128)} %pad_add_fusion.ids.zo.dzo.dro.mo, bf16[64,64,256]{2,1,0:T(8,128)(2,1)} %copy-done, s32[64,256]{1,0:T(8,128)} %copy-done.9, bf16[2,320,80]{2,1,0:T(8,128)(2,1)} %get-tuple-element.61.rest_1_.wt.rest_2_, ...), custom_call_target="tpu_custom_call" | custom-call | flops 500000000 | bytes 8388608 | tf_op jit(solution)/shard_map/pallas_call | solution.py:217
  59.5 0.0 collective-permute-start.2
  59.5 0.0 copy-done.10
  59.5 0.6 convert_element_type.15.lnmid
  60.1 0.0 collective-permute-done.3.qo
  60.1 0.0 copy-start.3
  60.1 3.8 %collective-permute-done.2.qp = bf16[64,64,256]{2,1,0:T(8,128)(2,1)S(1)} collective-permute-done((bf16[64,64,256]{2,1,0:T(8,128)(2,1)}, bf16[64,64,256]{2,1,0:T(8,128)(2,1)S(1)}, u32[]{:S(2)}, u32[]{:S(2)}) %collective-permute-start.2) | collective-permute-done | bytes 2097184 | tf_op jit(solution)/shard_map/ppermute | solution.py:654
  63.9 0.0 copy-start.5
  63.9 0.0 copy-done.3
  63.9 1.3 copy-done.5
  65.2 11.3 %shard_map.155.x = f32[64,128,256]{2,1,0:T(8,128)} custom-call(s32[2]{0:T(128)} %pad_add_fusion.ids.zo.dzo.dro.mo, bf16[64,64,256]{2,1,0:T(8,128)(2,1)} %get-tuple-element.65.ap, bf16[64,64,256]{2,1,0:T(8,128)(2,1)} %get-tuple-element.66.ao, bf16[64,64,256]{2,1,0:T(8,128)(2,1)} %get-tuple-element.67.bp, bf16[64,64,256]{2,1,0:T(8,128)(2,1)} %get-tuple-element.68.bo, ...), custom_call_target="tpu_custom_call" | custom-call | flops 1000000000 | bytes 20971520 | tf_op jit(solution)/shard_map/pallas_call | solution.py:278
  76.5 13.4 %shard_map.156.z.zp = bf16[128,64,256]{2,1,0:T(8,128)(2,1)} custom-call(f32[64,128,256]{2,1,0:T(8,128)} %shard_map.155.x, bf16[64,64,256]{2,1,0:T(8,128)(2,1)} %copy-done, bf16[64,64,256]{2,1,0:T(8,128)(2,1)} %bitcast.17, bf16[2,320,80]{2,1,0:T(8,128)(2,1)} %get-tuple-element.61.rest_1_.wt.rest_2_, f32[2,64,256]{2,1,0:T(8,128)} %get-tuple-element.62.rest_2_.gain.rest_3_, ...), custom_call_target="tpu_custom_call" | custom-call | flops 1000000000 | bytes 20971520 | tf_op jit(solution)/shard_map/pallas_call | solution.py:331
  89.9 0.0 copy-start.1
  89.9 13.3 %shard_map.157 = (bf16[64,128,256]{2,1,0:T(8,128)(2,1)}, bf16[64,128,256]{2,1,0:T(8,128)(2,1)}, bf16[64,128,128]{2,1,0:T(8,128)(2,1)}, bf16[64,128,128]{2,1,0:T(8,128)(2,1)}) custom-call(s32[2]{0:T(128)} %pad_add_fusion.ids.zo.dzo.dro.mo, bf16[128,64,256]{2,1,0:T(8,128)(2,1)} %shard_map.156.z.zp, s32[64,256]{1,0:T(8,128)} %copy-done.9, s32[64,256]{1,0:T(8,128)} %bitcast.25, ...), custom_call_target="tpu_custom_call" | custom-call | flops 1000000000 | bytes 16777216 | tf_op jit(solution)/shard_map/pallas_call | solution.py:217
  103.2 0.2 collective-permute-start.5
  103.4 0.4 collective-permute-start.4
  103.7 0.0 copy-done.1
  103.7 1.7 collective-permute-start.6
  105.5 8.1 %collective-permute-done.4.ar = bf16[64,128,128]{2,1,0:T(8,128)(2,1)S(1)} collective-permute-done((bf16[64,128,128]{2,1,0:T(8,128)(2,1)}, bf16[64,128,128]{2,1,0:T(8,128)(2,1)S(1)}, u32[]{:S(2)}, u32[]{:S(2)}) %collective-permute-start.4) | collective-permute-done | bytes 2097184 | tf_op jit(solution)/shard_map/ppermute | solution.py:654
  113.6 0.0 copy-start.7
  113.6 0.0 collective-permute-done.5.bp
  113.6 1.3 copy-done.7
  114.9 0.0 copy-start.6
  114.9 2.0 copy-done.6
  116.9 11.2 %shard_map.158.x = f32[64,128,256]{2,1,0:T(8,128)} custom-call(s32[2]{0:T(128)} %pad_add_fusion.ids.zo.dzo.dro.mo, bf16[64,128,128]{2,1,0:T(8,128)(2,1)} %get-tuple-element.70.ak, bf16[64,128,128]{2,1,0:T(8,128)(2,1)} %copy-done.7, bf16[64,128,256]{2,1,0:T(8,128)(2,1)} %get-tuple-element.72.b, bf16[64,128,256]{2,1,0:T(8,128)(2,1)} %copy-done.6), custom_call_target="tpu_custom_call" | custom-call | flops 1000000000 | bytes 20971520 | tf_op jit(solution)/shard_map/pallas_call | solution.py:278
  128.1 0.0 copy-start.2
  128.1 0.0 copy-start.4
  128.1 23.4 %collective-permute-done.6.dzp.drp = bf16[64,64,256]{2,1,0:T(8,128)(2,1)} collective-permute-done((bf16[64,64,256]{2,1,0:T(8,128)(2,1)S(1)}, bf16[64,64,256]{2,1,0:T(8,128)(2,1)}, u32[]{:S(2)}, u32[]{:S(2)}) %collective-permute-start.6) | collective-permute-done | bytes 2097184 | tf_op jit(solution)/shard_map/ppermute | solution.py:651
  151.5 21.2 %shard_map.159 = (bf16[64,64,256]{2,1,0:T(8,128)(2,1)}, bf16[64,128,256]{2,1,0:T(8,128)(2,1)}, bf16[128,64,256]{2,1,0:T(8,128)(2,1)}, f32[64,128]{1,0:T(8,128)},...) custom-call(s32[2]{0:T(128)} %pad_add_fusion.ids.zo.dzo.dro.mo, ...), custom_call_target="tpu_custom_call" | custom-call | flops 1000000000 | bytes 31457280 | tf_op jit(solution)/shard_map/pallas_call | solution.py:432
  172.8 0.1 collective-permute-start.7
  172.8 0.0 copy-done.2
  172.9 0.5 collective-permute-start.10
  173.3 0.0 copy-done.4
  173.3 0.1 collective-permute-start.9
  173.4 6.9 %collective-permute-done.7.dxp = bf16[64,128,256]{2,1,0:T(8,128)(2,1)} collective-permute-done((bf16[64,128,256]{2,1,0:T(8,128)(2,1)}, bf16[64,128,256]{2,1,0:T(8,128)(2,1)}, u32[]{:S(2)}, u32[]{:S(2)}) %collective-permute-start.7) | collective-permute-done | bytes 4194336 | tf_op jit(solution)/shard_map/ppermute | solution.py:654
  180.3 12.5 %shard_map.160 = (bf16[64,128,256]{2,1,0:T(8,128)(2,1)}, bf16[64,128,256]{2,1,0:T(8,128)(2,1)}) custom-call(s32[2]{0:T(128)} %pad_add_fusion.ids.zo.dzo.dro.mo, bf16[64,128,256]{2,1,0:T(8,128)(2,1)} %get-tuple-element.75.a, bf16[64,128,256]{2,1,0:T(8,128)(2,1)} %get-tuple-element.72.b, bf16[64,128,256]{2,1,0:T(8,128)(2,1)} %get-tuple-element.76.dx, ...), custom_call_target="tpu_custom_call" | custom-call | flops 1000000000 | bytes 25165824 | tf_op jit(solution)/shard_map/pallas_call | solution.py:278
  192.8 22.7 %shard_map.161 = (bf16[128,64,256]{2,1,0:T(8,128)(2,1)}, f32[320,64]{1,0:T(8,128)}, f32[256,128]{1,0:T(8,128)}, f32[64,128]{1,0:T(8,128)}, f32[64,128]{1,0:T(8,128)}) custom-call(bf16[128,64,256]{2,1,0:T(8,128)(2,1)} %shard_map.156.z.zp, bf16[64,128,256]{2,1,0:T(8,128)(2,1)} %get-tuple-element.77.da, bf16[64,128,256]{2,1,0:T(8,128)(2,1)} %get-tuple-element.78.db, ...), custom_call_target="tpu_custom_call" | custom-call | flops 1000000000 | bytes 31457280 | tf_op jit(solution)/shard_map/pallas_call | solution.py:516
  215.6 23.2 %shard_map.162 = (bf16[64,128,256]{2,1,0:T(8,128)(2,1)}, bf16[64,128,128]{2,1,0:T(8,128)(2,1)}, bf16[64,128,128]{2,1,0:T(8,128)(2,1)}, bf16[128,64,256]{2,1,0:T(...) custom-call(s32[2]{0:T(128)} %pad_add_fusion.ids.zo.dzo.dro.mo, ...), custom_call_target="tpu_custom_call" | custom-call | flops 1000000000 | bytes 31457280 | tf_op jit(solution)/shard_map/pallas_call | solution.py:432
  238.8 0.2 collective-permute-start.8
  239.0 0.0 collective-permute-done.10.ro
  239.0 0.0 copy-start.8
  239.0 0.0 collective-permute-done.9.rp
  239.0 4.3 %collective-permute-done.8.dxr = bf16[64,128,128]{2,1,0:T(8,128)(2,1)} collective-permute-done((bf16[64,128,128]{2,1,0:T(8,128)(2,1)}, bf16[64,128,128]{2,1,0:T(8,128)(2,1)}, u32[]{:S(2)}, u32[]{:S(2)}) %collective-permute-start.8) | collective-permute-done | bytes 2097184 | tf_op jit(solution)/shard_map/ppermute | solution.py:654
  243.4 0.0 copy-done.8
  243.4 12.1 %shard_map.163 = (bf16[64,64,256]{2,1,0:T(8,128)(2,1)}, bf16[64,64,256]{2,1,0:T(8,128)(2,1)}) custom-call(s32[2]{0:T(128)} %pad_add_fusion.ids.zo.dzo.dro.mo, bf16[64,128,256]{2,1,0:T(8,128)(2,1)} %get-tuple-element.81.dx, bf16[64,64,256]{2,1,0:T(8,128)(2,1)} %get-tuple-element.67.bp, bf16[64,64,256]{2,1,0:T(8,128)(2,1)} %get-tuple-element.68.bo, ...), custom_call_target="tpu_custom_call" | custom-call | flops 1000000000 | bytes 29360128 | tf_op jit(solution)/shard_map/pallas_call | solution.py:278
  255.5 12.6 %shard_map.164 = (bf16[64,64,256]{2,1,0:T(8,128)(2,1)}, f32[320,64]{1,0:T(8,128)}, f32[256,128]{1,0:T(8,128)}, f32[64,128]{1,0:T(8,128)}, f32[64,128]{1,0:T(8,128)}) custom-call(bf16[64,64,256]{2,1,0:T(8,128)(2,1)} %bitcast.19, bf16[64,64,256]{2,1,0:T(8,128)(2,1)} %get-tuple-element.84.da, bf16[64,64,256]{2,1,0:T(8,128)(2,1)} %get-tuple-element.85.db, ...), custom_call_target="tpu_custom_call" | custom-call | flops 500000000 | bytes 15728640 | tf_op jit(solution)/shard_map/pallas_call | solution.py:516
  268.0 23.3 %grad_sum.1.src = f32[512,128]{1,0:T(8,128)} custom-call(f32[320,64]{1,0:T(8,128)} %get-tuple-element.88.w0, f32[256,128]{1,0:T(8,128)} %get-tuple-element.89.b0, f32[64,128]{1,0:T(8,128)} %get-tuple-element.90.q0, f32[64,128]{1,0:T(8,128)} %get-tuple-element.91.g0, f32[64,128]{1,0:T(8,128)} %get-tuple-element.92.l0, f32[64,64]{1,0:T(8,128)} %get-tuple-element.93.wo0, ...), custom_call_target="tpu_custom_call" | custom-call | flops 1000000 | bytes 1048576 | tf_op jit(solution)/shard_map/grad_sum/pallas_call | solution.py:606
  291.4 1.8 shard_map.165
Async XLA Ops:
  0.6 49.6 %collective-permute-start = (bf16[64,64,256]{2,1,0:T(8,128)(2,1)}, bf16[64,64,256]{2,1,0:T(8,128)(2,1)S(1)}, u32[]{:S(2)}, u32[]{:S(2)}) collective-permute-start(bf16[64,64,256]{2,1,0:T(8,128)(2,1)} %bitcast.15), channel_id=1, source_target_pairs={{0,2},{2,0},{1,3},{3,1},{4,6},{6,4},{5,7},{7,5},{8,10},{10,8},{9,1... | collective-permute-start | bytes 6291464 | tf_op jit(solution)/shard_map/ppermute | solution.py:651
  3.7 47.2 %collective-permute-start.1 = (s32[64,256]{1,0:T(8,128)}, s32[64,256]{1,0:T(8,128)S(1)}, u32[]{:S(2)}, u32[]{:S(2)}) collective-permute-start(s32[64,256]{1,0:T(8,128)} %bitcast.23), channel_id=1, source_target_pairs={{0,2},{2,0},{1,3},{3,1},{4,6},{6,4},{5,7},{7,5},{8,10},{10,8},{9,1... | collective-permute-start | bytes 196616 | tf_op jit(solution)/shard_map/ppermute | solution.py:651
  10.0 49.5 %copy-start.10 = (bf16[2,2,64]{2,1,0:T(2,128)(2,1)S(1)}, bf16[2,2,64]{2,1,0:T(2,128)(2,1)}, u32[]{:S(2)}) copy-start(bf16[2,2,64]{2,1,0:T(2,128)(2,1)} %param.15) | copy-start | bytes 1540
  17.4 42.7 %collective-permute-start.3 = (bf16[64,64,256]{2,1,0:T(8,128)(2,1)}, bf16[64,64,256]{2,1,0:T(8,128)(2,1)S(1)}, u32[]{:S(2)}, u32[]{:S(2)}) collective-permute-start(bf16[64,64,256]{2,1,0:T(8,128)(2,1)} %get-tuple-element.68.bo), channel_id=1, source_target_pairs={{0,1},{1,0},{2,3},{3,2},{4,5},{5,4},{6,7},{7,6},{8,9},{9,8},{10,11... | collective-permute-start | bytes 6291464 | tf_op jit(solution)/shard_map/ppermute | solution.py:654
  50.2 1.3 copy-start
  51.5 0.6 copy-start.9
  59.5 4.4 %collective-permute-start.2 = (bf16[64,64,256]{2,1,0:T(8,128)(2,1)}, bf16[64,64,256]{2,1,0:T(8,128)(2,1)S(1)}, u32[]{:S(2)}, u32[]{:S(2)}) collective-permute-start(bf16[64,64,256]{2,1,0:T(8,128)(2,1)} %get-tuple-element.67.bp), channel_id=1, source_target_pairs={{0,1},{1,0},{2,3},{3,2},{4,5},{5,4},{6,7},{7,6},{8,9},{9,8},{10,11... | collective-permute-start | bytes 6291464 | tf_op jit(solution)/shard_map/ppermute | solution.py:654
  60.1 3.8 %copy-start.3 = (bf16[64,64,256]{2,1,0:T(8,128)(2,1)}, bf16[64,64,256]{2,1,0:T(8,128)(2,1)S(1)}, u32[]{:S(2)}) copy-start(bf16[64,64,256]{2,1,0:T(8,128)(2,1)S(1)} %collective-permute-done.3.qo) | copy-start | bytes 6291460
  63.9 1.3 copy-start.5
  89.9 13.9 %copy-start.1 = (bf16[1,64,256,64]{2,3,1,0:T(8,128)(2,1)S(1)}, bf16[1,64,256,64]{2,3,1,0:T(8,128)(2,1)}, u32[]{:S(2)}) copy-start(bf16[1,64,256,64]{2,3,1,0:T(8,128)(2,1)} %param.11) | copy-start | bytes 6291460
  103.2 10.4 %collective-permute-start.5 = (bf16[64,128,256]{2,1,0:T(8,128)(2,1)}, bf16[64,128,256]{2,1,0:T(8,128)(2,1)S(1)}, u32[]{:S(2)}, u32[]{:S(2)}) collective-permute-start(bf16[64,128,256]{2,1,0:T(8,128)(2,1)} %get-tuple-element.72.b), channel_id=1, source_target_pairs={{0,1},{1,0},{2,3},{3,2},{4,5},{5,4},{6,7},{7,6},{8,9},{9,8},{10,11... | collective-permute-start | bytes 12582920 | tf_op jit(solution)/shard_map/ppermute | solution.py:654
  103.4 10.2 %collective-permute-start.4 = (bf16[64,128,128]{2,1,0:T(8,128)(2,1)}, bf16[64,128,128]{2,1,0:T(8,128)(2,1)S(1)}, u32[]{:S(2)}, u32[]{:S(2)}) collective-permute-start(bf16[64,128,128]{2,1,0:T(8,128)(2,1)} %get-tuple-element.71), channel_id=1, source_target_pairs={{0,1},{1,0},{2,3},{3,2},{4,5},{5,4},{6,7},{7,6},{8,9},{9,8},{10,11... | collective-permute-start | bytes 6291464 | tf_op jit(solution)/shard_map/ppermute | solution.py:654
  103.7 47.8 %collective-permute-start.6 = (bf16[64,64,256]{2,1,0:T(8,128)(2,1)S(1)}, bf16[64,64,256]{2,1,0:T(8,128)(2,1)}, u32[]{:S(2)}, u32[]{:S(2)}) collective-permute-start(bf16[64,64,256]{2,1,0:T(8,128)(2,1)S(1)} %bitcast.22), channel_id=1, source_target_pairs={{0,2},{2,0},{1,3},{3,1},{4,6},{6,4},{5,7},{7,5},{8,10},{10,8},{9,1... | collective-permute-start | bytes 6291464 | tf_op jit(solution)/shard_map/ppermute | solution.py:651
  113.6 1.3 copy-start.7
  114.9 2.0 copy-start.6
  128.1 44.7 %copy-start.2 = (bf16[64,64,256]{2,1,0:T(8,128)(2,1)S(1)}, bf16[64,64,256]{2,1,0:T(8,128)(2,1)}, u32[]{:S(2)}) copy-start(bf16[64,64,256]{2,1,0:T(8,128)(2,1)} %get-tuple-element.66.ao) | copy-start | bytes 6291460
  128.1 45.2 %copy-start.4 = (bf16[64,64,256]{2,1,0:T(8,128)(2,1)S(1)}, bf16[64,64,256]{2,1,0:T(8,128)(2,1)}, u32[]{:S(2)}) copy-start(bf16[64,64,256]{2,1,0:T(8,128)(2,1)} %get-tuple-element.65.ap) | copy-start | bytes 6291460
  172.8 7.6 %collective-permute-start.7 = (bf16[64,128,256]{2,1,0:T(8,128)(2,1)}, bf16[64,128,256]{2,1,0:T(8,128)(2,1)}, u32[]{:S(2)}, u32[]{:S(2)}) collective-permute-start(bf16[64,128,256]{2,1,0:T(8,128)(2,1)} %get-tuple-element.76.dx), channel_id=1, source_target_pairs={{0,1},{1,0},{2,3},{3,2},{4,5},{5,4},{6,7},{7,6},{8,9},{9,8},{10,11... | collective-permute-start | bytes 12582920 | tf_op jit(solution)/shard_map/ppermute | solution.py:654
  172.9 66.2 %collective-permute-start.10 = (bf16[64,64,256]{2,1,0:T(8,128)(2,1)S(1)}, bf16[64,64,256]{2,1,0:T(8,128)(2,1)S(1)}, u32[]{:S(2)}, u32[]{:S(2)}) collective-permute-start(bf16[64,64,256]{2,1,0:T(8,128)(2,1)S(1)} %copy-done.2), channel_id=1, source_target_pairs={{0,1},{1,0},{2,3},{3,2},{4,5},{5,4},{6,7},{7,6},{8,9},{9,8},{10,11... | collective-permute-start | bytes 6291464 | tf_op jit(solution)/shard_map/ppermute | solution.py:654
  173.3 65.7 %collective-permute-start.9 = (bf16[64,64,256]{2,1,0:T(8,128)(2,1)S(1)}, bf16[64,64,256]{2,1,0:T(8,128)(2,1)}, u32[]{:S(2)}, u32[]{:S(2)}) collective-permute-start(bf16[64,64,256]{2,1,0:T(8,128)(2,1)S(1)} %copy-done.4), channel_id=1, source_target_pairs={{0,1},{1,0},{2,3},{3,2},{4,5},{5,4},{6,7},{7,6},{8,9},{9,8},{10,11... | collective-permute-start | bytes 6291464 | tf_op jit(solution)/shard_map/ppermute | solution.py:654
  238.8 4.6 %collective-permute-start.8 = (bf16[64,128,128]{2,1,0:T(8,128)(2,1)}, bf16[64,128,128]{2,1,0:T(8,128)(2,1)}, u32[]{:S(2)}, u32[]{:S(2)}) collective-permute-start(bf16[64,128,128]{2,1,0:T(8,128)(2,1)} %get-tuple-element.83), channel_id=1, source_target_pairs={{0,1},{1,0},{2,3},{3,2},{4,5},{5,4},{6,7},{7,6},{8,9},{9,8},{10,11... | collective-permute-start | bytes 6291464 | tf_op jit(solution)/shard_map/ppermute | solution.py:654
  239.0 4.4 %copy-start.8 = (bf16[64,64,256]{2,1,0:T(8,128)(2,1)}, bf16[64,64,256]{2,1,0:T(8,128)(2,1)S(1)}, u32[]{:S(2)}) copy-start(bf16[64,64,256]{2,1,0:T(8,128)(2,1)S(1)} %collective-permute-done.10.ro) | copy-start | bytes 6291460
where the time goes:
time: 295 us; the launch traced here: 293 us
  Pallas kernels  195 us (66%)
  waiting for transfers between devices  80.1 us (27%)
  starting transfers between devices  6.26 us (2%)
  local copies, waits for them, and re-layouts  5.88 us (2%)
  other arithmetic  4.9 us (2%)
    ppermute x3, waiting for transfers between devices, over_x(): return lax.ppermute(v, 'dap', x_pairs)  57 us
    pallas_call x4, Pallas kernels, tri_call(): call(kernel, (C // CB,), [SMEM_SPEC] + ([cspec((C, C) + args[0].shape[2:]...  47.1 us
    pallas_call x2, Pallas kernels, post_backward(): fn(ids, x, *z_args, *dz_args, wt, gain, lbias, wot, w_out, lnmid, perm)  44.4 us
    pallas_call x2, Pallas kernels, pre_backward(): return fn(z, da, db, dpg, *dr_args, *m_args, wt, w_proj, gain, lbias, perm)  35.3 us
    pallas_call x3, Pallas kernels, pre_forward(): return fn(ids, z, *masks, wt, gain, lbias, perm)  28 us
    pallas_call x1, Pallas kernels, sum_grads(): pl.pallas_call(functools.partial(grads_kernel, n_dp, n_dap), out_shape=ja...  23.3 us
    ppermute x8, waiting for transfers between devices, over_c(): return lax.ppermute(v, 'dap', c_pairs)  23.1 us
    pallas_call x1, Pallas kernels, post_forward(): return fn(x0, zp, zo, wt, gain, lbias, wot, lnmid, perm)[0]  13.4 us
  transfers between devices with their start and end apart: 11, of which 7 were waited for; matrix products, arithmetic and copies ran while one was open for 2% of the time, Pallas kernels for 29%

commit v1 on v0

v1 whole, which is shorter than its diff:
```python
import functools

import jax
import jax.numpy as jnp
from jax import lax
from jax.experimental import pallas as pl
from jax.experimental.pallas import tpu as pltpu
from jax.sharding import PartitionSpec as P


EPS = 1e-5
F32 = jnp.float32
BF16 = jnp.bfloat16
INTERPRET = False
C = 64
RB = 16
DELAY = 4
LANES = 128
W2 = 256
HALF = 0.5
MEGA = 10 ** 6
GIGA = 10 ** 9
MIB = 2 ** 20
VMEM_LIMIT = 56 * 1024 * 1024


MESH_ID = pl.DeviceIdType.MESH


def dot_nn(a, b):
    return lax.dot_general(a, b, (((1,), (0,)), ((), ())), preferred_element_type=F32)


def dot_nt(a, b):
    return lax.dot_general(a, b, (((1,), (1,)), ((), ())), preferred_element_type=F32)


def dot_tn(a, b):
    return lax.dot_general(a, b, (((0,), (0,)), ((), ())), preferred_element_type=F32)


def norm_rows(zf):
    mean = jnp.mean(zf, axis=0, keepdims=True)
    cen = zf - mean
    var = jnp.mean(cen * cen, axis=0, keepdims=True)
    rstd = lax.rsqrt(var + EPS)
    return cen * rstd, rstd


def staggered(first, second):
    for i in range(RB + DELAY):
        if i < RB:
            first(i)
        if i >= DELAY:
            second(i - DELAY)


def fold(v):
    return v[:, :LANES] + v[:, LANES:]


def to_cmajor(perm, src, dst):
    n = src.shape[-1]
    for grp in range(C // RB):
        blk = src[:, grp * RB:(grp + 1) * RB, :].reshape(W2, n)
        out = dot_nn(perm, blk)
        dst(grp, out.reshape(RB, RB, n))


def to_rows(perm, src, dst):
    n = src.shape[-1]
    for grp in range(C // RB):
        blk = src[grp * RB:(grp + 1) * RB, :, :].reshape(W2, n)
        out = dot_nn(perm, blk)
        dst[:, grp * RB:(grp + 1) * RB, :] = out.reshape(RB, RB, n).astype(BF16)


def split_cols(v, core):
    lo, hi = v[..., :LANES], v[..., LANES:]
    lane = lax.broadcasted_iota(jnp.int32, lo.shape, lo.ndim - 1)
    axis = lo.ndim - 1
    first = jnp.where(lane < C, lo, pltpu.roll(hi, C, axis))
    second = jnp.where(lane < C, pltpu.roll(lo, C, axis), hi)
    mine = jnp.where(core == 0, first, second)
    other = jnp.where(core == 0, second, first)
    return mine, other


KA = C + RB


def prep_kernel(w_proj, b_proj, ln_in, w_out, b_out, wt_aug, wot_aug, gain, lbias, perm, scr):
    n = gain.shape[-1]
    for k in range(2):
        scr[:] = jnp.zeros_like(scr)
        scr[0:C, 0:5 * C] = w_proj[k].astype(F32)
        scr[C:C + 1, 0:5 * C] = b_proj[pl.ds(k, 1), :]
        wt_aug[k] = (HALF * jnp.transpose(scr[:]))[0:5 * C, 0:KA].astype(BF16)
        scr[:] = jnp.zeros_like(scr)
        scr[0:C, 0:C] = w_out[k].astype(F32)
        scr[C:C + 1, 0:C] = b_out[pl.ds(k, 1), :]
        scr[C + 8:C + 10, 0:C] = ln_in[k]
        small = jnp.transpose(scr[:, 0:LANES])
        wot_aug[k] = (HALF * small)[0:C, 0:KA].astype(BF16)
        gain[k] = jnp.broadcast_to(small[0:C, C + 8:C + 9], (C, n))
        lbias[k] = jnp.broadcast_to(small[0:C, C + 9:C + 10], (C, n))
    r = lax.broadcasted_iota(jnp.int32, (W2, W2), 0)
    q = lax.broadcasted_iota(jnp.int32, (W2, W2), 1)
    perm[:] = jnp.where(q == RB * (r % RB) + r // RB, 1.0, 0.0).astype(BF16)


def prepare(n, ln_in, w_proj, b_proj, w_out, b_out):
    sds = jax.ShapeDtypeStruct
    outs = [sds((2, 5 * C, KA), BF16), sds((2, C, KA), BF16), sds((2, C, n), F32), sds((2, C, n), F32), sds((W2, W2), BF16)]
    args = (w_proj, b_proj.astype(F32), ln_in.astype(F32), w_out, b_out.astype(F32))
    return call(prep_kernel, (1,), [full_spec(v.shape) for v in args], [full_spec(o.shape) for o in outs], outs, [pltpu.VMEM((LANES, 384), F32)], MEGA, MIB)(*args)


def with_ones(zh):
    row = lax.broadcasted_iota(jnp.int32, (RB, zh.shape[-1]), 0)
    return jnp.concatenate([zh, jnp.where(row == 0, 1.0, 0.0).astype(BF16)], axis=0)


def pre_fwd_kernel(z, mask, wt, gain, lbias, perm, a, b, a_s, b_s):
    for i in range(RB):
        a_s[i], b_s[i] = project(z[i].astype(F32), mask[pl.ds(i, 1), :].astype(F32), wt, gain, lbias)

    def put_a(grp, v):
        a[grp * RB:(grp + 1) * RB] = v.astype(BF16)

    def put_b(grp, v):
        b[grp * RB:(grp + 1) * RB] = v.astype(BF16)

    to_cmajor(perm[:], a_s, put_a)
    to_cmajor(perm[:], b_s, put_b)


def full_spec(shape):
    return pl.BlockSpec(shape, lambda s: (0,) * len(shape))


SMEM_SPEC = pl.BlockSpec(memory_space=pltpu.SMEM)


def call(kernel, grid, in_specs, out_specs, out_shape, scratch, flops, bytes_accessed, trans=0):
    return pl.pallas_call(
        kernel,
        grid=grid,
        in_specs=in_specs,
        out_specs=out_specs,
        out_shape=out_shape,
        scratch_shapes=scratch,
        interpret=INTERPRET,
        cost_estimate=pl.CostEstimate(flops=flops, bytes_accessed=bytes_accessed, transcendentals=trans),
        compiler_params=pltpu.CompilerParams(dimension_semantics=("arbitrary",) * len(grid), vmem_limit_bytes=VMEM_LIMIT),
    )


def blk_spec(shape, k):
    return pl.BlockSpec((None,) + tuple(shape[1:]), lambda s: (k,) + (0,) * (len(shape) - 1))


def pre_forward(z, mask, par):
    rows, _, n = z.shape
    specs, args = weights_specs(par, 0, False)
    cspec = pl.BlockSpec((C, RB, n), lambda s: (0, s, 0))
    return call(
        pre_fwd_kernel, (rows // RB,),
        [pl.BlockSpec((RB, C, n), lambda s: (s, 0, 0)), pl.BlockSpec((RB, n), lambda s: (s, 0))] + specs + [full_spec((W2, W2))],
        [cspec] * 2, [jax.ShapeDtypeStruct((C, rows, n), BF16)] * 2, [pltpu.VMEM((RB, C, n), BF16)] * 2, GIGA, 8 * MIB)(z, mask, *args, par[-1])


CB = 8
T_STEPS = C // CB


def global_rows(ids, partner):
    x, c = ids[0], ids[1]
    cc = 1 - c if partner else c
    return pl.multiple_of(C * (2 * (1 - x) + cc), C), pl.multiple_of(C * (2 * x + cc), C)


def place(dst, src_mine, src_other, ids):
    for (peer, own), partner in ((src_mine, False), (src_other, True)):
        off_peer, off_own = global_rows(ids, partner)
        dst[pl.ds(off_peer, C), :] = peer
        dst[pl.ds(off_own, C), :] = own


def halves(ref):
    return ref[0:C, :], ref[C:LANES, :]


def tri_spec(shape, row_blk=0):
    return pl.BlockSpec((CB,) + tuple(shape[1:]), lambda s: (jnp.minimum(s, T_STEPS - 1), row_blk, 0))


def row_blk(s):
    return jnp.maximum(s - T_STEPS, 0)


def r_spec(n, off=0):
    return pl.BlockSpec((RB, C, n), lambda s: (row_blk(s) + off, 0, 0))


def c_spec(n):
    return pl.BlockSpec((C, RB, n), lambda s: (0, row_blk(s), 0))


def two_specs(shape):
    zeros = (0,) * (len(shape) - 1)
    return [pl.BlockSpec(shape, lambda s: (jnp.clip(s - T_STEPS, 0, 3),) + zeros), pl.BlockSpec(shape, lambda s: (jnp.maximum(s - T_STEPS - 4, 0),) + zeros)]


def m_spec(n):
    return pl.BlockSpec((RB, n), lambda s: (row_blk(s), 0))


def pick(r, peer, own):
    return jnp.where(r < 4, peer, own)


def channels(step):
    return [(ch, step * CB + ch) for ch in range(CB)]


def mid_norm(x, xh_s, lnmid, blk, xn_s, rstd_s):
    tot = x[0]
    for c in range(1, C):
        tot = tot + x[c]
    mean = tot * (1.0 / C)
    d = x[0] - mean
    sq = d * d
    for c in range(1, C):
        d = x[c] - mean
        sq = sq + d * d
    rstd = lax.rsqrt(sq * (1.0 / C) + EPS)
    rstd_s[:] = rstd
    for c in range(C):
        xn = (x[c] - mean) * rstd
        xn_s[c] = xn
        xh_s[c] = (xn * lnmid[blk, 0, c] + lnmid[blk, 1, c]).astype(BF16)


def gate_of(zf, wt, gain, lbias):
    zn, _ = norm_rows(zf)
    zh = (zn * gain[:] + lbias[:]).astype(BF16)
    return jnp.tanh(dot_nn(wt[4 * C:5 * C], with_ones(zh)))


def project(zf, m, wt, gain, lbias):
    zn, _ = norm_rows(zf)
    zh = (zn * gain[:] + lbias[:]).astype(BF16)
    p = dot_nn(wt[0:4 * C], with_ones(zh))
    a = ((1.0 + jnp.tanh(p[0:C])) * (p[C:2 * C] * m)).astype(BF16)
    b = ((1.0 + jnp.tanh(p[2 * C:3 * C])) * (p[3 * C:4 * C] * m)).astype(BF16)
    return a, b


def fwd_kernel(ids, ap, ao, bp, bo, qp, qo, zp, zo, mp, mo, wt0, gain0, lbias0, wot0, wt1, gain1, lbias1, lnmid, perm, zmid, xn, rstd, a1, b1, a1k, a1s, x_s, full, xh_s, xi_s, a_s, b_s):
    step = pl.program_id(0)

    @pl.when(step < T_STEPS)
    def _():
        for ch, dst in channels(step):
            buf = full.at[ch % 2]
            place(buf, (bp[ch], bo[ch]), (qp[ch], qo[ch]), ids)
            x_s[dst] = dot_nt(jnp.concatenate([ap[ch], ao[ch]], axis=0), buf[:])

    @pl.when(step >= T_STEPS)
    def _():
        r = step - T_STEPS
        mid_norm(x_s.at[:, pl.ds(pl.multiple_of(r * RB, RB), RB), :], xh_s, lnmid, 0, xn, rstd)
        to_rows(perm[:], xh_s, xi_s)

        def update(i):
            zf = pick(r, zp[i], zo[i]).astype(F32)
            upd = dot_nn(wot0[:], with_ones(xi_s[i]))
            zmid[i] = (zf + (1.0 + gate_of(zf, wt0, gain0, lbias0)) * upd).astype(BF16)

        def sides(i):
            m = pick(r, mp[pl.ds(i, 1), :], mo[pl.ds(i, 1), :]).astype(F32)
            a_s[i], b_s[i] = project(zmid[i].astype(F32), m, wt1, gain1, lbias1)

        staggered(update, sides)

        def put_a(grp, v):
            a1[grp * RB:(grp + 1) * RB] = v.astype(BF16)
            mine, other = split_cols(v, ids[1])
            a1k[grp * RB:(grp + 1) * RB] = mine.astype(BF16)
            a1s[grp * RB:(grp + 1) * RB] = other.astype(BF16)

        def put_b(grp, v):
            b1[grp * RB:(grp + 1) * RB] = v.astype(BF16)

        to_cmajor(perm[:], a_s, put_a)
        to_cmajor(perm[:], b_s, put_b)


def weights_specs(par, blk, with_out):
    wt, wot, gain, lbias, _ = par
    specs = [blk_spec(wt.shape, blk), blk_spec(gain.shape, blk), blk_spec(gain.shape, blk)]
    args = [wt, gain, lbias]
    if with_out:
        specs.append(blk_spec(wot.shape, blk))
        args.append(wot)
    return specs, args


def fwd_fused(ids, sides, zp, zo, masks, par, lnmid):
    n = zp.shape[-1]
    s0, w0 = weights_specs(par, 0, True)
    s1, w1 = weights_specs(par, 1, False)
    sds, vm = jax.ShapeDtypeStruct, pltpu.VMEM
    c_out, h_out = sds((C, LANES, n), BF16), sds((C, LANES, LANES), BF16)
    return call(
        fwd_kernel, (T_STEPS + 8,),
        [SMEM_SPEC] + [tri_spec(v.shape) for v in sides] + two_specs((RB, C, n)) + two_specs((RB, n)) + s0 + s1 + [SMEM_SPEC, full_spec((W2, W2))],
        [r_spec(n), c_spec(n), m_spec(n), c_spec(n), c_spec(n), c_spec(LANES), c_spec(LANES)],
        [sds((LANES, C, n), BF16), sds((C, LANES, n), F32), sds((LANES, n), F32), c_out, c_out, h_out, h_out],
        [vm((C, LANES, n), F32), vm((2, n, n), BF16), vm((C, RB, n), BF16), vm((RB, C, n), BF16), vm((RB, C, n), BF16), vm((RB, C, n), BF16)],
        GIGA, 40 * MIB)(ids, *sides, zp, zo, *masks, *w0, *w1, lnmid, par[-1])


def mid_back(dxc_s, xn, rstd, lnmid, blk, acc_mg, acc_mb, emit):
    m1 = m2 = None
    for c in range(C):
        dy = dxc_s[c]
        dyx = dy * xn[c]
        gn = lnmid[blk, 0, c]
        m1 = dy * gn if m1 is None else m1 + dy * gn
        m2 = dyx * gn if m2 is None else m2 + dyx * gn
        acc_mg[c] += fold(dyx[0:8] + dyx[8:RB])
        acc_mb[c] += fold(dy[0:8] + dy[8:RB])
    m1 = m1 * (1.0 / C)
    m2 = m2 * (1.0 / C)
    for c in range(C):
        emit(c, rstd * (dxc_s[c] * lnmid[blk, 0, c] - m1 - xn[c] * m2))


def clear(step, accs):
    @pl.when(step == 0)
    def _():
        for acc in accs:
            acc[:] = jnp.zeros_like(acc)


def turn_kernel(ids, ak, ar, b, bq, z, dzp, dzo, wt, gain, lbias, wot, wo, lnmid, perm, znew, dx, dpg, acc_bg, acc_bo, acc_wo, acc_mg, acc_mb, x_s, xh_s, xi_s, dxi_s, dub_s, dxc_s, xn_s, r_s):
    step = pl.program_id(0)
    xx = ids[0]
    clear(step, (acc_bg, acc_bo, acc_wo, acc_mg, acc_mb))

    @pl.when(step < T_STEPS)
    def _():
        for ch, dst in channels(step):
            out = dot_tn(ak[ch], b[ch]) + dot_tn(ar[ch], bq[ch])
            x_s[dst, pl.ds(pl.multiple_of(C * (1 - xx), C), C), :] = out[0:C]
            x_s[dst, pl.ds(pl.multiple_of(C * xx, C), C), :] = out[C:LANES]

    @pl.when(step >= T_STEPS)
    def _():
        r = step - T_STEPS
        mid_norm(x_s.at[:, pl.ds(pl.multiple_of(r * RB, RB), RB), :], xh_s, lnmid, 1, xn_s, r_s)
        to_rows(perm[:], xh_s, xi_s)
        sums = [acc_bg[:], acc_bo[:], acc_wo[:]]

        def gates(i):
            zf = z[i].astype(F32)
            dz = pick(r, dzp[i], dzo[i]).astype(F32)
            t = gate_of(zf, wt, gain, lbias)
            upd = dot_nn(wot[:], with_ones(xi_s[i]))
            t1 = 1.0 + t
            znew[i] = (zf + t1 * upd).astype(BF16)
            d_upd = (HALF * dz) * t1
            d_pg = d_upd * (upd * (1.0 - t))
            dpg[i] = d_pg.astype(BF16)
            dub_s[i] = d_upd.astype(BF16)
            sums[0] += fold(d_pg)
            sums[1] += fold(d_upd)

        def products(i):
            dxi_s[i] = dot_nn(wo[:], dub_s[i]).astype(BF16)
            sums[2] += dot_nt(dub_s[i], xi_s[i])

        staggered(gates, products)
        acc_bg[:], acc_bo[:], acc_wo[:] = sums

        def put(grp, v):
            dxc_s[grp * RB:(grp + 1) * RB] = v

        to_cmajor(perm[:], dxi_s, put)

        def emit(c, v):
            dx[c] = v.astype(BF16)

        mid_back(dxc_s, xn_s, r_s[:], lnmid, 1, acc_mg, acc_mb, emit)


ACC_POST = ((C, LANES), (C, LANES), (C, C), (C, 8, LANES), (C, 8, LANES))
ACC_PRE = ((5 * C, C), (4 * C, LANES), (C, LANES), (C, LANES))


def turn_fused(ids, sides, z_mid, dz_parts, par, w_out, lnmid):
    n = z_mid.shape[-1]
    s1, w1 = weights_specs(par, 1, True)
    sds, vm = jax.ShapeDtypeStruct, pltpu.VMEM
    return call(
        turn_kernel, (T_STEPS + 8,),
        [SMEM_SPEC] + [tri_spec(v.shape) for v in sides] + [r_spec(n)] + two_specs((RB, C, n)) + s1 + [blk_spec(w_out.shape, 1), SMEM_SPEC, full_spec((W2, W2))],
        [two_specs((RB, C, n))[1], c_spec(n), r_spec(n)] + [full_spec(s) for s in ACC_POST],
        [sds((C, C, n), BF16), sds((C, LANES, n), BF16), sds((LANES, C, n), BF16)] + [sds(s, F32) for s in ACC_POST],
        [vm((C, LANES, n), F32), vm((C, RB, n), BF16)] + [vm((RB, C, n), BF16)] * 3 + [vm((C, RB, n), F32)] * 2 + [vm((RB, n), F32)],
        GIGA, 40 * MIB)(ids, *sides, z_mid, *dz_parts, *w1, w_out, lnmid, par[-1])


def pre_back_stages(z, dpg, mask_of, res_of, dst, wt, w, gain, lbias, dai_s, dbi_s, dp_s, zh_s, zn_s, rs_s, acc_b, sums):
    def gates(i):
        zn, rstd = norm_rows(z[i].astype(F32))
        zn_s[i] = zn
        rs_s[i] = jnp.broadcast_to(rstd, (8, rstd.shape[-1]))
        zh = (zn * gain[:] + lbias[:]).astype(BF16)
        zh_s[i] = zh
        p = dot_nn(wt[0:4 * C], with_ones(zh))
        m = HALF * mask_of(i).astype(F32)
        for side, ref in ((0, dai_s), (1, dbi_s)):
            base = side * 2 * C
            dm = ref[i].astype(F32) * m
            t = jnp.tanh(p[base:base + C])
            dv = dm * (1.0 + t)
            dg = dv * (p[base + C:base + 2 * C] * (1.0 - t))
            for k, d in ((2 * side, dg), (2 * side + 1, dv)):
                acc_b[k * C:(k + 1) * C] += fold(d)
                dp_s[i, k * C:(k + 1) * C] = d.astype(BF16)
        dp_s[i, 4 * C:5 * C] = dpg[i]

    def products(i):
        dp = dp_s[i]
        dzh = dot_nn(w[:], dp).astype(BF16).astype(F32)
        sums[0] += dot_nt(dp, zh_s[i])
        zn, rstd = zn_s[i], rs_s[i, 0:1, :]
        sums[1] += fold(dzh * zn)
        sums[2] += fold(dzh)
        dzn = dzh * gain[:]
        m1 = jnp.mean(dzn, axis=0, keepdims=True)
        m2 = jnp.mean(dzn * zn, axis=0, keepdims=True)
        dst[i] = (res_of(i).astype(F32) + rstd * (dzn - m1 - zn * m2)).astype(BF16)

    return gates, products


def back_kernel(ids, a, b, dx, dxq, z, dpg1, dzp, dzo, mp, mo, xn, rstd, zp, zo, wt1, gain1, lbias1, w1, wt0, gain0, lbias0, wot0, wo0, lnmid, perm, dzm, dx0, dxk, dxs, dpg0, acc_w, acc_b, acc_g, acc_lb, acc_bg, acc_bo, acc_wo, acc_mg, acc_mb, da_s, db_s, full, dai_s, dbi_s, dp_s, zh_s, zn_s, rs_s, xh_s, xi_s, dxi_s, dub_s, dxc_s):
    step = pl.program_id(0)
    clear(step, (acc_w, acc_b, acc_g, acc_lb, acc_bg, acc_bo, acc_wo, acc_mg, acc_mb))

    @pl.when(step < T_STEPS)
    def _():
        for ch, dst in channels(step):
            buf = full.at[ch % 2]
            place(buf, halves(dx.at[ch]), halves(dxq.at[ch]), ids)
            da_s[dst] = dot_nt(b[ch], buf[:]).astype(BF16)
            db_s[dst] = dot_nn(a[ch], buf[:]).astype(BF16)

    @pl.when(step >= T_STEPS)
    def _():
        r = step - T_STEPS
        rows = pl.ds(pl.multiple_of(r * RB, RB), RB)
        to_rows(perm[:], da_s.at[:, rows, :], dai_s)
        to_rows(perm[:], db_s.at[:, rows, :], dbi_s)
        for c in range(C):
            xh_s[c] = (xn[c] * lnmid[0, 0, c] + lnmid[0, 1, c]).astype(BF16)
        to_rows(perm[:], xh_s, xi_s)
        pre = [acc_w[:], acc_g[:], acc_lb[:]]
        pre_gates, pre_products = pre_back_stages(
            z, dpg1, lambda i: pick(r, mp[pl.ds(i, 1), :], mo[pl.ds(i, 1), :]), lambda i: pick(r, dzp[i], dzo[i]), dzm,
            wt1, w1, gain1, lbias1, dai_s, dbi_s, dp_s, zh_s, zn_s, rs_s, acc_b, pre)
        staggered(pre_gates, pre_products)
        acc_w[:], acc_g[:], acc_lb[:] = pre
        post = [acc_bg[:], acc_bo[:], acc_wo[:]]

        def gates(i):
            t = gate_of(pick(r, zp[i], zo[i]).astype(F32), wt0, gain0, lbias0)
            upd = dot_nn(wot0[:], with_ones(xi_s[i]))
            d_upd = (HALF * dzm[i].astype(F32)) * (1.0 + t)
            d_pg = d_upd * (upd * (1.0 - t))
            dpg0[i] = d_pg.astype(BF16)
            dub_s[i] = d_upd.astype(BF16)
            post[0] += fold(d_pg)
            post[1] += fold(d_upd)

        def products(i):
            dxi_s[i] = dot_nn(wo0[:], dub_s[i]).astype(BF16)
            post[2] += dot_nt(dub_s[i], xi_s[i])

        staggered(gates, products)
        acc_bg[:], acc_bo[:], acc_wo[:] = post

        def put(grp, v):
            dxc_s[grp * RB:(grp + 1) * RB] = v

        to_cmajor(perm[:], dxi_s, put)

        def emit(c, v):
            dx0[c] = v.astype(BF16)
            mine, other = split_cols(v, ids[1])
            dxk[c] = mine.astype(BF16)
            dxs[c] = other.astype(BF16)

        mid_back(dxc_s, xn, rstd[:], lnmid, 0, acc_mg, acc_mb, emit)


def back_fused(ids, sides, z_mid, dpg1, dz_parts, masks, xn, rstd, z_parts, par, w_proj, w_out, lnmid):
    n = z_mid.shape[-1]
    s1, w1 = weights_specs(par, 1, False)
    s0, w0 = weights_specs(par, 0, True)
    sds, vm = jax.ShapeDtypeStruct, pltpu.VMEM
    two = two_specs((RB, C, n))
    rows = vm((RB, C, n), BF16)
    accs = ACC_PRE + ACC_POST
    return call(
        back_kernel, (T_STEPS + 8,),
        [SMEM_SPEC] + [tri_spec(v.shape) for v in sides] + [r_spec(n), r_spec(n)] + two + two_specs((RB, n)) + [c_spec(n), m_spec(n)] + two
        + s1 + [blk_spec(w_proj.shape, 1)] + s0 + [blk_spec(w_out.shape, 0), SMEM_SPEC, full_spec((W2, W2))],
        [two[1], c_spec(n), c_spec(LANES), c_spec(LANES), r_spec(n)] + [full_spec(s) for s in accs],
        [sds((C, C, n), BF16), sds((C, LANES, n), BF16), sds((C, LANES, LANES), BF16), sds((C, LANES, LANES), BF16), sds((LANES, C, n), BF16)] + [sds(s, F32) for s in accs],
        [vm((C, LANES, n), BF16)] * 2 + [vm((2, n, n), BF16), rows, rows, vm((RB, 5 * C, n), BF16), rows, vm((RB, C, n), F32), vm((RB, 8, n), F32), vm((C, RB, n), BF16), rows, rows, rows, vm((C, RB, n), F32)],
        GIGA, 60 * MIB)(ids, *sides, z_mid, dpg1, *dz_parts, *masks, xn, rstd, *z_parts, *w1, w_proj, *w0, w_out, lnmid, par[-1])


def last_kernel(ids, dx, bp, bo, qp, qo, dxk, dxr, ap, ao, rp, ro, z, dpg, dres, mask, wt, gain, lbias, w, perm, dz, acc_w, acc_b, acc_g, acc_lb, da_s, db_s, full, tmp, dai_s, dbi_s, dp_s, zh_s, zn_s, rs_s):
    step = pl.program_id(0)
    xx = ids[0]
    clear(step, (acc_w, acc_b, acc_g, acc_lb))

    @pl.when(step < T_STEPS)
    def _():
        for ch, dst in channels(step):
            buf = full.at[ch % 2]
            place(buf, (bp[ch], bo[ch]), (qp[ch], qo[ch]), ids)
            da_s[dst] = dot_nn(dx[ch], buf[:]).astype(BF16)
            tmp[ch % 2] = dot_tn(dxk[ch], jnp.concatenate([ap[ch], ao[ch]], axis=0)) + dot_tn(dxr[ch], jnp.concatenate([rp[ch], ro[ch]], axis=0))
            db_s[dst] = tmp[ch % 2, pl.ds(pl.multiple_of(C * xx, C), C), :].astype(BF16)

    @pl.when(step >= T_STEPS)
    def _():
        rows = pl.ds(pl.multiple_of((step - T_STEPS) * RB, RB), RB)
        to_rows(perm[:], da_s.at[:, rows, :], dai_s)
        to_rows(perm[:], db_s.at[:, rows, :], dbi_s)
        sums = [acc_w[:], acc_g[:], acc_lb[:]]
        staggered(*pre_back_stages(
            z, dpg, lambda i: mask[pl.ds(i, 1), :], lambda i: dres[i], dz,
            wt, w, gain, lbias, dai_s, dbi_s, dp_s, zh_s, zn_s, rs_s, acc_b, sums))
        acc_w[:], acc_g[:], acc_lb[:] = sums


def last_fused(ids, sides, z, dpg, dres, mask, par, w_proj):
    n = z.shape[-1]
    s0, w0 = weights_specs(par, 0, False)
    sds, vm = jax.ShapeDtypeStruct, pltpu.VMEM
    rows = vm((RB, C, n), BF16)
    return call(
        last_kernel, (T_STEPS + 4,),
        [SMEM_SPEC, tri_spec((C, C, n), 1)] + [tri_spec(v.shape) for v in sides[1:]] + [r_spec(n), r_spec(n, 4), r_spec(n), m_spec(n)] + s0 + [blk_spec(w_proj.shape, 0), full_spec((W2, W2))],
        [r_spec(n)] + [full_spec(s) for s in ACC_PRE],
        [sds((C, C, n), BF16)] + [sds(s, F32) for s in ACC_PRE],
        [vm((C, C, n), BF16)] * 2 + [vm((2, n, n), BF16), vm((2, LANES, n), F32), rows, rows, vm((RB, 5 * C, n), BF16), rows, vm((RB, C, n), F32), vm((RB, 8, n), F32)],
        GIGA, 40 * MIB)(ids, *sides, z, dpg, dres, mask, *w0, w_proj, par[-1])


PACK = 512


def grads_kernel(n_dp, n_dap, w0, b0, q0, g0, l0, wo0, o0, mg0, mb0, w1, b1, q1, g1, l1, wo1, o1, mg1, mb1, out, buf, recv_a, red, recv_b, gath, vec, send_a, rcv_a, send_b, rcv_b, send_c, rcv_c, send_d, rcv_d):
    dp, dap = lax.axis_index("dp"), lax.axis_index("dap")
    big, small = PACK // n_dap, PACK // n_dap // n_dp
    bar = pltpu.get_barrier_semaphore()
    for k in range(1, n_dap):
        pl.semaphore_signal(bar, inc=1, device_id=(dp, lax.rem(dap + k, n_dap)), device_id_type=MESH_ID)
    for k in range(1, n_dp):
        pl.semaphore_signal(bar, inc=1, device_id=(lax.rem(dp + k, n_dp), dap), device_id_type=MESH_ID)

    buf[0:5 * C, 0:C] = w0[:]
    buf[0:5 * C, C:2 * C] = HALF * w1[:]
    buf[5 * C:6 * C, 0:C] = HALF * wo0[:]
    buf[5 * C:6 * C, C:2 * C] = HALF * wo1[:]

    def put(k, base, ref, scale):
        v = ref[:]
        if v.ndim == 3:
            v = jnp.sum(v, axis=1)
        rows = v.shape[0]
        tot = scale * jnp.sum(v, axis=1, keepdims=True)
        lane = lax.broadcasted_iota(jnp.int32, (rows, LANES), 1)
        vec[base:base + rows, :] = jnp.where(lane == k, tot, vec[base:base + rows, :])

    vec[:] = jnp.zeros_like(vec)
    put(0, 0, b0, 1.0)
    put(0, 4 * C, q0, HALF)
    put(1, 0, b1, HALF)
    put(1, 4 * C, q1, HALF)
    for k, (ref, scale) in enumerate(((g0, 1.0), (l0, 1.0), (g1, HALF), (l1, HALF), (mg0, HALF), (mb0, HALF), (mg1, HALF), (mb1, HALF), (o0, HALF), (o1, HALF))):
        put(2 + k, 0, ref, scale)
    vt = jnp.transpose(vec[:])
    for t in range(3):
        buf[6 * C + RB * t:6 * C + RB * t + RB, :] = vt[0:RB, LANES * t:LANES * (t + 1)]
    buf[6 * C + 48:PACK, :] = jnp.zeros((PACK - 6 * C - 48, LANES), F32)

    pl.semaphore_wait(bar, n_dap + n_dp - 2)

    def copies(count, make):
        made = [make(k) for k in range(1, count)]
        for cp in made:
            cp.start()
        return made

    def to_dap(k):
        return (dp, lax.rem(dap + k, n_dap))

    def to_dp(k):
        return (lax.rem(dp + k, n_dp), dap)

    def rows_of(idx, size):
        return pl.ds(pl.multiple_of(idx * size, size), size)

    stage = copies(n_dap, lambda k: pltpu.make_async_remote_copy(buf.at[rows_of(lax.rem(dap + k, n_dap), big)], recv_a.at[k - 1], send_a.at[k - 1], rcv_a.at[k - 1], device_id=to_dap(k), device_id_type=MESH_ID))
    tot = buf[rows_of(dap, big), :]
    for k, cp in enumerate(stage):
        cp.wait_recv()
        tot = tot + recv_a[k]
    red[:] = tot
    for cp in stage:
        cp.wait_send()

    stage = copies(n_dp, lambda k: pltpu.make_async_remote_copy(red.at[rows_of(lax.rem(dp + k, n_dp), small)], recv_b.at[k - 1], send_b.at[k - 1], rcv_b.at[k - 1], device_id=to_dp(k), device_id_type=MESH_ID))
    tot = red[rows_of(dp, small), :]
    for k, cp in enumerate(stage):
        cp.wait_recv()
        tot = tot + recv_b[k]
    gath[rows_of(dp, small), :] = tot
    for cp in stage:
        cp.wait_send()

    mine = gath.at[rows_of(dp, small)]
    stage = copies(n_dp, lambda k: pltpu.make_async_remote_copy(mine, mine, send_c.at[k - 1], rcv_c.at[k - 1], device_id=to_dp(k), device_id_type=MESH_ID))
    for cp in stage:
        cp.wait()

    stage = copies(n_dap, lambda k: pltpu.make_async_remote_copy(gath, out.at[rows_of(dap, big)], send_d.at[k - 1], rcv_d.at[k - 1], device_id=to_dap(k), device_id_type=MESH_ID))
    out[rows_of(dap, big), :] = gath[:]
    for cp in stage:
        cp.wait()


def sum_grads(n_dp, n_dap, parts):
    big, small = PACK // n_dap, PACK // n_dap // n_dp
    dma = pltpu.SemaphoreType.DMA
    return pl.pallas_call(
        functools.partial(grads_kernel, n_dp, n_dap),
        out_shape=jax.ShapeDtypeStruct((PACK, LANES), F32),
        in_specs=[pl.BlockSpec(memory_space=pltpu.VMEM)] * len(parts),
        out_specs=pl.BlockSpec(memory_space=pltpu.VMEM),
        scratch_shapes=[pltpu.VMEM((PACK, LANES), F32), pltpu.VMEM((n_dap - 1, big, LANES), F32), pltpu.VMEM((big, LANES), F32), pltpu.VMEM((max(n_dp - 1, 1), small, LANES), F32), pltpu.VMEM((big, LANES), F32), pltpu.VMEM((384, LANES), F32)]
        + [dma((n_dap - 1,))] * 2 + [dma((max(n_dp - 1, 1),))] * 4 + [dma((n_dap - 1,))] * 2,
        name="grad_sum",
        cost_estimate=pl.CostEstimate(flops=MEGA, bytes_accessed=MIB, transcendentals=0),
        compiler_params=pltpu.CompilerParams(collective_id=0, has_side_effects=True),
    )(*parts)


def unpack_kernel(src, ln_in, gw, bp, lm, gwo, bo):
    t = jnp.transpose(src[0:6 * C, :])
    for k in range(2):
        gw[k] = t[k * C:(k + 1) * C, 0:5 * C]
        gwo[k] = t[k * C:(k + 1) * C, 5 * C:6 * C]
    base = 6 * C
    bp[:, 0:LANES] = src[base:base + 2, :]
    bp[:, LANES:W2] = src[base + RB:base + 18, :]
    bp[:, W2:320] = src[base + 32:base + 34, 0:C]
    for k in range(2):
        ln_in[k] = src[base + 2 + 2 * k:base + 4 + 2 * k, 0:C]
        lm[k] = src[base + 6 + 2 * k:base + 8 + 2 * k, 0:C]
    bo[:] = src[base + 10:base + 12, 0:C]


def unpack(flat):
    outs = [jax.ShapeDtypeStruct(s, F32) for s in ((2, 2, C), (2, C, 5 * C), (2, 5 * C), (2, 2, C), (2, C, C), (2, C))]
    return call(unpack_kernel, (1,), [full_spec(flat.shape)], [full_spec(o.shape) for o in outs], outs, [], MEGA, MIB)(flat)


SUM = sum_grads


def solution(mesh):
    def plan(z_pair, pair_mask, dz_out, ln_in, w_proj, b_proj, ln_mid, w_out, b_out):
        n = z_pair.shape[2]
        dap = lax.axis_index("dap")
        ids = jnp.stack([dap // 2, dap % 2]).astype(jnp.int32)
        x_pairs = [(0, 2), (2, 0), (1, 3), (3, 1)]
        c_pairs = [(0, 1), (1, 0), (2, 3), (3, 2)]

        def over_x(v):
            return lax.ppermute(v, "dap", x_pairs)

        def over_c(v):
            return lax.ppermute(v, "dap", c_pairs)

        par = prepare(n, ln_in, w_proj, b_proj, w_out, b_out)
        lnmid = ln_mid.astype(F32)
        m_own = pair_mask[0]
        z_own = jnp.transpose(z_pair[0], (0, 2, 1))
        dz_own = jnp.transpose(dz_out[0], (0, 2, 1))
        m_peer = over_x(m_own)
        z_peer = over_x(z_own)
        z_peer, dz_src = lax.optimization_barrier((z_peer, dz_own))
        dz_peer = over_x(dz_src)
        masks = (m_peer, m_own)

        ao, bo = pre_forward(z_own, m_own, par)
        qo, ro = over_c(bo), over_c(ao)
        ap, bp = pre_forward(z_peer, m_peer, par)
        qp, rp = over_c(bp), over_c(ap)
        z_mid, xn, rstd, a1, b1, a1k, a1s = fwd_fused(ids, (ap, ao, bp, bo, qp, qo), z_peer, z_own, masks, par, lnmid)
        a1r, b1p = over_c(a1s), over_c(b1)
        z_new, dx1, dpg1, bg1, bo1, wo1, mg1, mb1 = turn_fused(ids, (a1k, a1r, b1, b1p), z_mid, (dz_peer, dz_own), par, w_out, lnmid)
        dx1p = over_c(dx1)
        dz_mid, dx0, dx0k, dx0s, dpg0, w1, b1s, g1, lb1, bg0, bo0, wo0, mg0, mb0 = back_fused(ids, (a1, b1, dx1, dx1p), z_mid, dpg1, (dz_peer, dz_own), masks, xn, rstd, (z_peer, z_own), par, w_proj, w_out, lnmid)
        dx0r = over_c(dx0s)
        dz, w0, b0s, g0, lb0 = last_fused(ids, (dx0, bp, bo, qp, qo, dx0k, dx0r, ap, ao, rp, ro), z_own, dpg0, dz_mid, m_own, par, w_proj)

        flat = SUM(mesh.shape["dp"], mesh.shape["dap"], (w0, b0s, bg0, g0, lb0, wo0, bo0, mg0, mb0, w1, b1s, bg1, g1, lb1, wo1, bo1, mg1, mb1))
        g_ln_in, gw, g_bp, g_lm, gwo, g_bo = unpack(flat)
        z_res = jnp.transpose(z_new, (0, 2, 1))[None]
        dz_res = jnp.transpose(dz, (0, 2, 1))[None]
        return z_res, dz_res, g_ln_in, gw, g_bp, g_lm, gwo, g_bo

    row_spec = P("dp", "dap")
    return jax.shard_map(plan, mesh=mesh, in_specs=(row_spec, row_spec, row_spec, P(), P(), P(), P(), P(), P()), out_specs=(row_spec, row_spec, P(), P(), P(), P(), P(), P()), check_vma=False)
```

time: 295 us -> 288 us (0.976)
  Pallas kernels: 195 us -> 177 us
  waiting for transfers between devices: 80.1 us -> 94.7 us
    ppermute x3, waiting for transfers between devices: 57 us -> 80.2 us  [over_x(): return lax.ppermute(v, 'dap', x_pairs)]
    pallas_call x12 -> x6, Pallas kernels: 168 us -> 150 us  [the longest x1 50.5 us: back_fused(): call(back_kernel, (T_STEPS + 8,), [SMEM_SPEC] + [tri_spec(v.shape) for v...]
    ppermute x8, waiting for transfers between devices: 23.1 us -> 14.6 us  [over_c(): return lax.ppermute(v, 'dap', c_pairs)]
  transfers between devices with their start and end apart: 11 -> 11, of which waited for: 7 -> 6; matrix products, arithmetic and copies ran while one was open for 2% -> 2% of each run, Pallas kernels for 29% -> 23%
where the time goes in v1:
time: 288 us; the launch traced here: 287 us
  Pallas kernels  177 us (61%)
  waiting for transfers between devices  94.7 us (33%)
  starting transfers between devices  6.01 us (2%)
  other arithmetic  4.9 us (2%)
  local copies, waits for them, and re-layouts  4.54 us (2%)
    ppermute x3, waiting for transfers between devices, over_x(): return lax.ppermute(v, 'dap', x_pairs)  80.2 us
    pallas_call x1, Pallas kernels, back_fused(): call(back_kernel, (T_STEPS + 8,), [SMEM_SPEC] + [tri_spec(v.shape) for v...  50.5 us
    pallas_call x1, Pallas kernels, fwd_fused(): call(fwd_kernel, (T_STEPS + 8,), [SMEM_SPEC] + [tri_spec(v.shape) for v i...  32.3 us
    pallas_call x1, Pallas kernels, turn_fused(): call(turn_kernel, (T_STEPS + 8,), [SMEM_SPEC] + [tri_spec(v.shape) for v...  29.5 us
    pallas_call x1, Pallas kernels, sum_grads(): pl.pallas_call(functools.partial(grads_kernel, n_dp, n_dap), out_shape=ja...  23.3 us
    pallas_call x1, Pallas kernels, last_fused(): call(last_kernel, (T_STEPS + 4,), [SMEM_SPEC, tri_spec((C, C, n), 1)] + [...  22.6 us
    pallas_call x2, Pallas kernels, pre_forward(): call(pre_fwd_kernel, (rows // RB,), [pl.BlockSpec((RB, C, n), lambda s: (...  14.7 us
    ppermute x8, waiting for transfers between devices, over_c(): return lax.ppermute(v, 'dap', c_pairs)  14.6 us
  transfers between devices with their start and end apart: 11, of which 6 were waited for; matrix products, arithmetic and copies ran while one was open for 2% of the time, Pallas kernels for 23%

profile of v1, /device:TPU:0, one launch (start us, length us, event | category | flops | bytes accessed | tf_op | source)
XLA Modules:
  0.0 287.5 jit_solution(10947542613352531642)
XLA Ops:
  0.6 3.0 %collective-permute-start = (bf16[64,64,256]{2,1,0:T(8,128)(2,1)}, bf16[64,64,256]{2,1,0:T(8,128)(2,1)S(1)}, u32[]{:S(2)}, u32[]{:S(2)}) collective-permute-start(bf16[64,64,256]{2,1,0:T(8,128)(2,1)} %bitcast.15), channel_id=1, source_target_pairs={{0,2},{2,0},{1,3},{3,1},{4,6},{6,4},{5,7},{7,5},{8,10},{10,8},{9,1... | collective-permute-start | bytes 6291464 | tf_op jit(solution)/shard_map/ppermute | solution.py:701
  3.7 0.1 collective-permute-start.1
  3.7 1.3 convert_element_type.12.b_proj
  5.0 1.3 convert_element_type.13.ln_in
  6.3 1.2 convert_element_type.14.b_out
  7.5 1.9 shard_map.152
  9.4 7.4 %shard_map.154 = (bf16[64,64,256]{2,1,0:T(8,128)(2,1)}, bf16[64,64,256]{2,1,0:T(8,128)(2,1)}) custom-call(bf16[64,64,256]{2,1,0:T(8,128)(2,1)} %bitcast.16, s32[64,256]{1,0:T(8,128)} %bitcast.24, bf16[2,320,80]{2,1,0:T(8,128)(2,1)} %get-tuple-element.60.wt.wt0.wt1, f32[2,64,256]{2,1,0:T(8,128)} %get-tuple-element.61.gain.gain0.gain1, ...), custom_call_target="tpu_custom_call" | custom-call | flops 1000000000 | bytes 8388608 | tf_op jit(solution)/shard_map/pallas_call | solution.py:167
  16.8 0.0 copy-start.10
  16.8 0.0 collective-permute-start.3
  16.8 33.4 %collective-permute-done.z.zp = bf16[64,64,256]{2,1,0:T(8,128)(2,1)S(1)} collective-permute-done((bf16[64,64,256]{2,1,0:T(8,128)(2,1)}, bf16[64,64,256]{2,1,0:T(8,128)(2,1)S(1)}, u32[]{:S(2)}, u32[]{:S(2)}) %collective-permute-start) | collective-permute-done | bytes 2097184 | tf_op jit(solution)/shard_map/ppermute | solution.py:701
  50.2 0.0 copy-start.5
  50.2 0.7 collective-permute-done.1.mask.mp
  50.9 0.6 copy-done.5
  51.5 0.0 copy-start.9
  51.5 0.6 copy-done.9
  52.2 7.3 %shard_map.153 = (bf16[64,64,256]{2,1,0:T(8,128)(2,1)}, bf16[64,64,256]{2,1,0:T(8,128)(2,1)}) custom-call(bf16[64,64,256]{2,1,0:T(8,128)(2,1)} %copy-done.5, s32[64,256]{1,0:T(8,128)} %copy-done.9, bf16[2,320,80]{2,1,0:T(8,128)(2,1)} %get-tuple-element.60.wt.wt0.wt1, f32[2,64,256]{2,1,0:T(8,128)} %get-tuple-element.61.gain.gain0.gain1, ...), custom_call_target="tpu_custom_call" | custom-call | flops 1000000000 | bytes 8388608 | tf_op jit(solution)/shard_map/pallas_call | solution.py:167
  59.5 0.0 collective-permute-start.2
  59.5 0.0 copy-done.10
  59.5 0.6 convert_element_type.15.lnmid
  60.1 0.6 pad_add_fusion.ids
  60.7 0.0 collective-permute-done.3.qo
  60.7 0.0 copy-start.3
  60.7 3.3 %collective-permute-done.2.qp = bf16[64,64,256]{2,1,0:T(8,128)(2,1)} collective-permute-done((bf16[64,64,256]{2,1,0:T(8,128)(2,1)}, bf16[64,64,256]{2,1,0:T(8,128)(2,1)}, u32[]{:S(2)}, u32[]{:S(2)}) %collective-permute-start.2) | collective-permute-done | bytes 2097184 | tf_op jit(solution)/shard_map/ppermute | solution.py:704
  64.0 0.0 copy-done.3
  64.0 0.0 copy-start
  64.0 32.3 %shard_map.155 = (bf16[128,64,256]{2,1,0:T(8,128)(2,1)}, f32[64,128,256]{2,1,0:T(8,128)}, f32[128,256]{1,0:T(8,128)}, bf16[64,128,256]{2,1,0:T(8,128)(2,1)}, bf1...) custom-call(s32[2]{0:T(128)} %pad_add_fusion.ids, ...), custom_call_target="tpu_custom_call" | custom-call | flops 1000000000 | bytes 41943040 | tf_op jit(solution)/shard_map/pallas_call | solution.py:316
  96.2 0.2 collective-permute-start.5
  96.5 0.0 copy-done
  96.5 1.7 collective-permute-start.6
  98.2 0.1 collective-permute-start.4
  98.3 46.1 %collective-permute-done.6.dzp = bf16[64,64,256]{2,1,0:T(8,128)(2,1)S(1)} collective-permute-done((bf16[64,64,256]{2,1,0:T(8,128)(2,1)S(1)}, bf16[64,64,256]{2,1,0:T(8,128)(2,1)S(1)}, u32[]{:S(2)}, u32[]{:S(2)}) %collective-permute-start.6) | collective-permute-done | bytes 2097184 | tf_op jit(solution)/shard_map/ppermute | solution.py:701
  144.4 0.0 copy-start.1
  144.4 0.0 collective-permute-done.4.ar
  144.4 0.0 copy-start.8
  144.4 0.0 collective-permute-done.5.bq
  144.4 0.0 copy-start.6
  144.4 1.3 copy-done.8
  145.7 1.3 copy-done.6
  147.0 0.7 copy-done.1
  147.6 0.0 copy-start.2
  147.6 0.0 copy-start.4
  147.6 29.5 %shard_map.156 = (bf16[64,64,256]{2,1,0:T(8,128)(2,1)}, bf16[64,128,256]{2,1,0:T(8,128)(2,1)}, bf16[128,64,256]{2,1,0:T(8,128)(2,1)}, f32[64,128]{1,0:T(8,128)},...) custom-call(s32[2]{0:T(128)} %pad_add_fusion.ids, ...), custom_call_target="tpu_custom_call" | custom-call | flops 1000000000 | bytes 41943040 | tf_op jit(solution)/shard_map/pallas_call | solution.py:407
  177.2 0.1 collective-permute-start.7
  177.2 0.0 copy-done.2
  177.3 0.5 collective-permute-start.10
  177.7 0.0 copy-done.4
  177.7 0.1 collective-permute-start.9
  177.8 6.9 %collective-permute-done.7.dxq = bf16[64,128,256]{2,1,0:T(8,128)(2,1)} collective-permute-done((bf16[64,128,256]{2,1,0:T(8,128)(2,1)}, bf16[64,128,256]{2,1,0:T(8,128)(2,1)}, u32[]{:S(2)}, u32[]{:S(2)}) %collective-permute-start.7) | collective-permute-done | bytes 4194336 | tf_op jit(solution)/shard_map/ppermute | solution.py:704
  184.7 50.5 %shard_map.157 = (bf16[64,64,256]{2,1,0:T(8,128)(2,1)}, bf16[64,128,256]{2,1,0:T(8,128)(2,1)}, bf16[64,128,128]{2,1,0:T(8,128)(2,1)}, bf16[64,128,128]{2,1,0:T(8...) custom-call(s32[2]{0:T(128)} %pad_add_fusion.ids, ...), custom_call_target="tpu_custom_call" | custom-call | flops 1000000000 | bytes 62914560 | tf_op jit(solution)/shard_map/pallas_call | solution.py:519
  235.2 0.2 collective-permute-start.8
  235.4 0.0 collective-permute-done.10.ro
  235.4 0.0 copy-start.7
  235.4 0.0 collective-permute-done.9.rp
  235.4 4.4 %collective-permute-done.8.dxr = bf16[64,128,128]{2,1,0:T(8,128)(2,1)} collective-permute-done((bf16[64,128,128]{2,1,0:T(8,128)(2,1)}, bf16[64,128,128]{2,1,0:T(8,128)(2,1)}, u32[]{:S(2)}, u32[]{:S(2)}) %collective-permute-start.8) | collective-permute-done | bytes 2097184 | tf_op jit(solution)/shard_map/ppermute | solution.py:704
  239.8 0.0 copy-done.7
  239.8 22.6 %shard_map.158 = (bf16[64,64,256]{2,1,0:T(8,128)(2,1)}, f32[320,64]{1,0:T(8,128)}, f32[256,128]{1,0:T(8,128)}, f32[64,128]{1,0:T(8,128)}, f32[64,128]{1,0:T(8,128)}) custom-call(s32[2]{0:T(128)} %pad_add_fusion.ids, bf16[64,128,256]{2,1,0:T(8,128)(2,1)} %get-tuple-element.80.dx, bf16[64,64,256]{2,1,0:T(8,128)(2,1)} %get-tuple-element.66.bp, ...), custom_call_target="tpu_custom_call" | custom-call | flops 1000000000 | bytes 41943040 | tf_op jit(solution)/shard_map/pallas_call | solution.py:560
  262.4 23.3 %grad_sum.1.src = f32[512,128]{1,0:T(8,128)} custom-call(f32[320,64]{1,0:T(8,128)} %get-tuple-element.86.w0, f32[256,128]{1,0:T(8,128)} %get-tuple-element.87.b0, f32[64,128]{1,0:T(8,128)} %get-tuple-element.88.q0, f32[64,128]{1,0:T(8,128)} %get-tuple-element.89.g0, f32[64,128]{1,0:T(8,128)} %get-tuple-element.90.l0, f32[64,64]{1,0:T(8,128)} %get-tuple-element.91.wo0, ...), custom_call_target="tpu_custom_call" | custom-call | flops 1000000 | bytes 1048576 | tf_op jit(solution)/shard_map/grad_sum/pallas_call | solution.py:656
  285.7 1.8 shard_map.159
Async XLA Ops:
  0.6 49.6 %collective-permute-start = (bf16[64,64,256]{2,1,0:T(8,128)(2,1)}, bf16[64,64,256]{2,1,0:T(8,128)(2,1)S(1)}, u32[]{:S(2)}, u32[]{:S(2)}) collective-permute-start(bf16[64,64,256]{2,1,0:T(8,128)(2,1)} %bitcast.15), channel_id=1, source_target_pairs={{0,2},{2,0},{1,3},{3,1},{4,6},{6,4},{5,7},{7,5},{8,10},{10,8},{9,1... | collective-permute-start | bytes 6291464 | tf_op jit(solution)/shard_map/ppermute | solution.py:701
  3.7 47.2 %collective-permute-start.1 = (s32[64,256]{1,0:T(8,128)}, s32[64,256]{1,0:T(8,128)S(1)}, u32[]{:S(2)}, u32[]{:S(2)}) collective-permute-start(s32[64,256]{1,0:T(8,128)} %bitcast.23), channel_id=1, source_target_pairs={{0,2},{2,0},{1,3},{3,1},{4,6},{6,4},{5,7},{7,5},{8,10},{10,8},{9,1... | collective-permute-start | bytes 196616 | tf_op jit(solution)/shard_map/ppermute | solution.py:701
  16.8 42.7 %copy-start.10 = (bf16[2,2,64]{2,1,0:T(2,128)(2,1)S(1)}, bf16[2,2,64]{2,1,0:T(2,128)(2,1)}, u32[]{:S(2)}) copy-start(bf16[2,2,64]{2,1,0:T(2,128)(2,1)} %param.15) | copy-start | bytes 1540
  16.8 43.9 %collective-permute-start.3 = (bf16[64,64,256]{2,1,0:T(8,128)(2,1)}, bf16[64,64,256]{2,1,0:T(8,128)(2,1)S(1)}, u32[]{:S(2)}, u32[]{:S(2)}) collective-permute-start(bf16[64,64,256]{2,1,0:T(8,128)(2,1)} %get-tuple-element.67.bo), channel_id=1, source_target_pairs={{0,1},{1,0},{2,3},{3,2},{4,5},{5,4},{6,7},{7,6},{8,9},{9,8},{10,11... | collective-permute-start | bytes 6291464 | tf_op jit(solution)/shard_map/ppermute | solution.py:704
  50.2 1.3 copy-start.5
  51.5 0.6 copy-start.9
  59.5 4.5 %collective-permute-start.2 = (bf16[64,64,256]{2,1,0:T(8,128)(2,1)}, bf16[64,64,256]{2,1,0:T(8,128)(2,1)}, u32[]{:S(2)}, u32[]{:S(2)}) collective-permute-start(bf16[64,64,256]{2,1,0:T(8,128)(2,1)} %get-tuple-element.66.bp), channel_id=1, source_target_pairs={{0,1},{1,0},{2,3},{3,2},{4,5},{5,4},{6,7},{7,6},{8,9},{9,8},{10,11... | collective-permute-start | bytes 6291464 | tf_op jit(solution)/shard_map/ppermute | solution.py:704
  60.7 3.3 %copy-start.3 = (bf16[64,64,256]{2,1,0:T(8,128)(2,1)}, bf16[64,64,256]{2,1,0:T(8,128)(2,1)S(1)}, u32[]{:S(2)}) copy-start(bf16[64,64,256]{2,1,0:T(8,128)(2,1)S(1)} %collective-permute-done.3.qo) | copy-start | bytes 6291460
  64.0 32.5 %copy-start = (bf16[1,64,256,64]{2,3,1,0:T(8,128)(2,1)S(1)}, bf16[1,64,256,64]{2,3,1,0:T(8,128)(2,1)}, u32[]{:S(2)}) copy-start(bf16[1,64,256,64]{2,3,1,0:T(8,128)(2,1)} %param.11) | copy-start | bytes 6291460
  96.2 48.1 %collective-permute-start.5 = (bf16[64,128,256]{2,1,0:T(8,128)(2,1)}, bf16[64,128,256]{2,1,0:T(8,128)(2,1)S(1)}, u32[]{:S(2)}, u32[]{:S(2)}) collective-permute-start(bf16[64,128,256]{2,1,0:T(8,128)(2,1)} %get-tuple-element.71.b), channel_id=1, source_target_pairs={{0,1},{1,0},{2,3},{3,2},{4,5},{5,4},{6,7},{7,6},{8,9},{9,8},{10,11... | collective-permute-start | bytes 12582920 | tf_op jit(solution)/shard_map/ppermute | solution.py:704
  96.5 47.9 %collective-permute-start.6 = (bf16[64,64,256]{2,1,0:T(8,128)(2,1)S(1)}, bf16[64,64,256]{2,1,0:T(8,128)(2,1)S(1)}, u32[]{:S(2)}, u32[]{:S(2)}) collective-permute-start(bf16[64,64,256]{2,1,0:T(8,128)(2,1)S(1)} %bitcast.22), channel_id=1, source_target_pairs={{0,2},{2,0},{1,3},{3,1},{4,6},{6,4},{5,7},{7,5},{8,10},{10,8},{9,1... | collective-permute-start | bytes 6291464 | tf_op jit(solution)/shard_map/ppermute | solution.py:701
  98.2 46.2 %collective-permute-start.4 = (bf16[64,128,128]{2,1,0:T(8,128)(2,1)}, bf16[64,128,128]{2,1,0:T(8,128)(2,1)S(1)}, u32[]{:S(2)}, u32[]{:S(2)}) collective-permute-start(bf16[64,128,128]{2,1,0:T(8,128)(2,1)} %get-tuple-element.70), channel_id=1, source_target_pairs={{0,1},{1,0},{2,3},{3,2},{4,5},{5,4},{6,7},{7,6},{8,9},{9,8},{10,11... | collective-permute-start | bytes 6291464 | tf_op jit(solution)/shard_map/ppermute | solution.py:704
  144.4 3.3 %copy-start.1 = (bf16[64,64,256]{2,1,0:T(8,128)(2,1)}, bf16[64,64,256]{2,1,0:T(8,128)(2,1)S(1)}, u32[]{:S(2)}) copy-start(bf16[64,64,256]{2,1,0:T(8,128)(2,1)S(1)} %collective-permute-done.6.dzp) | copy-start | bytes 6291460
  144.4 1.3 copy-start.8
  144.4 2.6 copy-start.6
  147.6 29.6 %copy-start.2 = (bf16[64,64,256]{2,1,0:T(8,128)(2,1)S(1)}, bf16[64,64,256]{2,1,0:T(8,128)(2,1)}, u32[]{:S(2)}) copy-start(bf16[64,64,256]{2,1,0:T(8,128)(2,1)} %get-tuple-element.65.ao) | copy-start | bytes 6291460
  147.6 30.1 %copy-start.4 = (bf16[64,64,256]{2,1,0:T(8,128)(2,1)S(1)}, bf16[64,64,256]{2,1,0:T(8,128)(2,1)}, u32[]{:S(2)}) copy-start(bf16[64,64,256]{2,1,0:T(8,128)(2,1)} %get-tuple-element.64.ap) | copy-start | bytes 6291460
  177.2 7.6 %collective-permute-start.7 = (bf16[64,128,256]{2,1,0:T(8,128)(2,1)}, bf16[64,128,256]{2,1,0:T(8,128)(2,1)}, u32[]{:S(2)}, u32[]{:S(2)}) collective-permute-start(bf16[64,128,256]{2,1,0:T(8,128)(2,1)} %get-tuple-element.76.dx), channel_id=1, source_target_pairs={{0,1},{1,0},{2,3},{3,2},{4,5},{5,4},{6,7},{7,6},{8,9},{9,8},{10,11... | collective-permute-start | bytes 12582920 | tf_op jit(solution)/shard_map/ppermute | solution.py:704
  177.3 58.1 %collective-permute-start.10 = (bf16[64,64,256]{2,1,0:T(8,128)(2,1)S(1)}, bf16[64,64,256]{2,1,0:T(8,128)(2,1)S(1)}, u32[]{:S(2)}, u32[]{:S(2)}) collective-permute-start(bf16[64,64,256]{2,1,0:T(8,128)(2,1)S(1)} %copy-done.2), channel_id=1, source_target_pairs={{0,1},{1,0},{2,3},{3,2},{4,5},{5,4},{6,7},{7,6},{8,9},{9,8},{10,11... | collective-permute-start | bytes 6291464 | tf_op jit(solution)/shard_map/ppermute | solution.py:704
  177.7 57.6 %collective-permute-start.9 = (bf16[64,64,256]{2,1,0:T(8,128)(2,1)S(1)}, bf16[64,64,256]{2,1,0:T(8,128)(2,1)}, u32[]{:S(2)}, u32[]{:S(2)}) collective-permute-start(bf16[64,64,256]{2,1,0:T(8,128)(2,1)S(1)} %copy-done.4), channel_id=1, source_target_pairs={{0,1},{1,0},{2,3},{3,2},{4,5},{5,4},{6,7},{7,6},{8,9},{9,8},{10,11... | collective-permute-start | bytes 6291464 | tf_op jit(solution)/shard_map/ppermute | solution.py:704
  235.2 4.6 %collective-permute-start.8 = (bf16[64,128,128]{2,1,0:T(8,128)(2,1)}, bf16[64,128,128]{2,1,0:T(8,128)(2,1)}, u32[]{:S(2)}, u32[]{:S(2)}) collective-permute-start(bf16[64,128,128]{2,1,0:T(8,128)(2,1)} %get-tuple-element.82), channel_id=1, source_target_pairs={{0,1},{1,0},{2,3},{3,2},{4,5},{5,4},{6,7},{7,6},{8,9},{9,8},{10,11... | collective-permute-start | bytes 6291464 | tf_op jit(solution)/shard_map/ppermute | solution.py:704
  235.4 4.4 %copy-start.7 = (bf16[64,64,256]{2,1,0:T(8,128)(2,1)}, bf16[64,64,256]{2,1,0:T(8,128)(2,1)S(1)}, u32[]{:S(2)}) copy-start(bf16[64,64,256]{2,1,0:T(8,128)(2,1)S(1)} %collective-permute-done.10.ro) | copy-start | bytes 6291460

commit v2 on v1

--- a/solution.py
+++ b/solution.py
@@ -21,7 +21,7 @@
 MEGA = 10 ** 6
 GIGA = 10 ** 9
 MIB = 2 ** 20
-VMEM_LIMIT = 56 * 1024 * 1024
+VMEM_LIMIT = 67043328
 
 
 MESH_ID = pl.DeviceIdType.MESH
@@ -89,7 +89,7 @@
 KA = C + RB
 
 
-def prep_kernel(w_proj, b_proj, ln_in, w_out, b_out, wt_aug, wot_aug, gain, lbias, perm, scr):
+def prep_kernel(ids, lnmid, w_proj, b_proj, ln_in, w_out, b_out, wt_aug, wot_aug, gain, lbias, perm, scr):
     n = gain.shape[-1]
     for k in range(2):
         scr[:] = jnp.zeros_like(scr)
@@ -109,11 +109,11 @@
     perm[:] = jnp.where(q == RB * (r % RB) + r // RB, 1.0, 0.0).astype(BF16)
 
 
-def prepare(n, ln_in, w_proj, b_proj, w_out, b_out):
+def prepare(n, ids, lnmid, ln_in, w_proj, b_proj, w_out, b_out):
     sds = jax.ShapeDtypeStruct
     outs = [sds((2, 5 * C, KA), BF16), sds((2, C, KA), BF16), sds((2, C, n), F32), sds((2, C, n), F32), sds((W2, W2), BF16)]
     args = (w_proj, b_proj.astype(F32), ln_in.astype(F32), w_out, b_out.astype(F32))
-    return call(prep_kernel, (1,), [full_spec(v.shape) for v in args], [full_spec(o.shape) for o in outs], outs, [pltpu.VMEM((LANES, 384), F32)], MEGA, MIB)(*args)
+    return call(prep_kernel, (1,), [SMEM_SPEC, SMEM_SPEC] + [full_spec(v.shape) for v in args], [full_spec(o.shape) for o in outs], outs, [pltpu.VMEM((LANES, 384), F32)], MEGA, MIB)(ids, lnmid, *args)
 
 
 def with_ones(zh):
@@ -170,7 +170,7 @@
         [cspec] * 2, [jax.ShapeDtypeStruct((C, rows, n), BF16)] * 2, [pltpu.VMEM((RB, C, n), BF16)] * 2, GIGA, 8 * MIB)(z, mask, *args, par[-1])
 
 
-CB = 8
+CB = 16
 T_STEPS = C // CB
 
 
@@ -703,8 +703,8 @@
         def over_c(v):
             return lax.ppermute(v, "dap", c_pairs)
 
-        par = prepare(n, ln_in, w_proj, b_proj, w_out, b_out)
         lnmid = ln_mid.astype(F32)
+        par = prepare(n, ids, lnmid, ln_in, w_proj, b_proj, w_out, b_out)
         m_own = pair_mask[0]
         z_own = jnp.transpose(z_pair[0], (0, 2, 1))
         dz_own = jnp.transpose(dz_out[0], (0, 2, 1))

time: 288 us -> 276 us (0.958)
  Pallas kernels: 177 us -> 168 us
  local copies, waits for them, and re-layouts: 4.54 us -> 0 us
    unnamed x22 -> x0, local copies, waits for them, and re-layouts: 4.54 us -> none
  transfers between devices with their start and end apart: 11 -> 11, of which waited for: 6 -> 6; matrix products, arithmetic and copies ran while one was open for 2% -> 2% of each run, Pallas kernels for 23% -> 24%
where the time goes in v2:
time: 276 us; the launch traced here: 275 us
  Pallas kernels  168 us (61%)
  waiting for transfers between devices  94.5 us (34%)
  starting transfers between devices  6.03 us (2%)
  other arithmetic  5.59 us (2%)
    ppermute x3, waiting for transfers between devices, over_x(): return lax.ppermute(v, 'dap', x_pairs)  78.8 us
    pallas_call x1, Pallas kernels, back_fused(): call(back_kernel, (T_STEPS + 8,), [SMEM_SPEC] + [tri_spec(v.shape) for v...  48.2 us
    pallas_call x1, Pallas kernels, fwd_fused(): call(fwd_kernel, (T_STEPS + 8,), [SMEM_SPEC] + [tri_spec(v.shape) for v i...  30.3 us
    pallas_call x1, Pallas kernels, turn_fused(): call(turn_kernel, (T_STEPS + 8,), [SMEM_SPEC] + [tri_spec(v.shape) for v...  27.6 us
    pallas_call x1, Pallas kernels, sum_grads(): pl.pallas_call(functools.partial(grads_kernel, n_dp, n_dap), out_shape=ja...  23.3 us
    pallas_call x1, Pallas kernels, last_fused(): call(last_kernel, (T_STEPS + 4,), [SMEM_SPEC, tri_spec((C, C, n), 1)] + [...  20.7 us
    ppermute x8, waiting for transfers between devices, over_c(): return lax.ppermute(v, 'dap', c_pairs)  15.8 us
    pallas_call x2, Pallas kernels, pre_forward(): call(pre_fwd_kernel, (rows // RB,), [pl.BlockSpec((RB, C, n), lambda s: (...  14.6 us
  transfers between devices with their start and end apart: 11, of which 6 were waited for; matrix products, arithmetic and copies ran while one was open for 2% of the time, Pallas kernels for 24%

profile of v2, /device:TPU:0, one launch (start us, length us, event | category | flops | bytes accessed | tf_op | source)
XLA Modules:
  0.0 275.3 jit_solution(17443440522359078700)
XLA Ops:
  0.6 3.0 %collective-permute-start = (bf16[64,64,256]{2,1,0:T(8,128)(2,1)}, bf16[64,64,256]{2,1,0:T(8,128)(2,1)}, u32[]{:S(2)}, u32[]{:S(2)}) collective-permute-start(bf16[64,64,256]{2,1,0:T(8,128)(2,1)} %bitcast.15), channel_id=1, source_target_pairs={{0,2},{2,0},{1,3},{3,1},{4,6},{6,4},{5,7},{7,5},{8,10},{10,8},{9,1... | collective-permute-start | bytes 6291464 | tf_op jit(solution)/shard_map/ppermute | solution.py:701
  3.7 0.1 collective-permute-start.1
  3.7 1.3 convert_element_type.12.lnmid
  5.0 1.3 convert_element_type.13.b_proj
  6.3 1.3 convert_element_type.14.ln_in
  7.5 1.2 convert_element_type.15.b_out
  8.7 0.6 pad_add_fusion.ids
  9.3 2.0 shard_map.152
  11.3 7.3 %shard_map.154 = (bf16[64,64,256]{2,1,0:T(8,128)(2,1)}, bf16[64,64,256]{2,1,0:T(8,128)(2,1)}) custom-call(bf16[64,64,256]{2,1,0:T(8,128)(2,1)} %bitcast.16, s32[64,256]{1,0:T(8,128)} %bitcast.24, bf16[2,320,80]{2,1,0:T(8,128)(2,1)} %get-tuple-element.60.wt.wt0.wt1, f32[2,64,256]{2,1,0:T(8,128)} %get-tuple-element.61.gain.gain0.gain1, ...), custom_call_target="tpu_custom_call" | custom-call | flops 1000000000 | bytes 8388608 | tf_op jit(solution)/shard_map/pallas_call | solution.py:167
  18.6 0.0 collective-permute-start.3
  18.6 31.7 %collective-permute-done.z.zp = bf16[64,64,256]{2,1,0:T(8,128)(2,1)} collective-permute-done((bf16[64,64,256]{2,1,0:T(8,128)(2,1)}, bf16[64,64,256]{2,1,0:T(8,128)(2,1)}, u32[]{:S(2)}, u32[]{:S(2)}) %collective-permute-start) | collective-permute-done | bytes 2097184 | tf_op jit(solution)/shard_map/ppermute | solution.py:701
  50.3 0.7 collective-permute-done.1.mask.mp
  51.0 7.3 %shard_map.153 = (bf16[64,64,256]{2,1,0:T(8,128)(2,1)}, bf16[64,64,256]{2,1,0:T(8,128)(2,1)}) custom-call(bf16[64,64,256]{2,1,0:T(8,128)(2,1)} %collective-permute-done.z.zp, s32[64,256]{1,0:T(8,128)} %collective-permute-done.1.mask.mp, bf16[2,320,80]{2,1,0:T(8,128)(2,1)} %get-tuple-element.60.wt.wt0.wt1, f32[2,64,256]{2,1,0:T(8,128)} %get-tuple-element.61.gain.gain0.gain1, ...), custom_call_target="tpu_custom_call" | custom-call | flops 1000000000 | bytes 8388608 | tf_op jit(solution)/shard_map/pallas_call | solution.py:167
  58.3 0.0 collective-permute-start.2
  58.3 0.0 collective-permute-done.3.qo
  58.3 4.5 %collective-permute-done.2.qp = bf16[64,64,256]{2,1,0:T(8,128)(2,1)} collective-permute-done((bf16[64,64,256]{2,1,0:T(8,128)(2,1)}, bf16[64,64,256]{2,1,0:T(8,128)(2,1)}, u32[]{:S(2)}, u32[]{:S(2)}) %collective-permute-start.2) | collective-permute-done | bytes 2097184 | tf_op jit(solution)/shard_map/ppermute | solution.py:704
  62.8 30.3 %shard_map.155 = (bf16[128,64,256]{2,1,0:T(8,128)(2,1)}, f32[64,128,256]{2,1,0:T(8,128)}, f32[128,256]{1,0:T(8,128)}, bf16[64,128,256]{2,1,0:T(8,128)(2,1)}, bf1...) custom-call(s32[2]{0:T(128)} %pad_add_fusion.ids, ...), custom_call_target="tpu_custom_call" | custom-call | flops 1000000000 | bytes 41943040 | tf_op jit(solution)/shard_map/pallas_call | solution.py:316
  93.1 0.2 collective-permute-start.5
  93.3 1.7 collective-permute-start.6
  95.0 0.1 collective-permute-start.4
  95.1 46.4 %collective-permute-done.6.dzp = bf16[64,64,256]{2,1,0:T(8,128)(2,1)} collective-permute-done((bf16[64,64,256]{2,1,0:T(8,128)(2,1)}, bf16[64,64,256]{2,1,0:T(8,128)(2,1)}, u32[]{:S(2)}, u32[]{:S(2)}) %collective-permute-start.6) | collective-permute-done | bytes 2097184 | tf_op jit(solution)/shard_map/ppermute | solution.py:701
  141.5 0.0 collective-permute-done.4.ar
  141.5 0.0 collective-permute-done.5.bq
  141.5 27.6 %shard_map.156 = (bf16[64,64,256]{2,1,0:T(8,128)(2,1)}, bf16[64,128,256]{2,1,0:T(8,128)(2,1)}, bf16[128,64,256]{2,1,0:T(8,128)(2,1)}, f32[64,128]{1,0:T(8,128)},...) custom-call(s32[2]{0:T(128)} %pad_add_fusion.ids, ...), custom_call_target="tpu_custom_call" | custom-call | flops 1000000000 | bytes 41943040 | tf_op jit(solution)/shard_map/pallas_call | solution.py:407
  169.2 0.1 collective-permute-start.7
  169.3 0.5 collective-permute-start.10
  169.7 0.1 collective-permute-start.9
  169.8 6.9 %collective-permute-done.7.dxq = bf16[64,128,256]{2,1,0:T(8,128)(2,1)} collective-permute-done((bf16[64,128,256]{2,1,0:T(8,128)(2,1)}, bf16[64,128,256]{2,1,0:T(8,128)(2,1)}, u32[]{:S(2)}, u32[]{:S(2)}) %collective-permute-start.7) | collective-permute-done | bytes 4194336 | tf_op jit(solution)/shard_map/ppermute | solution.py:704
  176.7 48.2 %shard_map.157 = (bf16[64,64,256]{2,1,0:T(8,128)(2,1)}, bf16[64,128,256]{2,1,0:T(8,128)(2,1)}, bf16[64,128,128]{2,1,0:T(8,128)(2,1)}, bf16[64,128,128]{2,1,0:T(8...) custom-call(s32[2]{0:T(128)} %pad_add_fusion.ids, ...), custom_call_target="tpu_custom_call" | custom-call | flops 1000000000 | bytes 62914560 | tf_op jit(solution)/shard_map/pallas_call | solution.py:519
  225.0 0.2 collective-permute-start.8
  225.2 0.0 collective-permute-done.10.ro
  225.2 0.0 collective-permute-done.9.rp
  225.2 4.3 %collective-permute-done.8.dxr = bf16[64,128,128]{2,1,0:T(8,128)(2,1)} collective-permute-done((bf16[64,128,128]{2,1,0:T(8,128)(2,1)}, bf16[64,128,128]{2,1,0:T(8,128)(2,1)}, u32[]{:S(2)}, u32[]{:S(2)}) %collective-permute-start.8) | collective-permute-done | bytes 2097184 | tf_op jit(solution)/shard_map/ppermute | solution.py:704
  229.5 20.7 %shard_map.158 = (bf16[64,64,256]{2,1,0:T(8,128)(2,1)}, f32[320,64]{1,0:T(8,128)}, f32[256,128]{1,0:T(8,128)}, f32[64,128]{1,0:T(8,128)}, f32[64,128]{1,0:T(8,128)}) custom-call(s32[2]{0:T(128)} %pad_add_fusion.ids, bf16[64,128,256]{2,1,0:T(8,128)(2,1)} %get-tuple-element.80.dx, bf16[64,64,256]{2,1,0:T(8,128)(2,1)} %get-tuple-element.66.bp, ...), custom_call_target="tpu_custom_call" | custom-call | flops 1000000000 | bytes 41943040 | tf_op jit(solution)/shard_map/pallas_call | solution.py:560
  250.2 23.3 %grad_sum.1.src = f32[512,128]{1,0:T(8,128)} custom-call(f32[320,64]{1,0:T(8,128)} %get-tuple-element.86.w0, f32[256,128]{1,0:T(8,128)} %get-tuple-element.87.b0, f32[64,128]{1,0:T(8,128)} %get-tuple-element.88.q0, f32[64,128]{1,0:T(8,128)} %get-tuple-element.89.g0, f32[64,128]{1,0:T(8,128)} %get-tuple-element.90.l0, f32[64,64]{1,0:T(8,128)} %get-tuple-element.91.wo0, ...), custom_call_target="tpu_custom_call" | custom-call | flops 1000000 | bytes 1048576 | tf_op jit(solution)/shard_map/grad_sum/pallas_call | solution.py:656
  273.6 1.8 shard_map.159
Async XLA Ops:
  0.6 49.7 %collective-permute-start = (bf16[64,64,256]{2,1,0:T(8,128)(2,1)}, bf16[64,64,256]{2,1,0:T(8,128)(2,1)}, u32[]{:S(2)}, u32[]{:S(2)}) collective-permute-start(bf16[64,64,256]{2,1,0:T(8,128)(2,1)} %bitcast.15), channel_id=1, source_target_pairs={{0,2},{2,0},{1,3},{3,1},{4,6},{6,4},{5,7},{7,5},{8,10},{10,8},{9,1... | collective-permute-start | bytes 6291464 | tf_op jit(solution)/shard_map/ppermute | solution.py:701
  3.7 47.4 %collective-permute-start.1 = (s32[64,256]{1,0:T(8,128)}, s32[64,256]{1,0:T(8,128)}, u32[]{:S(2)}, u32[]{:S(2)}) collective-permute-start(s32[64,256]{1,0:T(8,128)} %bitcast.23), channel_id=1, source_target_pairs={{0,2},{2,0},{1,3},{3,1},{4,6},{6,4},{5,7},{7,5},{8,10},{10,8},{9,1... | collective-permute-start | bytes 196616 | tf_op jit(solution)/shard_map/ppermute | solution.py:701
  18.6 39.7 %collective-permute-start.3 = (bf16[64,64,256]{2,1,0:T(8,128)(2,1)}, bf16[64,64,256]{2,1,0:T(8,128)(2,1)}, u32[]{:S(2)}, u32[]{:S(2)}) collective-permute-start(bf16[64,64,256]{2,1,0:T(8,128)(2,1)} %get-tuple-element.67.bo), channel_id=1, source_target_pairs={{0,1},{1,0},{2,3},{3,2},{4,5},{5,4},{6,7},{7,6},{8,9},{9,8},{10,11... | collective-permute-start | bytes 6291464 | tf_op jit(solution)/shard_map/ppermute | solution.py:704
  58.3 4.5 %collective-permute-start.2 = (bf16[64,64,256]{2,1,0:T(8,128)(2,1)}, bf16[64,64,256]{2,1,0:T(8,128)(2,1)}, u32[]{:S(2)}, u32[]{:S(2)}) collective-permute-start(bf16[64,64,256]{2,1,0:T(8,128)(2,1)} %get-tuple-element.66.bp), channel_id=1, source_target_pairs={{0,1},{1,0},{2,3},{3,2},{4,5},{5,4},{6,7},{7,6},{8,9},{9,8},{10,11... | collective-permute-start | bytes 6291464 | tf_op jit(solution)/shard_map/ppermute | solution.py:704
  93.1 48.4 %collective-permute-start.5 = (bf16[64,128,256]{2,1,0:T(8,128)(2,1)}, bf16[64,128,256]{2,1,0:T(8,128)(2,1)}, u32[]{:S(2)}, u32[]{:S(2)}) collective-permute-start(bf16[64,128,256]{2,1,0:T(8,128)(2,1)} %get-tuple-element.71.b), channel_id=1, source_target_pairs={{0,1},{1,0},{2,3},{3,2},{4,5},{5,4},{6,7},{7,6},{8,9},{9,8},{10,11... | collective-permute-start | bytes 12582920 | tf_op jit(solution)/shard_map/ppermute | solution.py:704
  93.3 48.2 %collective-permute-start.6 = (bf16[64,64,256]{2,1,0:T(8,128)(2,1)}, bf16[64,64,256]{2,1,0:T(8,128)(2,1)}, u32[]{:S(2)}, u32[]{:S(2)}) collective-permute-start(bf16[64,64,256]{2,1,0:T(8,128)(2,1)} %bitcast.20), channel_id=1, source_target_pairs={{0,2},{2,0},{1,3},{3,1},{4,6},{6,4},{5,7},{7,5},{8,10},{10,8},{9,1... | collective-permute-start | bytes 6291464 | tf_op jit(solution)/shard_map/ppermute | solution.py:701
  95.0 46.5 %collective-permute-start.4 = (bf16[64,128,128]{2,1,0:T(8,128)(2,1)}, bf16[64,128,128]{2,1,0:T(8,128)(2,1)}, u32[]{:S(2)}, u32[]{:S(2)}) collective-permute-start(bf16[64,128,128]{2,1,0:T(8,128)(2,1)} %get-tuple-element.70), channel_id=1, source_target_pairs={{0,1},{1,0},{2,3},{3,2},{4,5},{5,4},{6,7},{7,6},{8,9},{9,8},{10,11... | collective-permute-start | bytes 6291464 | tf_op jit(solution)/shard_map/ppermute | solution.py:704
  169.2 7.6 %collective-permute-start.7 = (bf16[64,128,256]{2,1,0:T(8,128)(2,1)}, bf16[64,128,256]{2,1,0:T(8,128)(2,1)}, u32[]{:S(2)}, u32[]{:S(2)}) collective-permute-start(bf16[64,128,256]{2,1,0:T(8,128)(2,1)} %get-tuple-element.76.dx), channel_id=1, source_target_pairs={{0,1},{1,0},{2,3},{3,2},{4,5},{5,4},{6,7},{7,6},{8,9},{9,8},{10,11... | collective-permute-start | bytes 12582920 | tf_op jit(solution)/shard_map/ppermute | solution.py:704
  169.3 55.9 %collective-permute-start.10 = (bf16[64,64,256]{2,1,0:T(8,128)(2,1)}, bf16[64,64,256]{2,1,0:T(8,128)(2,1)}, u32[]{:S(2)}, u32[]{:S(2)}) collective-permute-start(bf16[64,64,256]{2,1,0:T(8,128)(2,1)} %get-tuple-element.65.ao), channel_id=1, source_target_pairs={{0,1},{1,0},{2,3},{3,2},{4,5},{5,4},{6,7},{7,6},{8,9},{9,8},{10,11... | collective-permute-start | bytes 6291464 | tf_op jit(solution)/shard_map/ppermute | solution.py:704
  169.7 55.4 %collective-permute-start.9 = (bf16[64,64,256]{2,1,0:T(8,128)(2,1)}, bf16[64,64,256]{2,1,0:T(8,128)(2,1)}, u32[]{:S(2)}, u32[]{:S(2)}) collective-permute-start(bf16[64,64,256]{2,1,0:T(8,128)(2,1)} %get-tuple-element.64.ap), channel_id=1, source_target_pairs={{0,1},{1,0},{2,3},{3,2},{4,5},{5,4},{6,7},{7,6},{8,9},{9,8},{10,11... | collective-permute-start | bytes 6291464 | tf_op jit(solution)/shard_map/ppermute | solution.py:704
  225.0 4.6 %collective-permute-start.8 = (bf16[64,128,128]{2,1,0:T(8,128)(2,1)}, bf16[64,128,128]{2,1,0:T(8,128)(2,1)}, u32[]{:S(2)}, u32[]{:S(2)}) collective-permute-start(bf16[64,128,128]{2,1,0:T(8,128)(2,1)} %get-tuple-element.82), channel_id=1, source_target_pairs={{0,1},{1,0},{2,3},{3,2},{4,5},{5,4},{6,7},{7,6},{8,9},{9,8},{10,11... | collective-permute-start | bytes 6291464 | tf_op jit(solution)/shard_map/ppermute | solution.py:704

commit v3 on v2

--- a/solution.py
+++ b/solution.py
@@ -216,8 +216,14 @@
     return pl.BlockSpec((RB, n), lambda s: (row_blk(s), 0))
 
 
-def pick(r, peer, own):
-    return jnp.where(r < 4, peer, own)
+def pick(own, peer_ref, own_ref, at):
+    return (own_ref if own else peer_ref)[at]
+
+
+def each_half(step, body):
+    r = step - T_STEPS
+    pl.when((r >= 0) & (r < 4))(lambda: body(r, False))
+    pl.when(r >= 4)(lambda: body(r, True))
 
 
 def channels(step):
@@ -267,19 +273,17 @@
             place(buf, (bp[ch], bo[ch]), (qp[ch], qo[ch]), ids)
             x_s[dst] = dot_nt(jnp.concatenate([ap[ch], ao[ch]], axis=0), buf[:])
 
-    @pl.when(step >= T_STEPS)
-    def _():
-        r = step - T_STEPS
+    def body(r, own):
         mid_norm(x_s.at[:, pl.ds(pl.multiple_of(r * RB, RB), RB), :], xh_s, lnmid, 0, xn, rstd)
         to_rows(perm[:], xh_s, xi_s)
 
         def update(i):
-            zf = pick(r, zp[i], zo[i]).astype(F32)
+            zf = pick(own, zp, zo, i).astype(F32)
             upd = dot_nn(wot0[:], with_ones(xi_s[i]))
             zmid[i] = (zf + (1.0 + gate_of(zf, wt0, gain0, lbias0)) * upd).astype(BF16)
 
         def sides(i):
-            m = pick(r, mp[pl.ds(i, 1), :], mo[pl.ds(i, 1), :]).astype(F32)
+            m = pick(own, mp, mo, (pl.ds(i, 1), slice(None))).astype(F32)
             a_s[i], b_s[i] = project(zmid[i].astype(F32), m, wt1, gain1, lbias1)
 
         staggered(update, sides)
@@ -295,6 +299,8 @@
 
         to_cmajor(perm[:], a_s, put_a)
         to_cmajor(perm[:], b_s, put_b)
+
+    each_half(step, body)
 
 
 def weights_specs(par, blk, with_out):
@@ -322,7 +328,7 @@
         GIGA, 40 * MIB)(ids, *sides, zp, zo, *masks, *w0, *w1, lnmid, par[-1])
 
 
-def mid_back(dxc_s, xn, rstd, lnmid, blk, acc_mg, acc_mb, emit):
+def mid_back(own, dxc_s, xn, rstd, lnmid, blk, acc_mg, acc_mb, emit):
     m1 = m2 = None
     for c in range(C):
         dy = dxc_s[c]
@@ -330,8 +336,9 @@
         gn = lnmid[blk, 0, c]
         m1 = dy * gn if m1 is None else m1 + dy * gn
         m2 = dyx * gn if m2 is None else m2 + dyx * gn
-        acc_mg[c] += fold(dyx[0:8] + dyx[8:RB])
-        acc_mb[c] += fold(dy[0:8] + dy[8:RB])
+        if own:
+            acc_mg[c] += fold(dyx[0:8] + dyx[8:RB])
+            acc_mb[c] += fold(dy[0:8] + dy[8:RB])
     m1 = m1 * (1.0 / C)
     m2 = m2 * (1.0 / C)
     for c in range(C):
@@ -357,33 +364,35 @@
             x_s[dst, pl.ds(pl.multiple_of(C * (1 - xx), C), C), :] = out[0:C]
             x_s[dst, pl.ds(pl.multiple_of(C * xx, C), C), :] = out[C:LANES]
 
-    @pl.when(step >= T_STEPS)
-    def _():
-        r = step - T_STEPS
+    def body(r, own):
         mid_norm(x_s.at[:, pl.ds(pl.multiple_of(r * RB, RB), RB), :], xh_s, lnmid, 1, xn_s, r_s)
         to_rows(perm[:], xh_s, xi_s)
         sums = [acc_bg[:], acc_bo[:], acc_wo[:]]
 
         def gates(i):
             zf = z[i].astype(F32)
-            dz = pick(r, dzp[i], dzo[i]).astype(F32)
+            dz = pick(own, dzp, dzo, i).astype(F32)
             t = gate_of(zf, wt, gain, lbias)
             upd = dot_nn(wot[:], with_ones(xi_s[i]))
             t1 = 1.0 + t
-            znew[i] = (zf + t1 * upd).astype(BF16)
+            if own:
+                znew[i] = (zf + t1 * upd).astype(BF16)
             d_upd = (HALF * dz) * t1
             d_pg = d_upd * (upd * (1.0 - t))
             dpg[i] = d_pg.astype(BF16)
             dub_s[i] = d_upd.astype(BF16)
-            sums[0] += fold(d_pg)
-            sums[1] += fold(d_upd)
+            if own:
+                sums[0] += fold(d_pg)
+                sums[1] += fold(d_upd)
 
         def products(i):
             dxi_s[i] = dot_nn(wo[:], dub_s[i]).astype(BF16)
-            sums[2] += dot_nt(dub_s[i], xi_s[i])
+            if own:
+                sums[2] += dot_nt(dub_s[i], xi_s[i])
 
         staggered(gates, products)
-        acc_bg[:], acc_bo[:], acc_wo[:] = sums
+        if own:
+            acc_bg[:], acc_bo[:], acc_wo[:] = sums
 
         def put(grp, v):
             dxc_s[grp * RB:(grp + 1) * RB] = v
@@ -393,7 +402,9 @@
         def emit(c, v):
             dx[c] = v.astype(BF16)
 
-        mid_back(dxc_s, xn_s, r_s[:], lnmid, 1, acc_mg, acc_mb, emit)
+        mid_back(own, dxc_s, xn_s, r_s[:], lnmid, 1, acc_mg, acc_mb, emit)
+
+    each_half(step, body)
 
 
 ACC_POST = ((C, LANES), (C, LANES), (C, C), (C, 8, LANES), (C, 8, LANES))
@@ -413,7 +424,7 @@
         GIGA, 40 * MIB)(ids, *sides, z_mid, *dz_parts, *w1, w_out, lnmid, par[-1])
 
 
-def pre_back_stages(z, dpg, mask_of, res_of, dst, wt, w, gain, lbias, dai_s, dbi_s, dp_s, zh_s, zn_s, rs_s, acc_b, sums):
+def pre_back_stages(own, z, dpg, mask_of, res_of, dst, wt, w, gain, lbias, dai_s, dbi_s, dp_s, zh_s, zn_s, rs_s, acc_b, sums):
     def gates(i):
         zn, rstd = norm_rows(z[i].astype(F32))
         zn_s[i] = zn
@@ -429,17 +440,19 @@
             dv = dm * (1.0 + t)
             dg = dv * (p[base + C:base + 2 * C] * (1.0 - t))
             for k, d in ((2 * side, dg), (2 * side + 1, dv)):
-                acc_b[k * C:(k + 1) * C] += fold(d)
+                if own:
+                    acc_b[k * C:(k + 1) * C] += fold(d)
                 dp_s[i, k * C:(k + 1) * C] = d.astype(BF16)
         dp_s[i, 4 * C:5 * C] = dpg[i]
 
     def products(i):
         dp = dp_s[i]
         dzh = dot_nn(w[:], dp).astype(BF16).astype(F32)
-        sums[0] += dot_nt(dp, zh_s[i])
         zn, rstd = zn_s[i], rs_s[i, 0:1, :]
-        sums[1] += fold(dzh * zn)
-        sums[2] += fold(dzh)
+        if own:
+            sums[0] += dot_nt(dp, zh_s[i])
+            sums[1] += fold(dzh * zn)
+            sums[2] += fold(dzh)
         dzn = dzh * gain[:]
         m1 = jnp.mean(dzn, axis=0, keepdims=True)
         m2 = jnp.mean(dzn * zn, axis=0, keepdims=True)
@@ -460,9 +473,7 @@
             da_s[dst] = dot_nt(b[ch], buf[:]).astype(BF16)
             db_s[dst] = dot_nn(a[ch], buf[:]).astype(BF16)
 
-    @pl.when(step >= T_STEPS)
-    def _():
-        r = step - T_STEPS
+    def body(r, own):
         rows = pl.ds(pl.multiple_of(r * RB, RB), RB)
         to_rows(perm[:], da_s.at[:, rows, :], dai_s)
         to_rows(perm[:], db_s.at[:, rows, :], dbi_s)
@@ -471,28 +482,32 @@
         to_rows(perm[:], xh_s, xi_s)
         pre = [acc_w[:], acc_g[:], acc_lb[:]]
         pre_gates, pre_products = pre_back_stages(
-            z, dpg1, lambda i: pick(r, mp[pl.ds(i, 1), :], mo[pl.ds(i, 1), :]), lambda i: pick(r, dzp[i], dzo[i]), dzm,
+            own, z, dpg1, lambda i: pick(own, mp, mo, (pl.ds(i, 1), slice(None))), lambda i: pick(own, dzp, dzo, i), dzm,
             wt1, w1, gain1, lbias1, dai_s, dbi_s, dp_s, zh_s, zn_s, rs_s, acc_b, pre)
         staggered(pre_gates, pre_products)
-        acc_w[:], acc_g[:], acc_lb[:] = pre
+        if own:
+            acc_w[:], acc_g[:], acc_lb[:] = pre
         post = [acc_bg[:], acc_bo[:], acc_wo[:]]
 
         def gates(i):
-            t = gate_of(pick(r, zp[i], zo[i]).astype(F32), wt0, gain0, lbias0)
+            t = gate_of(pick(own, zp, zo, i).astype(F32), wt0, gain0, lbias0)
             upd = dot_nn(wot0[:], with_ones(xi_s[i]))
             d_upd = (HALF * dzm[i].astype(F32)) * (1.0 + t)
             d_pg = d_upd * (upd * (1.0 - t))
             dpg0[i] = d_pg.astype(BF16)
             dub_s[i] = d_upd.astype(BF16)
-            post[0] += fold(d_pg)
-            post[1] += fold(d_upd)
+            if own:
+                post[0] += fold(d_pg)
+                post[1] += fold(d_upd)
 
         def products(i):
             dxi_s[i] = dot_nn(wo0[:], dub_s[i]).astype(BF16)
-            post[2] += dot_nt(dub_s[i], xi_s[i])
+            if own:
+                post[2] += dot_nt(dub_s[i], xi_s[i])
 
         staggered(gates, products)
-        acc_bg[:], acc_bo[:], acc_wo[:] = post
+        if own:
+            acc_bg[:], acc_bo[:], acc_wo[:] = post
 
         def put(grp, v):
             dxc_s[grp * RB:(grp + 1) * RB] = v
@@ -505,7 +520,9 @@
             dxk[c] = mine.astype(BF16)
             dxs[c] = other.astype(BF16)
 
-        mid_back(dxc_s, xn, rstd[:], lnmid, 0, acc_mg, acc_mb, emit)
+        mid_back(own, dxc_s, xn, rstd[:], lnmid, 0, acc_mg, acc_mb, emit)
+
+    each_half(step, body)
 
 
 def back_fused(ids, sides, z_mid, dpg1, dz_parts, masks, xn, rstd, z_parts, par, w_proj, w_out, lnmid):
@@ -547,7 +564,7 @@
         to_rows(perm[:], db_s.at[:, rows, :], dbi_s)
         sums = [acc_w[:], acc_g[:], acc_lb[:]]
         staggered(*pre_back_stages(
-            z, dpg, lambda i: mask[pl.ds(i, 1), :], lambda i: dres[i], dz,
+            True, z, dpg, lambda i: mask[pl.ds(i, 1), :], lambda i: dres[i], dz,
             wt, w, gain, lbias, dai_s, dbi_s, dp_s, zh_s, zn_s, rs_s, acc_b, sums))
         acc_w[:], acc_g[:], acc_lb[:] = sums
 
@@ -579,26 +596,26 @@
         pl.semaphore_signal(bar, inc=1, device_id=(lax.rem(dp + k, n_dp), dap), device_id_type=MESH_ID)
 
     buf[0:5 * C, 0:C] = w0[:]
-    buf[0:5 * C, C:2 * C] = HALF * w1[:]
-    buf[5 * C:6 * C, 0:C] = HALF * wo0[:]
-    buf[5 * C:6 * C, C:2 * C] = HALF * wo1[:]
-
-    def put(k, base, ref, scale):
+    buf[0:5 * C, C:2 * C] = w1[:]
+    buf[5 * C:6 * C, 0:C] = wo0[:]
+    buf[5 * C:6 * C, C:2 * C] = wo1[:]
+
+    def put(k, base, ref):
         v = ref[:]
         if v.ndim == 3:
             v = jnp.sum(v, axis=1)
         rows = v.shape[0]
-        tot = scale * jnp.sum(v, axis=1, keepdims=True)
+        tot = jnp.sum(v, axis=1, keepdims=True)
         lane = lax.broadcasted_iota(jnp.int32, (rows, LANES), 1)
         vec[base:base + rows, :] = jnp.where(lane == k, tot, vec[base:base + rows, :])
 
     vec[:] = jnp.zeros_like(vec)
-    put(0, 0, b0, 1.0)
-    put(0, 4 * C, q0, HALF)
-    put(1, 0, b1, HALF)
-    put(1, 4 * C, q1, HALF)
-    for k, (ref, scale) in enumerate(((g0, 1.0), (l0, 1.0), (g1, HALF), (l1, HALF), (mg0, HALF), (mb0, HALF), (mg1, HALF), (mb1, HALF), (o0, HALF), (o1, HALF))):
-        put(2 + k, 0, ref, scale)
+    put(0, 0, b0)
+    put(0, 4 * C, q0)
+    put(1, 0, b1)
+    put(1, 4 * C, q1)
+    for k, ref in enumerate((g0, l0, g1, l1, mg0, mb0, mg1, mb1, o0, o1)):
+        put(2 + k, 0, ref)
     vt = jnp.transpose(vec[:])
     for t in range(3):
         buf[6 * C + RB * t:6 * C + RB * t + RB, :] = vt[0:RB, LANES * t:LANES * (t + 1)]

time: 276 us -> 272 us (0.986)
  Pallas kernels: 168 us -> 165 us
    pallas_call x1, Pallas kernels: 48.2 us -> 45.3 us  [back_fused(): call(back_kernel, (T_STEPS + 8,), [SMEM_SPEC] + [tri_spec(v.shape) for v...]
  transfers between devices with their start and end apart: 11 -> 11, of which waited for: 6 -> 6; matrix products, arithmetic and copies ran while one was open for 2% -> 2% of each run, Pallas kernels for 24% -> 23%
where the time goes in v3:
time: 272 us
  Pallas kernels  165 us (61%)
  waiting for transfers between devices  94.6 us (35%)
  starting transfers between devices  6.02 us (2%)
  other arithmetic  5.59 us (2%)
    ppermute x3, waiting for transfers between devices, over_x(): return lax.ppermute(v, 'dap', x_pairs)  78.8 us
    pallas_call x1, Pallas kernels, back_fused(): call(back_kernel, (T_STEPS + 8,), [SMEM_SPEC] + [tri_spec(v.shape) for v...  45.3 us
    pallas_call x1, Pallas kernels, fwd_fused(): call(fwd_kernel, (T_STEPS + 8,), [SMEM_SPEC] + [tri_spec(v.shape) for v i...  29.8 us
    pallas_call x1, Pallas kernels, turn_fused(): call(turn_kernel, (T_STEPS + 8,), [SMEM_SPEC] + [tri_spec(v.shape) for v...  27.2 us
    pallas_call x1, Pallas kernels, sum_grads(): pl.pallas_call(functools.partial(grads_kernel, n_dp, n_dap), out_shape=ja...  23.3 us
    pallas_call x1, Pallas kernels, last_fused(): call(last_kernel, (T_STEPS + 4,), [SMEM_SPEC, tri_spec((C, C, n), 1)] + [...  20.9 us
    ppermute x8, waiting for transfers between devices, over_c(): return lax.ppermute(v, 'dap', c_pairs)  15.8 us
    pallas_call x2, Pallas kernels, pre_forward(): call(pre_fwd_kernel, (rows // RB,), [pl.BlockSpec((RB, C, n), lambda s: (...  14.6 us
  transfers between devices with their start and end apart: 11, of which 6 were waited for; matrix products, arithmetic and copies ran while one was open for 2% of the time, Pallas kernels for 23%

profile of v3, /device:TPU:0, one launch (start us, length us, event | category | flops | bytes accessed | tf_op | source)
XLA Modules:
  0.0 271.9 jit_solution(14834036532803979973)
XLA Ops:
  0.6 3.0 %collective-permute-start = (bf16[64,64,256]{2,1,0:T(8,128)(2,1)}, bf16[64,64,256]{2,1,0:T(8,128)(2,1)}, u32[]{:S(2)}, u32[]{:S(2)}) collective-permute-start(bf16[64,64,256]{2,1,0:T(8,128)(2,1)} %bitcast.15), channel_id=1, source_target_pairs={{0,2},{2,0},{1,3},{3,1},{4,6},{6,4},{5,7},{7,5},{8,10},{10,8},{9,1... | collective-permute-start | bytes 6291464 | tf_op jit(solution)/shard_map/ppermute | solution.py:718
  3.7 0.1 collective-permute-start.1
  3.7 1.3 convert_element_type.12.lnmid
  5.0 1.3 convert_element_type.13.b_proj
  6.3 1.3 convert_element_type.14.ln_in
  7.5 1.2 convert_element_type.15.b_out
  8.7 0.6 pad_add_fusion.ids
  9.3 2.0 shard_map.152
  11.3 7.3 %shard_map.154 = (bf16[64,64,256]{2,1,0:T(8,128)(2,1)}, bf16[64,64,256]{2,1,0:T(8,128)(2,1)}) custom-call(bf16[64,64,256]{2,1,0:T(8,128)(2,1)} %bitcast.16, s32[64,256]{1,0:T(8,128)} %bitcast.24, bf16[2,320,80]{2,1,0:T(8,128)(2,1)} %get-tuple-element.60.wt.wt0.wt1, f32[2,64,256]{2,1,0:T(8,128)} %get-tuple-element.61.gain.gain0.gain1, ...), custom_call_target="tpu_custom_call" | custom-call | flops 1000000000 | bytes 8388608 | tf_op jit(solution)/shard_map/pallas_call | solution.py:167
  18.6 0.0 collective-permute-start.3
  18.6 31.7 %collective-permute-done.z.zp = bf16[64,64,256]{2,1,0:T(8,128)(2,1)} collective-permute-done((bf16[64,64,256]{2,1,0:T(8,128)(2,1)}, bf16[64,64,256]{2,1,0:T(8,128)(2,1)}, u32[]{:S(2)}, u32[]{:S(2)}) %collective-permute-start) | collective-permute-done | bytes 2097184 | tf_op jit(solution)/shard_map/ppermute | solution.py:718
  50.3 0.7 collective-permute-done.1.mask.mp
  51.0 7.3 %shard_map.153 = (bf16[64,64,256]{2,1,0:T(8,128)(2,1)}, bf16[64,64,256]{2,1,0:T(8,128)(2,1)}) custom-call(bf16[64,64,256]{2,1,0:T(8,128)(2,1)} %collective-permute-done.z.zp, s32[64,256]{1,0:T(8,128)} %collective-permute-done.1.mask.mp, bf16[2,320,80]{2,1,0:T(8,128)(2,1)} %get-tuple-element.60.wt.wt0.wt1, f32[2,64,256]{2,1,0:T(8,128)} %get-tuple-element.61.gain.gain0.gain1, ...), custom_call_target="tpu_custom_call" | custom-call | flops 1000000000 | bytes 8388608 | tf_op jit(solution)/shard_map/pallas_call | solution.py:167
  58.3 0.0 collective-permute-start.2
  58.3 0.0 collective-permute-done.3.qo
  58.3 4.5 %collective-permute-done.2.qp = bf16[64,64,256]{2,1,0:T(8,128)(2,1)} collective-permute-done((bf16[64,64,256]{2,1,0:T(8,128)(2,1)}, bf16[64,64,256]{2,1,0:T(8,128)(2,1)}, u32[]{:S(2)}, u32[]{:S(2)}) %collective-permute-start.2) | collective-permute-done | bytes 2097184 | tf_op jit(solution)/shard_map/ppermute | solution.py:721
  62.8 29.8 %shard_map.155 = (bf16[128,64,256]{2,1,0:T(8,128)(2,1)}, f32[64,128,256]{2,1,0:T(8,128)}, f32[128,256]{1,0:T(8,128)}, bf16[64,128,256]{2,1,0:T(8,128)(2,1)}, bf1...) custom-call(s32[2]{0:T(128)} %pad_add_fusion.ids, ...), custom_call_target="tpu_custom_call" | custom-call | flops 1000000000 | bytes 41943040 | tf_op jit(solution)/shard_map/pallas_call | solution.py:322
  92.7 0.2 collective-permute-start.5
  92.9 1.7 collective-permute-start.6
  94.6 0.1 collective-permute-start.4
  94.7 46.4 %collective-permute-done.6.dzp = bf16[64,64,256]{2,1,0:T(8,128)(2,1)} collective-permute-done((bf16[64,64,256]{2,1,0:T(8,128)(2,1)}, bf16[64,64,256]{2,1,0:T(8,128)(2,1)}, u32[]{:S(2)}, u32[]{:S(2)}) %collective-permute-start.6) | collective-permute-done | bytes 2097184 | tf_op jit(solution)/shard_map/ppermute | solution.py:718
  141.1 0.0 collective-permute-done.4.ar
  141.1 0.0 collective-permute-done.5.bq
  141.1 27.2 %shard_map.156 = (bf16[64,64,256]{2,1,0:T(8,128)(2,1)}, bf16[64,128,256]{2,1,0:T(8,128)(2,1)}, bf16[128,64,256]{2,1,0:T(8,128)(2,1)}, f32[64,128]{1,0:T(8,128)},...) custom-call(s32[2]{0:T(128)} %pad_add_fusion.ids, ...), custom_call_target="tpu_custom_call" | custom-call | flops 1000000000 | bytes 41943040 | tf_op jit(solution)/shard_map/pallas_call | solution.py:418
  168.3 0.1 collective-permute-start.7
  168.4 0.5 collective-permute-start.10
  168.9 0.1 collective-permute-start.9
  169.0 6.9 %collective-permute-done.7.dxq = bf16[64,128,256]{2,1,0:T(8,128)(2,1)} collective-permute-done((bf16[64,128,256]{2,1,0:T(8,128)(2,1)}, bf16[64,128,256]{2,1,0:T(8,128)(2,1)}, u32[]{:S(2)}, u32[]{:S(2)}) %collective-permute-start.7) | collective-permute-done | bytes 4194336 | tf_op jit(solution)/shard_map/ppermute | solution.py:721
  175.9 45.3 %shard_map.157 = (bf16[64,64,256]{2,1,0:T(8,128)(2,1)}, bf16[64,128,256]{2,1,0:T(8,128)(2,1)}, bf16[64,128,128]{2,1,0:T(8,128)(2,1)}, bf16[64,128,128]{2,1,0:T(8...) custom-call(s32[2]{0:T(128)} %pad_add_fusion.ids, ...), custom_call_target="tpu_custom_call" | custom-call | flops 1000000000 | bytes 62914560 | tf_op jit(solution)/shard_map/pallas_call | solution.py:536
  221.2 0.2 collective-permute-start.8
  221.4 0.0 collective-permute-done.10.ro
  221.4 0.0 collective-permute-done.9.rp
  221.4 4.4 %collective-permute-done.8.dxr = bf16[64,128,128]{2,1,0:T(8,128)(2,1)} collective-permute-done((bf16[64,128,128]{2,1,0:T(8,128)(2,1)}, bf16[64,128,128]{2,1,0:T(8,128)(2,1)}, u32[]{:S(2)}, u32[]{:S(2)}) %collective-permute-start.8) | collective-permute-done | bytes 2097184 | tf_op jit(solution)/shard_map/ppermute | solution.py:721
  225.8 20.9 %shard_map.158 = (bf16[64,64,256]{2,1,0:T(8,128)(2,1)}, f32[320,64]{1,0:T(8,128)}, f32[256,128]{1,0:T(8,128)}, f32[64,128]{1,0:T(8,128)}, f32[64,128]{1,0:T(8,128)}) custom-call(s32[2]{0:T(128)} %pad_add_fusion.ids, bf16[64,128,256]{2,1,0:T(8,128)(2,1)} %get-tuple-element.80.dx, bf16[64,64,256]{2,1,0:T(8,128)(2,1)} %get-tuple-element.66.bp, ...), custom_call_target="tpu_custom_call" | custom-call | flops 1000000000 | bytes 41943040 | tf_op jit(solution)/shard_map/pallas_call | solution.py:577
  246.7 23.3 %grad_sum.1.src = f32[512,128]{1,0:T(8,128)} custom-call(f32[320,64]{1,0:T(8,128)} %get-tuple-element.86.w0, f32[256,128]{1,0:T(8,128)} %get-tuple-element.87.b0, f32[64,128]{1,0:T(8,128)} %get-tuple-element.88.q0, f32[64,128]{1,0:T(8,128)} %get-tuple-element.89.g0, f32[64,128]{1,0:T(8,128)} %get-tuple-element.90.l0, f32[64,64]{1,0:T(8,128)} %get-tuple-element.91.wo0, ...), custom_call_target="tpu_custom_call" | custom-call | flops 1000000 | bytes 1048576 | tf_op jit(solution)/shard_map/grad_sum/pallas_call | solution.py:673
  270.1 1.8 shard_map.159
Async XLA Ops:
  0.6 49.7 %collective-permute-start = (bf16[64,64,256]{2,1,0:T(8,128)(2,1)}, bf16[64,64,256]{2,1,0:T(8,128)(2,1)}, u32[]{:S(2)}, u32[]{:S(2)}) collective-permute-start(bf16[64,64,256]{2,1,0:T(8,128)(2,1)} %bitcast.15), channel_id=1, source_target_pairs={{0,2},{2,0},{1,3},{3,1},{4,6},{6,4},{5,7},{7,5},{8,10},{10,8},{9,1... | collective-permute-start | bytes 6291464 | tf_op jit(solution)/shard_map/ppermute | solution.py:718
  3.7 47.4 %collective-permute-start.1 = (s32[64,256]{1,0:T(8,128)}, s32[64,256]{1,0:T(8,128)}, u32[]{:S(2)}, u32[]{:S(2)}) collective-permute-start(s32[64,256]{1,0:T(8,128)} %bitcast.23), channel_id=1, source_target_pairs={{0,2},{2,0},{1,3},{3,1},{4,6},{6,4},{5,7},{7,5},{8,10},{10,8},{9,1... | collective-permute-start | bytes 196616 | tf_op jit(solution)/shard_map/ppermute | solution.py:718
  18.6 39.7 %collective-permute-start.3 = (bf16[64,64,256]{2,1,0:T(8,128)(2,1)}, bf16[64,64,256]{2,1,0:T(8,128)(2,1)}, u32[]{:S(2)}, u32[]{:S(2)}) collective-permute-start(bf16[64,64,256]{2,1,0:T(8,128)(2,1)} %get-tuple-element.67.bo), channel_id=1, source_target_pairs={{0,1},{1,0},{2,3},{3,2},{4,5},{5,4},{6,7},{7,6},{8,9},{9,8},{10,11... | collective-permute-start | bytes 6291464 | tf_op jit(solution)/shard_map/ppermute | solution.py:721
  58.3 4.5 %collective-permute-start.2 = (bf16[64,64,256]{2,1,0:T(8,128)(2,1)}, bf16[64,64,256]{2,1,0:T(8,128)(2,1)}, u32[]{:S(2)}, u32[]{:S(2)}) collective-permute-start(bf16[64,64,256]{2,1,0:T(8,128)(2,1)} %get-tuple-element.66.bp), channel_id=1, source_target_pairs={{0,1},{1,0},{2,3},{3,2},{4,5},{5,4},{6,7},{7,6},{8,9},{9,8},{10,11... | collective-permute-start | bytes 6291464 | tf_op jit(solution)/shard_map/ppermute | solution.py:721
  92.7 48.4 %collective-permute-start.5 = (bf16[64,128,256]{2,1,0:T(8,128)(2,1)}, bf16[64,128,256]{2,1,0:T(8,128)(2,1)}, u32[]{:S(2)}, u32[]{:S(2)}) collective-permute-start(bf16[64,128,256]{2,1,0:T(8,128)(2,1)} %get-tuple-element.71.b), channel_id=1, source_target_pairs={{0,1},{1,0},{2,3},{3,2},{4,5},{5,4},{6,7},{7,6},{8,9},{9,8},{10,11... | collective-permute-start | bytes 12582920 | tf_op jit(solution)/shard_map/ppermute | solution.py:721
  92.9 48.2 %collective-permute-start.6 = (bf16[64,64,256]{2,1,0:T(8,128)(2,1)}, bf16[64,64,256]{2,1,0:T(8,128)(2,1)}, u32[]{:S(2)}, u32[]{:S(2)}) collective-permute-start(bf16[64,64,256]{2,1,0:T(8,128)(2,1)} %bitcast.20), channel_id=1, source_target_pairs={{0,2},{2,0},{1,3},{3,1},{4,6},{6,4},{5,7},{7,5},{8,10},{10,8},{9,1... | collective-permute-start | bytes 6291464 | tf_op jit(solution)/shard_map/ppermute | solution.py:718
  94.6 46.5 %collective-permute-start.4 = (bf16[64,128,128]{2,1,0:T(8,128)(2,1)}, bf16[64,128,128]{2,1,0:T(8,128)(2,1)}, u32[]{:S(2)}, u32[]{:S(2)}) collective-permute-start(bf16[64,128,128]{2,1,0:T(8,128)(2,1)} %get-tuple-element.70), channel_id=1, source_target_pairs={{0,1},{1,0},{2,3},{3,2},{4,5},{5,4},{6,7},{7,6},{8,9},{9,8},{10,11... | collective-permute-start | bytes 6291464 | tf_op jit(solution)/shard_map/ppermute | solution.py:721
  168.3 7.6 %collective-permute-start.7 = (bf16[64,128,256]{2,1,0:T(8,128)(2,1)}, bf16[64,128,256]{2,1,0:T(8,128)(2,1)}, u32[]{:S(2)}, u32[]{:S(2)}) collective-permute-start(bf16[64,128,256]{2,1,0:T(8,128)(2,1)} %get-tuple-element.76.dx), channel_id=1, source_target_pairs={{0,1},{1,0},{2,3},{3,2},{4,5},{5,4},{6,7},{7,6},{8,9},{9,8},{10,11... | collective-permute-start | bytes 12582920 | tf_op jit(solution)/shard_map/ppermute | solution.py:721
  168.4 53.0 %collective-permute-start.10 = (bf16[64,64,256]{2,1,0:T(8,128)(2,1)}, bf16[64,64,256]{2,1,0:T(8,128)(2,1)}, u32[]{:S(2)}, u32[]{:S(2)}) collective-permute-start(bf16[64,64,256]{2,1,0:T(8,128)(2,1)} %get-tuple-element.65.ao), channel_id=1, source_target_pairs={{0,1},{1,0},{2,3},{3,2},{4,5},{5,4},{6,7},{7,6},{8,9},{9,8},{10,11... | collective-permute-start | bytes 6291464 | tf_op jit(solution)/shard_map/ppermute | solution.py:721
  168.9 52.5 %collective-permute-start.9 = (bf16[64,64,256]{2,1,0:T(8,128)(2,1)}, bf16[64,64,256]{2,1,0:T(8,128)(2,1)}, u32[]{:S(2)}, u32[]{:S(2)}) collective-permute-start(bf16[64,64,256]{2,1,0:T(8,128)(2,1)} %get-tuple-element.64.ap), channel_id=1, source_target_pairs={{0,1},{1,0},{2,3},{3,2},{4,5},{5,4},{6,7},{7,6},{8,9},{9,8},{10,11... | collective-permute-start | bytes 6291464 | tf_op jit(solution)/shard_map/ppermute | solution.py:721
  221.2 4.6 %collective-permute-start.8 = (bf16[64,128,128]{2,1,0:T(8,128)(2,1)}, bf16[64,128,128]{2,1,0:T(8,128)(2,1)}, u32[]{:S(2)}, u32[]{:S(2)}) collective-permute-start(bf16[64,128,128]{2,1,0:T(8,128)(2,1)} %get-tuple-element.82), channel_id=1, source_target_pairs={{0,1},{1,0},{2,3},{3,2},{4,5},{5,4},{6,7},{7,6},{8,9},{9,8},{10,11... | collective-permute-start | bytes 6291464 | tf_op jit(solution)/shard_map/ppermute | solution.py:721

commit v4 on v3

--- a/solution.py
+++ b/solution.py
@@ -142,7 +142,7 @@
 SMEM_SPEC = pl.BlockSpec(memory_space=pltpu.SMEM)
 
 
-def call(kernel, grid, in_specs, out_specs, out_shape, scratch, flops, bytes_accessed, trans=0):
+def call(kernel, grid, in_specs, out_specs, out_shape, scratch, flops, bytes_accessed, remote=None):
     return pl.pallas_call(
         kernel,
         grid=grid,
@@ -151,8 +151,8 @@
         out_shape=out_shape,
         scratch_shapes=scratch,
         interpret=INTERPRET,
-        cost_estimate=pl.CostEstimate(flops=flops, bytes_accessed=bytes_accessed, transcendentals=trans),
-        compiler_params=pltpu.CompilerParams(dimension_semantics=("arbitrary",) * len(grid), vmem_limit_bytes=VMEM_LIMIT),
+        cost_estimate=pl.CostEstimate(flops=flops, bytes_accessed=bytes_accessed, transcendentals=0),
+        compiler_params=pltpu.CompilerParams(dimension_semantics=("arbitrary",) * len(grid), vmem_limit_bytes=VMEM_LIMIT, collective_id=remote, has_side_effects=remote is not None),
     )
 
 
@@ -224,6 +224,41 @@
     r = step - T_STEPS
     pl.when((r >= 0) & (r < 4))(lambda: body(r, False))
     pl.when(r >= 4)(lambda: body(r, True))
+
+
+def here():
+    dap = lax.axis_index("dap")
+    return dap // 2, dap % 2
+
+
+def from_partner(step, pairs, send, recv):
+    dp, dap = lax.axis_index("dp"), lax.axis_index("dap")
+    other = (dp, dap + 1 - 2 * (dap % 2))
+
+    def copy(k, t):
+        src, dst = pairs[k]
+        blk = pl.ds(pl.multiple_of(t * CB, CB), CB)
+        return pltpu.make_async_remote_copy(src.at[blk], dst.at[blk], send.at[k, t], recv.at[k, t], device_id=other, device_id_type=MESH_ID)
+
+    @pl.when(step == 0)
+    def _():
+        bar = pltpu.get_barrier_semaphore()
+        pl.semaphore_signal(bar, inc=1, device_id=other, device_id_type=MESH_ID)
+        pl.semaphore_wait(bar, 1)
+        for t in range(T_STEPS):
+            for k in range(len(pairs)):
+                copy(k, t).start()
+
+    @pl.when(step < T_STEPS)
+    def _():
+        for k in range(len(pairs)):
+            copy(k, step).wait_recv()
+
+    @pl.when(step == T_STEPS)
+    def _():
+        for t in range(T_STEPS):
+            for k in range(len(pairs)):
+                copy(k, t).wait_send()
 
 
 def channels(step):
@@ -352,15 +387,16 @@
             acc[:] = jnp.zeros_like(acc)
 
 
-def turn_kernel(ids, ak, ar, b, bq, z, dzp, dzo, wt, gain, lbias, wot, wo, lnmid, perm, znew, dx, dpg, acc_bg, acc_bo, acc_wo, acc_mg, acc_mb, x_s, xh_s, xi_s, dxi_s, dub_s, dxc_s, xn_s, r_s):
+def turn_kernel(ak, b, a_send, b_send, z, dzp, dzo, wt, gain, lbias, wot, wo, lnmid, perm, znew, dx, dpg, acc_bg, acc_bo, acc_wo, acc_mg, acc_mb, x_s, xh_s, xi_s, dxi_s, dub_s, dxc_s, xn_s, r_s, ar_s, bq_s, send, recv):
     step = pl.program_id(0)
-    xx = ids[0]
+    xx, _ = here()
+    from_partner(step, ((a_send, ar_s), (b_send, bq_s)), send, recv)
     clear(step, (acc_bg, acc_bo, acc_wo, acc_mg, acc_mb))
 
     @pl.when(step < T_STEPS)
     def _():
         for ch, dst in channels(step):
-            out = dot_tn(ak[ch], b[ch]) + dot_tn(ar[ch], bq[ch])
+            out = dot_tn(ak[ch], b[ch]) + dot_tn(ar_s[dst], bq_s[dst])
             x_s[dst, pl.ds(pl.multiple_of(C * (1 - xx), C), C), :] = out[0:C]
             x_s[dst, pl.ds(pl.multiple_of(C * xx, C), C), :] = out[C:LANES]
 
@@ -411,17 +447,17 @@
 ACC_PRE = ((5 * C, C), (4 * C, LANES), (C, LANES), (C, LANES))
 
 
-def turn_fused(ids, sides, z_mid, dz_parts, par, w_out, lnmid):
+def turn_fused(sides, z_mid, dz_parts, par, w_out, lnmid):
     n = z_mid.shape[-1]
     s1, w1 = weights_specs(par, 1, True)
     sds, vm = jax.ShapeDtypeStruct, pltpu.VMEM
     return call(
         turn_kernel, (T_STEPS + 8,),
-        [SMEM_SPEC] + [tri_spec(v.shape) for v in sides] + [r_spec(n)] + two_specs((RB, C, n)) + s1 + [blk_spec(w_out.shape, 1), SMEM_SPEC, full_spec((W2, W2))],
+        [tri_spec(v.shape) for v in sides[:2]] + [pl.BlockSpec(memory_space=pl.ANY)] * 2 + [r_spec(n)] + two_specs((RB, C, n)) + s1 + [blk_spec(w_out.shape, 1), SMEM_SPEC, full_spec((W2, W2))],
         [two_specs((RB, C, n))[1], c_spec(n), r_spec(n)] + [full_spec(s) for s in ACC_POST],
         [sds((C, C, n), BF16), sds((C, LANES, n), BF16), sds((LANES, C, n), BF16)] + [sds(s, F32) for s in ACC_POST],
-        [vm((C, LANES, n), F32), vm((C, RB, n), BF16)] + [vm((RB, C, n), BF16)] * 3 + [vm((C, RB, n), F32)] * 2 + [vm((RB, n), F32)],
-        GIGA, 40 * MIB)(ids, *sides, z_mid, *dz_parts, *w1, w_out, lnmid, par[-1])
+        [vm((C, LANES, n), F32), vm((C, RB, n), BF16)] + [vm((RB, C, n), BF16)] * 3 + [vm((C, RB, n), F32)] * 2 + [vm((RB, n), F32), vm((C, LANES, LANES), BF16), vm((C, LANES, n), BF16)] + [pltpu.SemaphoreType.DMA((2, T_STEPS))] * 2,
+        GIGA, 40 * MIB, 1)(*sides, z_mid, *dz_parts, *w1, w_out, lnmid, par[-1])
 
 
 def pre_back_stages(own, z, dpg, mask_of, res_of, dst, wt, w, gain, lbias, dai_s, dbi_s, dp_s, zh_s, zn_s, rs_s, acc_b, sums):
@@ -461,15 +497,17 @@
     return gates, products
 
 
-def back_kernel(ids, a, b, dx, dxq, z, dpg1, dzp, dzo, mp, mo, xn, rstd, zp, zo, wt1, gain1, lbias1, w1, wt0, gain0, lbias0, wot0, wo0, lnmid, perm, dzm, dx0, dxk, dxs, dpg0, acc_w, acc_b, acc_g, acc_lb, acc_bg, acc_bo, acc_wo, acc_mg, acc_mb, da_s, db_s, full, dai_s, dbi_s, dp_s, zh_s, zn_s, rs_s, xh_s, xi_s, dxi_s, dub_s, dxc_s):
+def back_kernel(a, b, dx, dx_send, z, dpg1, dzp, dzo, mp, mo, xn, rstd, zp, zo, wt1, gain1, lbias1, w1, wt0, gain0, lbias0, wot0, wo0, lnmid, perm, dzm, dx0, dxk, dxs, dpg0, acc_w, acc_b, acc_g, acc_lb, acc_bg, acc_bo, acc_wo, acc_mg, acc_mb, da_s, db_s, full, dai_s, dbi_s, dp_s, zh_s, zn_s, rs_s, xh_s, xi_s, dxi_s, dub_s, dxc_s, dxq_s, send, recv):
     step = pl.program_id(0)
+    ids = here()
+    from_partner(step, ((dx_send, dxq_s),), send, recv)
     clear(step, (acc_w, acc_b, acc_g, acc_lb, acc_bg, acc_bo, acc_wo, acc_mg, acc_mb))
 
     @pl.when(step < T_STEPS)
     def _():
         for ch, dst in channels(step):
             buf = full.at[ch % 2]
-            place(buf, halves(dx.at[ch]), halves(dxq.at[ch]), ids)
+            place(buf, halves(dx.at[ch]), halves(dxq_s.at[dst]), ids)
             da_s[dst] = dot_nt(b[ch], buf[:]).astype(BF16)
             db_s[dst] = dot_nn(a[ch], buf[:]).astype(BF16)
 
@@ -525,7 +563,7 @@
     each_half(step, body)
 
 
-def back_fused(ids, sides, z_mid, dpg1, dz_parts, masks, xn, rstd, z_parts, par, w_proj, w_out, lnmid):
+def back_fused(sides, z_mid, dpg1, dz_parts, masks, xn, rstd, z_parts, par, w_proj, w_out, lnmid):
     n = z_mid.shape[-1]
     s1, w1 = weights_specs(par, 1, False)
     s0, w0 = weights_specs(par, 0, True)
@@ -535,12 +573,12 @@
     accs = ACC_PRE + ACC_POST
     return call(
         back_kernel, (T_STEPS + 8,),
-        [SMEM_SPEC] + [tri_spec(v.shape) for v in sides] + [r_spec(n), r_spec(n)] + two + two_specs((RB, n)) + [c_spec(n), m_spec(n)] + two
+        [tri_spec(v.shape) for v in sides[:3]] + [pl.BlockSpec(memory_space=pl.ANY)] + [r_spec(n), r_spec(n)] + two + two_specs((RB, n)) + [c_spec(n), m_spec(n)] + two
         + s1 + [blk_spec(w_proj.shape, 1)] + s0 + [blk_spec(w_out.shape, 0), SMEM_SPEC, full_spec((W2, W2))],
         [two[1], c_spec(n), c_spec(LANES), c_spec(LANES), r_spec(n)] + [full_spec(s) for s in accs],
         [sds((C, C, n), BF16), sds((C, LANES, n), BF16), sds((C, LANES, LANES), BF16), sds((C, LANES, LANES), BF16), sds((LANES, C, n), BF16)] + [sds(s, F32) for s in accs],
-        [vm((C, LANES, n), BF16)] * 2 + [vm((2, n, n), BF16), rows, rows, vm((RB, 5 * C, n), BF16), rows, vm((RB, C, n), F32), vm((RB, 8, n), F32), vm((C, RB, n), BF16), rows, rows, rows, vm((C, RB, n), F32)],
-        GIGA, 60 * MIB)(ids, *sides, z_mid, dpg1, *dz_parts, *masks, xn, rstd, *z_parts, *w1, w_proj, *w0, w_out, lnmid, par[-1])
+        [vm((C, LANES, n), BF16)] * 2 + [vm((2, n, n), BF16), rows, rows, vm((RB, 5 * C, n), BF16), rows, vm((RB, C, n), F32), vm((RB, 8, n), F32), vm((C, RB, n), BF16), rows, rows, rows, vm((C, RB, n), F32), vm((C, LANES, n), BF16)] + [pltpu.SemaphoreType.DMA((1, T_STEPS))] * 2,
+        GIGA, 60 * MIB, 2)(*sides, z_mid, dpg1, *dz_parts, *masks, xn, rstd, *z_parts, *w1, w_proj, *w0, w_out, lnmid, par[-1])
 
 
 def last_kernel(ids, dx, bp, bo, qp, qo, dxk, dxr, ap, ao, rp, ro, z, dpg, dres, mask, wt, gain, lbias, w, perm, dz, acc_w, acc_b, acc_g, acc_lb, da_s, db_s, full, tmp, dai_s, dbi_s, dp_s, zh_s, zn_s, rs_s):
@@ -736,10 +774,8 @@
         ap, bp = pre_forward(z_peer, m_peer, par)
         qp, rp = over_c(bp), over_c(ap)
         z_mid, xn, rstd, a1, b1, a1k, a1s = fwd_fused(ids, (ap, ao, bp, bo, qp, qo), z_peer, z_own, masks, par, lnmid)
-        a1r, b1p = over_c(a1s), over_c(b1)
-        z_new, dx1, dpg1, bg1, bo1, wo1, mg1, mb1 = turn_fused(ids, (a1k, a1r, b1, b1p), z_mid, (dz_peer, dz_own), par, w_out, lnmid)
-        dx1p = over_c(dx1)
-        dz_mid, dx0, dx0k, dx0s, dpg0, w1, b1s, g1, lb1, bg0, bo0, wo0, mg0, mb0 = back_fused(ids, (a1, b1, dx1, dx1p), z_mid, dpg1, (dz_peer, dz_own), masks, xn, rstd, (z_peer, z_own), par, w_proj, w_out, lnmid)
+        z_new, dx1, dpg1, bg1, bo1, wo1, mg1, mb1 = turn_fused((a1k, b1, a1s, b1), z_mid, (dz_peer, dz_own), par, w_out, lnmid)
+        dz_mid, dx0, dx0k, dx0s, dpg0, w1, b1s, g1, lb1, bg0, bo0, wo0, mg0, mb0 = back_fused((a1, b1, dx1, dx1), z_mid, dpg1, (dz_peer, dz_own), masks, xn, rstd, (z_peer, z_own), par, w_proj, w_out, lnmid)
         dx0r = over_c(dx0s)
         dz, w0, b0s, g0, lb0 = last_fused(ids, (dx0, bp, bo, qp, qo, dx0k, dx0r, ap, ao, rp, ro), z_own, dpg0, dz_mid, m_own, par, w_proj)
 

time: 272 us -> 242 us (0.89)
  waiting for transfers between devices: 94.6 us -> 53 us
  Pallas kernels: 165 us -> 174 us
  local copies, waits for them, and re-layouts: 0 us -> 3.16 us
    ppermute x3, waiting for transfers between devices: 78.8 us -> 46.3 us  [over_x(): return lax.ppermute(v, 'dap', x_pairs)]
    ppermute x8 -> x5, waiting for transfers between devices: 15.8 us -> 6.64 us  [over_c(): return lax.ppermute(v, 'dap', c_pairs)]
    pallas_call x2, Pallas kernels: 72.5 us -> 81.1 us  [the longest x1 48 us: back_fused(): call(back_kernel, (T_STEPS + 8,), [tri_spec(v.shape) for v in sides[:3]]...]
    unnamed x0 -> x1, local copies, waits for them, and re-layouts: none -> 3.16 us
  transfers between devices with their start and end apart: 11 -> 8, of which waited for: 6 -> 5; matrix products, arithmetic and copies ran while one was open for 2% -> 2% of each run, Pallas kernels for 23% -> 53%
where the time goes in v4:
time: 242 us
  Pallas kernels  174 us (72%)
  waiting for transfers between devices  53 us (22%)
  other arithmetic  5.64 us (2%)
  starting transfers between devices  5.53 us (2%)
  local copies, waits for them, and re-layouts  3.16 us (1%)
    pallas_call x1, Pallas kernels, back_fused(): call(back_kernel, (T_STEPS + 8,), [tri_spec(v.shape) for v in sides[:3]]...  48 us
    ppermute x3, waiting for transfers between devices, over_x(): return lax.ppermute(v, 'dap', x_pairs)  46.3 us
    pallas_call x1, Pallas kernels, turn_fused(): call(turn_kernel, (T_STEPS + 8,), [tri_spec(v.shape) for v in sides[:2]]...  33.1 us
    pallas_call x1, Pallas kernels, fwd_fused(): call(fwd_kernel, (T_STEPS + 8,), [SMEM_SPEC] + [tri_spec(v.shape) for v i...  29.9 us
    pallas_call x1, Pallas kernels, sum_grads(): pl.pallas_call(functools.partial(grads_kernel, n_dp, n_dap), out_shape=ja...  23.3 us
    pallas_call x1, Pallas kernels, last_fused(): call(last_kernel, (T_STEPS + 4,), [SMEM_SPEC, tri_spec((C, C, n), 1)] + [...  20.9 us
    pallas_call x2, Pallas kernels, pre_forward(): call(pre_fwd_kernel, (rows // RB,), [pl.BlockSpec((RB, C, n), lambda s: (...  14.6 us
    ppermute x5, waiting for transfers between devices, over_c(): return lax.ppermute(v, 'dap', c_pairs)  6.64 us
  transfers between devices with their start and end apart: 8, of which 5 were waited for; matrix products, arithmetic and copies ran while one was open for 2% of the time, Pallas kernels for 53%

profile of v4, /device:TPU:0, one launch (start us, length us, event | category | flops | bytes accessed | tf_op | source)
XLA Modules:
  0.0 241.6 jit_solution(15944531831730325079)
XLA Ops:
  0.6 3.0 %collective-permute-start = (bf16[64,64,256]{2,1,0:T(8,128)(2,1)}, bf16[64,64,256]{2,1,0:T(8,128)(2,1)}, u32[]{:S(2)}, u32[]{:S(2)}) collective-permute-start(bf16[64,64,256]{2,1,0:T(8,128)(2,1)} %bitcast.15), channel_id=1, source_target_pairs={{0,2},{2,0},{1,3},{3,1},{4,6},{6,4},{5,7},{7,5},{8,10},{10,8},{9,1... | collective-permute-start | bytes 6291464 | tf_op jit(solution)/shard_map/ppermute | solution.py:756
  3.7 0.1 collective-permute-start.1
  3.7 1.3 convert_element_type.12.lnmid
  5.0 1.3 convert_element_type.13.b_proj
  6.3 1.3 convert_element_type.14.ln_in
  7.5 1.2 convert_element_type.15.b_out
  8.7 0.6 pad_add_fusion.ids
  9.4 1.9 shard_map.152
  11.3 7.3 %shard_map.154 = (bf16[64,64,256]{2,1,0:T(8,128)(2,1)}, bf16[64,64,256]{2,1,0:T(8,128)(2,1)}) custom-call(bf16[64,64,256]{2,1,0:T(8,128)(2,1)} %bitcast.16, s32[64,256]{1,0:T(8,128)} %bitcast.25, bf16[2,320,80]{2,1,0:T(8,128)(2,1)} %get-tuple-element.60.wt.wt0.wt1, f32[2,64,256]{2,1,0:T(8,128)} %get-tuple-element.61.gain.gain0.gain1, ...), custom_call_target="tpu_custom_call" | custom-call | flops 1000000000 | bytes 8388608 | tf_op jit(solution)/shard_map/pallas_call | solution.py:167
  18.7 0.0 collective-permute-start.3
  18.7 31.6 %collective-permute-done.z.zp = bf16[64,64,256]{2,1,0:T(8,128)(2,1)} collective-permute-done((bf16[64,64,256]{2,1,0:T(8,128)(2,1)}, bf16[64,64,256]{2,1,0:T(8,128)(2,1)}, u32[]{:S(2)}, u32[]{:S(2)}) %collective-permute-start) | collective-permute-done | bytes 2097184 | tf_op jit(solution)/shard_map/ppermute | solution.py:756
  50.3 0.7 collective-permute-done.1.mask.mp
  51.0 7.3 %shard_map.153 = (bf16[64,64,256]{2,1,0:T(8,128)(2,1)}, bf16[64,64,256]{2,1,0:T(8,128)(2,1)}) custom-call(bf16[64,64,256]{2,1,0:T(8,128)(2,1)} %collective-permute-done.z.zp, s32[64,256]{1,0:T(8,128)} %collective-permute-done.1.mask.mp, bf16[2,320,80]{2,1,0:T(8,128)(2,1)} %get-tuple-element.60.wt.wt0.wt1, f32[2,64,256]{2,1,0:T(8,128)} %get-tuple-element.61.gain.gain0.gain1, ...), custom_call_target="tpu_custom_call" | custom-call | flops 1000000000 | bytes 8388608 | tf_op jit(solution)/shard_map/pallas_call | solution.py:167
  58.3 0.0 collective-permute-start.2
  58.3 1.8 collective-permute-start.4
  60.1 0.2 collective-permute-start.7
  60.3 0.4 collective-permute-start.6
  60.7 0.0 collective-permute-done.3.qo
  60.7 2.2 collective-permute-done.2.qp
  62.8 29.9 %shard_map.155 = (bf16[128,64,256]{2,1,0:T(8,128)(2,1)}, f32[64,128,256]{2,1,0:T(8,128)}, f32[128,256]{1,0:T(8,128)}, bf16[64,128,256]{2,1,0:T(8,128)(2,1)}, bf1...) custom-call(s32[2]{0:T(128)} %pad_add_fusion.ids, ...), custom_call_target="tpu_custom_call" | custom-call | flops 1000000000 | bytes 41943040 | tf_op jit(solution)/shard_map/pallas_call | solution.py:357
  92.7 14.0 %collective-permute-done.4.dzp = bf16[64,64,256]{2,1,0:T(8,128)(2,1)} collective-permute-done((bf16[64,64,256]{2,1,0:T(8,128)(2,1)}, bf16[64,64,256]{2,1,0:T(8,128)(2,1)}, u32[]{:S(2)}, u32[]{:S(2)}) %collective-permute-start.4) | collective-permute-done | bytes 2097184 | tf_op jit(solution)/shard_map/ppermute | solution.py:756
  106.7 33.1 %shard_map.156 = (bf16[64,64,256]{2,1,0:T(8,128)(2,1)}, bf16[64,128,256]{2,1,0:T(8,128)(2,1)}, bf16[128,64,256]{2,1,0:T(8,128)(2,1)}, f32[64,128]{1,0:T(8,128)},...) custom-call(bf16[64,128,128]{2,1,0:T(8,128)(2,1)} %get-tuple-element.69.ak, ...), custom_call_target="tpu_custom_call" | custom-call | flops 1000000000 | bytes 41943040 | tf_op jit(solution)/shard_map/pallas_call | solution.py:454
  139.8 48.0 %shard_map.157 = (bf16[64,64,256]{2,1,0:T(8,128)(2,1)}, bf16[64,128,256]{2,1,0:T(8,128)(2,1)}, bf16[64,128,128]{2,1,0:T(8,128)(2,1)}, bf16[64,128,128]{2,1,0:T(8...) custom-call(bf16[64,128,256]{2,1,0:T(8,128)(2,1)} %get-tuple-element, ...), custom_call_target="tpu_custom_call" | custom-call | flops 1000000000 | bytes 62914560 | tf_op jit(solution)/shard_map/pallas_call | solution.py:574
  187.8 0.1 collective-permute-start.5
  187.9 0.0 collective-permute-done.7.ro
  187.9 0.0 collective-permute-done.6.rp
  187.9 4.5 %collective-permute-done.5.dxr = bf16[64,128,128]{2,1,0:T(8,128)(2,1)} collective-permute-done((bf16[64,128,128]{2,1,0:T(8,128)(2,1)}, bf16[64,128,128]{2,1,0:T(8,128)(2,1)}, u32[]{:S(2)}, u32[]{:S(2)}) %collective-permute-start.5) | collective-permute-done | bytes 2097184 | tf_op jit(solution)/shard_map/ppermute | solution.py:759
  192.4 20.9 %shard_map.158 = (bf16[64,64,256]{2,1,0:T(8,128)(2,1)}, f32[320,64]{1,0:T(8,128)}, f32[256,128]{1,0:T(8,128)}, f32[64,128]{1,0:T(8,128)}, f32[64,128]{1,0:T(8,128)}) custom-call(s32[2]{0:T(128)} %pad_add_fusion.ids, bf16[64,128,256]{2,1,0:T(8,128)(2,1)} %get-tuple-element.80.dx, bf16[64,64,256]{2,1,0:T(8,128)(2,1)} %get-tuple-element.66.bp, ...), custom_call_target="tpu_custom_call" | custom-call | flops 1000000000 | bytes 41943040 | tf_op jit(solution)/shard_map/pallas_call | solution.py:615
  213.3 23.3 %grad_sum.1.src = f32[512,128]{1,0:T(8,128)} custom-call(f32[320,64]{1,0:T(8,128)} %get-tuple-element.86.w0, f32[256,128]{1,0:T(8,128)} %get-tuple-element.87.b0, f32[64,128]{1,0:T(8,128)} %get-tuple-element.88.q0, f32[64,128]{1,0:T(8,128)} %get-tuple-element.89.g0, f32[64,128]{1,0:T(8,128)} %get-tuple-element.90.l0, f32[64,64]{1,0:T(8,128)} %get-tuple-element.91.wo0, ...), custom_call_target="tpu_custom_call" | custom-call | flops 1000000 | bytes 1048576 | tf_op jit(solution)/shard_map/grad_sum/pallas_call | solution.py:711
  236.7 1.8 shard_map.159
  238.4 3.2 %copy.18 = bf16[1,64,256,64]{2,3,1,0:T(8,128)(2,1)} copy(bf16[1,64,256,64]{2,3,1,0:T(8,128)(2,1)} %bitcast.23) | data formatting | bytes 4194304
Async XLA Ops:
  0.6 49.7 %collective-permute-start = (bf16[64,64,256]{2,1,0:T(8,128)(2,1)}, bf16[64,64,256]{2,1,0:T(8,128)(2,1)}, u32[]{:S(2)}, u32[]{:S(2)}) collective-permute-start(bf16[64,64,256]{2,1,0:T(8,128)(2,1)} %bitcast.15), channel_id=1, source_target_pairs={{0,2},{2,0},{1,3},{3,1},{4,6},{6,4},{5,7},{7,5},{8,10},{10,8},{9,1... | collective-permute-start | bytes 6291464 | tf_op jit(solution)/shard_map/ppermute | solution.py:756
  3.7 47.4 %collective-permute-start.1 = (s32[64,256]{1,0:T(8,128)}, s32[64,256]{1,0:T(8,128)}, u32[]{:S(2)}, u32[]{:S(2)}) collective-permute-start(s32[64,256]{1,0:T(8,128)} %bitcast.24), channel_id=1, source_target_pairs={{0,2},{2,0},{1,3},{3,1},{4,6},{6,4},{5,7},{7,5},{8,10},{10,8},{9,1... | collective-permute-start | bytes 196616 | tf_op jit(solution)/shard_map/ppermute | solution.py:756
  18.7 42.0 %collective-permute-start.3 = (bf16[64,64,256]{2,1,0:T(8,128)(2,1)}, bf16[64,64,256]{2,1,0:T(8,128)(2,1)}, u32[]{:S(2)}, u32[]{:S(2)}) collective-permute-start(bf16[64,64,256]{2,1,0:T(8,128)(2,1)} %get-tuple-element.67.bo), channel_id=1, source_target_pairs={{0,1},{1,0},{2,3},{3,2},{4,5},{5,4},{6,7},{7,6},{8,9},{9,8},{10,11... | collective-permute-start | bytes 6291464 | tf_op jit(solution)/shard_map/ppermute | solution.py:759
  58.3 4.5 %collective-permute-start.2 = (bf16[64,64,256]{2,1,0:T(8,128)(2,1)}, bf16[64,64,256]{2,1,0:T(8,128)(2,1)}, u32[]{:S(2)}, u32[]{:S(2)}) collective-permute-start(bf16[64,64,256]{2,1,0:T(8,128)(2,1)} %get-tuple-element.66.bp), channel_id=1, source_target_pairs={{0,1},{1,0},{2,3},{3,2},{4,5},{5,4},{6,7},{7,6},{8,9},{9,8},{10,11... | collective-permute-start | bytes 6291464 | tf_op jit(solution)/shard_map/ppermute | solution.py:759
  58.3 48.4 %collective-permute-start.4 = (bf16[64,64,256]{2,1,0:T(8,128)(2,1)}, bf16[64,64,256]{2,1,0:T(8,128)(2,1)}, u32[]{:S(2)}, u32[]{:S(2)}) collective-permute-start(bf16[64,64,256]{2,1,0:T(8,128)(2,1)} %bitcast.20), channel_id=1, source_target_pairs={{0,2},{2,0},{1,3},{3,1},{4,6},{6,4},{5,7},{7,5},{8,10},{10,8},{9,1... | collective-permute-start | bytes 6291464 | tf_op jit(solution)/shard_map/ppermute | solution.py:756
  60.1 127.8 %collective-permute-start.7 = (bf16[64,64,256]{2,1,0:T(8,128)(2,1)}, bf16[64,64,256]{2,1,0:T(8,128)(2,1)}, u32[]{:S(2)}, u32[]{:S(2)}) collective-permute-start(bf16[64,64,256]{2,1,0:T(8,128)(2,1)} %get-tuple-element.65.ao), channel_id=1, source_target_pairs={{0,1},{1,0},{2,3},{3,2},{4,5},{5,4},{6,7},{7,6},{8,9},{9,8},{10,11... | collective-permute-start | bytes 6291464 | tf_op jit(solution)/shard_map/ppermute | solution.py:759
  60.3 127.6 %collective-permute-start.6 = (bf16[64,64,256]{2,1,0:T(8,128)(2,1)}, bf16[64,64,256]{2,1,0:T(8,128)(2,1)}, u32[]{:S(2)}, u32[]{:S(2)}) collective-permute-start(bf16[64,64,256]{2,1,0:T(8,128)(2,1)} %get-tuple-element.64.ap), channel_id=1, source_target_pairs={{0,1},{1,0},{2,3},{3,2},{4,5},{5,4},{6,7},{7,6},{8,9},{9,8},{10,11... | collective-permute-start | bytes 6291464 | tf_op jit(solution)/shard_map/ppermute | solution.py:759
  187.8 4.6 %collective-permute-start.5 = (bf16[64,128,128]{2,1,0:T(8,128)(2,1)}, bf16[64,128,128]{2,1,0:T(8,128)(2,1)}, u32[]{:S(2)}, u32[]{:S(2)}) collective-permute-start(bf16[64,128,128]{2,1,0:T(8,128)(2,1)} %get-tuple-element.82), channel_id=1, source_target_pairs={{0,1},{1,0},{2,3},{3,2},{4,5},{5,4},{6,7},{7,6},{8,9},{9,8},{10,11... | collective-permute-start | bytes 6291464 | tf_op jit(solution)/shard_map/ppermute | solution.py:759
